TPU v7x, 128 devices: a whole 4x4x4 slice. The times are simulated.
128 devices in a mesh: row: 4 (over z), col: 32 (over y, x, core).
Axes of the slice: x: 4, y: 4, z: 4, core: 2. Of those that a mesh axis runs over, the one named last changes fastest.
Arguments:
- inv_depth: float32 [256, 3072], P(('row', 'col')), may hold values from 0.2 to 1
- rotation: float32 [3, 256], P(None, ('row', 'col')), may hold values from -0.05 to 0.05
- translation: float32 [3, 256], P(None, ('row', 'col')), may hold values from -0.25 to 0.25
- edge_target: int32 [256, 24], P(('row', 'col')), may hold values from 0 to 255, as said below
- flow_obs: float32 [2, 256, 24, 3072], P(None, ('row', 'col')), may hold values from -2.8 to 2.8
- weight: float32 [2, 256, 24, 3072], P(None, ('row', 'col')), may hold values from 0.1 to 1
Outputs:
- depth_next: float32 [256, 3072], P(('row', 'col'))
- pose_step: float32 [6, 256], P(None, ('row', 'col'))
Inputs may be any that keep to these rules, and one draw needn't show every extreme that they name: `edge_target`: each keyframe's targets are distinct, differ from the keyframe itself, are sorted ascending, and lie in the keyframe's own block of 64 consecutive keyframes or in one of the two neighbouring blocks, the blocks counted cyclically.
All inputs are finite; a program needn't handle non-finite values.
Results may differ from a plain program's by a relative error of at most 0.0003.
Values sent between devices are 32-bit elements; how exact they have to be, the bound alone decides.
A program may use at most 128 MiB of HBM per device.

v0:
```python
import jax
import jax.numpy as jnp
from jax import lax
from jax.sharding import Mesh
from jax.sharding import PartitionSpec as P

IMG_H = 48
IMG_W = 64
COL = ("col_0", "col_1", "col_2")
ROW_COL = ("row", "col_0", "col_1", "col_2")


PRECISE = lax.Precision.HIGHEST
DAMP_DEPTH = 0.1
LEVENBERG = 0.1
RIDGE = 0.001


def copy_for_each(shard, axis):
    devices = lax.axis_size(axis)
    return lax.all_to_all(
        jnp.broadcast_to(shard[None], (devices, *shard.shape)), axis, 0, 0, tiled=True
    )


def joined_along(blocks, dim):
    dims = list(blocks.shape[1:])
    dims[dim] *= blocks.shape[0]
    return jnp.moveaxis(blocks, 0, dim).reshape(dims)


def collect_2(shard, axis, dim):
    blocks = copy_for_each(shard, axis)
    return joined_along(blocks, dim)


def with_halo(cells, sides, width):
    for axis, dim in sides:
        count = lax.axis_size(axis)
        head = lax.slice_in_dim(cells, 0, width, axis=dim)
        tail = lax.slice_in_dim(cells, cells.shape[dim] - width, cells.shape[dim], axis=dim)
        cells = jnp.concatenate(
            [
                lax.ppermute(tail, axis, [(i, (i + 1) % count) for i in range(count)]),
                cells,
                lax.ppermute(head, axis, [((i + 1) % count, i) for i in range(count)]),
            ],
            axis=dim,
        )
    return cells


def from_behind(shard, axis, by):
    devices = lax.axis_size(axis)
    return lax.ppermute(shard, axis, [(i, (i + by) % devices) for i in range(devices)])


def split_up(shard, dim, devices):
    dims = shard.shape
    blocks = shard.reshape(*dims[:dim], devices, dims[dim] // devices, *dims[dim + 1 :])
    return jnp.moveaxis(blocks, dim, 0)


def sent_and_summed(shard, axis, dim):
    devices = lax.axis_size(axis)
    blocks = lax.all_to_all(split_up(shard, dim, devices), axis, 0, 0, tiled=True)
    return jnp.sum(blocks, axis=0)


def gather_turned(arrays, axis, dims):
    turned = [jnp.moveaxis(a, dim, 0) for a, dim in zip(arrays, dims)]
    both = jnp.concatenate([t.reshape(len(t), -1) for t in turned], axis=1)
    result, at, outs = (lax.all_gather(both, axis, axis=0, tiled=True), 0, [])
    for t, dim in zip(turned, dims):
        piece = result[:, at : at + t[0].size].reshape(-1, *t.shape[1:])
        outs.append(jnp.moveaxis(piece, 0, dim))
        at += t[0].size
    return tuple(outs)


def one_axis_at_a_time(shard, axes):
    for axis in axes:
        shard = lax.psum(shard, axis)
    return shard


def pixel_grid(pixel_count):
    pixel_index = jnp.arange(pixel_count, dtype=jnp.int32)
    across = (pixel_index % IMG_W).astype(jnp.float32)
    downward = (pixel_index // IMG_W).astype(jnp.float32)
    return ((across + 0.5) / IMG_W - 0.5, (downward + 0.5 - 0.5 * IMG_H) / IMG_W)


def edge_terms(relative, target_depth, flows, weights, across, downward):
    spin_x, spin_y, spin_z, move_x, move_y, move_z = [relative[i][:, None] for i in range(6)]
    point_x = across + spin_y - spin_z * downward + move_x * target_depth
    point_y = downward + spin_z * across - spin_x + move_y * target_depth
    point_z = 1.0 + spin_x * downward - spin_y * across + move_z * target_depth
    recip_z = 1.0 / point_z
    image_u = point_x * recip_z
    image_v = point_y * recip_z
    resid_u = flows[0] - (image_u - across)
    resid_v = flows[1] - (image_v - downward)
    slope_u = recip_z * (move_x - image_u * move_z)
    slope_v = recip_z * (move_y - image_v * move_z)
    depth_recip = target_depth * recip_z
    blank_map = jnp.zeros_like(recip_z)
    jac_u = jnp.stack(
        [
            -image_u * downward * recip_z,
            (1.0 + image_u * across) * recip_z,
            -downward * recip_z,
            depth_recip,
            blank_map,
            -image_u * depth_recip,
        ]
    )
    jac_v = jnp.stack(
        [
            (-1.0 - image_v * downward) * recip_z,
            image_v * across * recip_z,
            across * recip_z,
            blank_map,
            depth_recip,
            -image_v * depth_recip,
        ]
    )
    weight_u = weights[0]
    weight_v = weights[1]
    depth_grad = weight_u * slope_u * resid_u + weight_v * slope_v * resid_v
    depth_curv = weight_u * slope_u * slope_u + weight_v * slope_v * slope_v
    scaled_u = weight_u * jac_u
    scaled_v = weight_v * jac_v
    coupling = scaled_u * slope_u + scaled_v * slope_v
    block = jnp.einsum("aep,bep->eab", scaled_u, jac_u, precision=PRECISE) + jnp.einsum(
        "aep,bep->eab", scaled_v, jac_v, precision=PRECISE
    )
    pose_grad = jnp.einsum("aep,ep->ea", scaled_u, resid_u, precision=PRECISE) + jnp.einsum(
        "aep,ep->ea", scaled_v, resid_v, precision=PRECISE
    )
    return (depth_grad, depth_curv, coupling, block, pose_grad)


def solve_frames(block_table):
    frame_count = block_table.shape[0]
    matrix = block_table[:, :36].reshape(frame_count, 6, 6).transpose(1, 2, 0)
    right_side = block_table[:, 36:].T
    factor = {}
    for i in range(6):
        for j in range(i + 1):
            element = matrix[i, j]
            if i == j:
                element = element * (1.0 + LEVENBERG) + RIDGE
            for k in range(j):
                element = element - factor[i, k] * factor[j, k]
            factor[i, j] = jnp.sqrt(element) if i == j else element / factor[j, j]
    forward = []
    for i in range(6):
        element = right_side[i]
        for k in range(i):
            element = element - factor[i, k] * forward[k]
        forward.append(element / factor[i, i])
    result = [None] * 6
    for i in reversed(range(6)):
        element = forward[i]
        for k in range(i + 1, 6):
            element = element - factor[k, i] * result[k]
        result[i] = element / factor[i, i]
    return jnp.stack(result, 1)


def spread(values):
    grouped = collect_2(values, COL, 0)
    return with_halo(grouped[None], (("row", 0),), 1)


def collect(buffer):
    from_next = from_behind(buffer[0], "row", -1)
    from_prev = from_behind(buffer[2], "row", 1)
    return sent_and_summed(buffer[1] + from_next + from_prev, COL, 0)


def shards(inv_depth, rotation, translation, edge_target, flow_obs, weight):
    frames_dev, pixels = inv_depth.shape
    per_frame = edge_target.shape[1]
    edges = frames_dev * per_frame
    columns = lax.axis_size(COL)
    loop_size = lax.axis_size("row")
    group_size = frames_dev * columns
    total_frames = group_size * loop_size
    my_row = lax.axis_index("row")
    first_frame = (my_row * columns + lax.axis_index(COL)) * frames_dev
    targets = edge_target.reshape(edges)
    sources = first_frame + jnp.arange(edges, dtype=jnp.int32) // per_frame
    offsets = (targets // group_size - my_row + 1 + loop_size) % loop_size
    slot_index = offsets * group_size + targets % group_size
    across, downward = pixel_grid(pixels)
    pose_parts = gather_turned((rotation, translation), ROW_COL, (1, 1))
    pose_all = jnp.concatenate(pose_parts, 0)
    frame_ids = jnp.arange(total_frames, dtype=jnp.int32)
    src_hot = (sources[:, None] == frame_ids[None, :]).astype(jnp.float32)
    tgt_hot = (targets[:, None] == frame_ids[None, :]).astype(jnp.float32)
    pair_hot = src_hot - tgt_hot
    relative = jnp.dot(pair_hot, pose_all.T, precision=PRECISE).T
    nearby_depth = spread(inv_depth).reshape(3 * group_size, pixels)
    target_depth = jnp.take(nearby_depth, slot_index, axis=0)
    depth_grad, depth_curv, coupling, block, pose_grad = edge_terms(
        relative,
        target_depth,
        flow_obs.reshape(2, edges, pixels),
        weight.reshape(2, edges, pixels),
        across,
        downward,
    )
    slot_hot = (jnp.arange(3 * group_size, dtype=jnp.int32)[:, None] == slot_index[None, :]).astype(
        jnp.float32
    )

    def coalesce(values):
        flat_rows = values.reshape(edges, -1)
        summed = jnp.dot(slot_hot, flat_rows, precision=PRECISE)
        return summed.reshape((3, group_size) + values.shape[1:])

    depth_sums = collect(coalesce(jnp.stack([depth_grad, depth_curv], 1)))
    grad_sum = depth_sums[:, 0]
    inverse = 1.0 / (DAMP_DEPTH + depth_sums[:, 1])
    scaled = grad_sum * inverse
    returned = spread(jnp.stack([inverse, scaled], 1)).reshape(3 * group_size, 2, pixels)
    at_edges = jnp.take(returned, slot_index, axis=0)
    reduced = block - jnp.einsum(
        "aep,bep->eab", coupling * at_edges[:, 0][None], coupling, precision=PRECISE
    )
    reduced_grad = pose_grad - jnp.einsum("aep,ep->ea", coupling, at_edges[:, 1], precision=PRECISE)
    flat_block = reduced.reshape(edges, 36)
    out_rows = jnp.concatenate([flat_block, reduced_grad], 1)
    in_rows = jnp.concatenate([flat_block, -reduced_grad], 1)
    block_table = jnp.dot(src_hot.T, out_rows, precision=PRECISE) + jnp.dot(
        tgt_hot.T, in_rows, precision=PRECISE
    )
    block_table = one_axis_at_a_time(block_table, ROW_COL)
    frame_steps = solve_frames(block_table)
    own_step = lax.dynamic_slice_in_dim(frame_steps, first_frame, frames_dev, 0)
    motion = jnp.dot(pair_hot, frame_steps, precision=PRECISE)
    correction = jnp.einsum("aep,ea->ep", coupling, motion, precision=PRECISE)
    fix_sum = collect(coalesce(correction))
    depth_next = inv_depth + (grad_sum - fix_sum) * inverse
    return (depth_next, own_step.T)


def solution(mesh):
    finer = Mesh(
        mesh.devices.reshape(mesh.shape["row"], 4, 4, 2), ("row", "col_0", "col_1", "col_2")
    )
    in_specs = (
        P(ROW_COL, None),
        P(None, ROW_COL),
        P(None, ROW_COL),
        P(ROW_COL, None),
        P(None, ROW_COL, None, None),
        P(None, ROW_COL, None, None),
    )
    out_specs = (P(ROW_COL, None), P(None, ROW_COL))
    return jax.shard_map(
        shards, mesh=finer, in_specs=in_specs, out_specs=out_specs, check_vma=False
    )
```

profile of v0, /device:TPU:1, one launch (start us, length us, event | category | flops | bytes accessed | tf_op | source)
XLA Modules:
  0.0 463.6 jit_solution(2016711733986007781)
XLA Ops:
  2.6 8.6 %all-to-all-start = ((f32[32,2,3072]{2,1,0:T(2,128)}), f32[32,2,3072]{2,1,0:T(2,128)S(1)}, u32[]{:S(2)}, u32[]{:S(2)}) async-start(f32[32,2,3072]{2,1,0:T(2,128)} %broadcast_in_dim.30), calls=%async_computation | async-start | bytes 1572864 | tf_op jit(solution)/shard_map/all_to_all | solution.py:21
  14.7 37.9 %all-gather = f32[128,2,6]{2,1,0:T(2,128)S(1)} all-gather(f32[1,2,6]{2,1,0:T(2,128)S(1)} %maximum_bitcast_fusion.1), channel_id=1, replica_groups=mesh['row'=4,'col_0'=4,'col_1'=4,'col_2'=2] {'row','col_0','col_1','col_2'}, dimensions={0}, use_global_device_ids=true | all-gather | bytes 6192 | tf_op jit(solution)/shard_map/all_gather | solution.py:73
  59.7 14.1 %collective-permute-done.1 = f32[1,64,3072]{2,1,0:T(8,128)S(1)} collective-permute-done((f32[1,64,3072]{2,1,0:T(8,128)S(1)}, f32[1,64,3072]{2,1,0:T(8,128)S(1)}, u32[]{:S(2)}, u32[]{:S(2)}) %collective-permute-start.1) | collective-permute-done | bytes 786464 | tf_op jit(solution)/shard_map/ppermute | solution.py:46
  101.2 27.2 %collective-permute-done.3 = f32[64,2,3072]{2,1,0:T(2,128)} collective-permute-done((f32[64,2,3072]{2,1,0:T(2,128)}, f32[64,2,3072]{2,1,0:T(2,128)}, u32[]{:S(2)}, u32[]{:S(2)}) %collective-permute-start.3) | collective-permute-done | bytes 1572896 | tf_op jit(solution)/shard_map/ppermute | solution.py:55
  132.2 6.1 %all-to-all-start.1 = ((f32[32,2,2,3072]{3,2,1,0:T(2,128)}), f32[32,2,2,3072]{3,2,1,0:T(2,128)S(1)}, u32[]{:S(2)}, u32[]{:S(2)}) async-start(f32[32,2,2,3072]{3,2,1,0:T(2,128)} %bitcast.445), calls=%async_computation.1 | async-start | bytes 3145728 | tf_op jit(solution)/shard_map/all_to_all | solution.py:66
  141.7 18.8 %all-to-all-done.1 = f32[32,2,2,3072]{3,2,1,0:T(2,128)S(1)} async-done(((f32[32,2,2,3072]{3,2,1,0:T(2,128)}), f32[32,2,2,3072]{3,2,1,0:T(2,128)S(1)}, u32[]{:S(2)}, u32[]{:S(2)}) %all-to-all-start.1) | async-done | bytes 1572896 | tf_op jit(solution)/shard_map/all_to_all | solution.py:66
  163.1 5.7 %all-to-all-start.2 = ((f32[32,2,2,3072]{3,2,1,0:T(2,128)}), f32[32,2,2,3072]{3,2,1,0:T(2,128)S(1)}, u32[]{:S(2)}, u32[]{:S(2)}) async-start(f32[32,2,2,3072]{3,2,1,0:T(2,128)} %broadcast_in_dim.37), calls=%async_computation.2 | async-start | bytes 3145728 | tf_op jit(solution)/shard_map/all_to_all | solution.py:21
  173.7 17.5 %all-to-all-done.2 = f32[32,2,2,3072]{3,2,1,0:T(2,128)S(1)} async-done(((f32[32,2,2,3072]{3,2,1,0:T(2,128)}), f32[32,2,2,3072]{3,2,1,0:T(2,128)S(1)}, u32[]{:S(2)}, u32[]{:S(2)}) %all-to-all-start.2) | async-done | bytes 1572896 | tf_op jit(solution)/shard_map/all_to_all | solution.py:21
  198.5 27.4 %collective-permute-done.5 = f32[1,64,2,3072]{3,2,1,0:T(2,128)S(1)} collective-permute-done((f32[1,64,2,3072]{3,2,1,0:T(2,128)S(1)}, f32[1,64,2,3072]{3,2,1,0:T(2,128)S(1)}, u32[]{:S(2)}, u32[]{:S(2)}) %collective-permute-start.5) | collective-permute-done | bytes 1572896 | tf_op jit(solution)/shard_map/ppermute | solution.py:46
  240.1 9.1 %broadcast_multiply_fusion = (f32[6,48,3072]{2,1,0:T(8,128)}, f32[6,48,3072]{2,1,0:T(8,128)S(1)}, f32[6,48,3072]{2,1,0:T(8,128)}, f32[6,48,3072]{2,1,0:T(8,128)}) fusion(f32[48,3072]{1,0:T(8,128)} %bitcast.449, f32[48,3072]{1,0:T(8,128)} %get-tuple-element.58, f32[48,3072]{1,0:T(8,128)} %get-tuple-element.55, ...), kind=kLoop, calls=%fused_computation.22 | loop fusion | flops 5308416 | bytes 24182784 | tf_op jit(solution)/shard_map/mul | solution.py:231
  249.2 12.9 %fusion.2 = f32[48,1,6]{2,1,0:T(1,128)} fusion(f32[6,48,3072]{2,1,0:T(8,128)S(1)} %get-tuple-element.38, f32[48,2,3072]{2,1,0:T(2,128)S(1)} %broadcast_select_fusion), kind=kOutput, calls=%fused_computation.4 | convolution fusion | flops 10616832 | bytes 4129920 | tf_op jit(solution)/shard_map/aep,ep->ea/dot_general | solution.py:233
  262.9 18.1 %fusion.8 = f32[48,6,6]{2,1,0:T(8,128)} fusion(f32[6,48,3072]{2,1,0:T(8,128)} %get-tuple-element.40, f32[6,48,3072]{2,1,0:T(8,128)} %get-tuple-element.60), kind=kOutput, calls=%fused_computation.10 | convolution fusion | flops 63700992 | bytes 7084800 | tf_op jit(solution)/shard_map/aep,bep->eab/dot_general | solution.py:135
  281.0 12.8 %fusion.6 = f32[48,1,6]{2,1,0:T(1,128)} fusion(f32[6,48,3072]{2,1,0:T(8,128)S(1)} %copy-done.1, f32[48,3072,1]{1,0,2:T(8,128)S(1)} %bitcast.451), kind=kOutput, calls=%fused_computation.8 | convolution fusion | flops 10616832 | bytes 4129920 | tf_op jit(solution)/shard_map/aep,ep->ea/dot_general | solution.py:138
  294.6 16.7 %fusion.17 = f32[48,6,6]{2,1,0:T(8,128)S(1)} fusion(f32[48,6,6]{2,1,0:T(8,128)} %fusion.8, f32[6,48,3072]{2,1,0:T(8,128)} %multiply_dynamic-update-slice_fusion.4, f32[6,48,3072]{2,1,0:T(8,128)} %get-tuple-element.39), kind=kOutput, calls=%fused_computation.28 | convolution fusion | flops 63702720 | bytes 7091712 | tf_op jit(solution)/shard_map/aep,bep->eab/dot_general | solution.py:135
  311.3 13.0 %fusion.10 = f32[48,1,6]{2,1,0:T(1,128)} fusion(f32[6,48,3072]{2,1,0:T(8,128)S(1)} %copy-done, f32[48,3072,1]{1,0,2:T(8,128)S(1)} %bitcast.450), kind=kOutput, calls=%fused_computation.12 | convolution fusion | flops 10616832 | bytes 4129920 | tf_op jit(solution)/shard_map/aep,ep->ea/dot_general | solution.py:138
  324.2 14.9 %fusion.22 = f32[48,6,6]{2,1,0:T(8,128)} fusion(f32[48,6,6]{2,1,0:T(8,128)S(1)} %fusion.17, f32[6,48,3072]{2,1,0:T(8,128)S(1)} %get-tuple-element.38, f32[6,48,3072]{2,1,0:T(8,128)S(1)} %copy-done.2), kind=kOutput, calls=%fused_computation.29 | convolution fusion | flops 63702720 | bytes 7091712 | tf_op jit(solution)/shard_map/aep,bep->eab/dot_general | solution.py:230
  345.5 12.3 %psum.28 = f32[256,42]{0,1:T(8,128)} all-reduce(f32[256,42]{0,1:T(8,128)} %convolution_add_fusion), channel_id=1, replica_groups=mesh['row'=4,'col_0'=4,'col_1'=4,'col_2'=2] {'row'}, use_global_device_ids=true, to_apply=%region_1.2 | all-reduce | flops 10752 | bytes 86016 | tf_op jit(solution)/shard_map/psum | solution.py:83
  357.8 15.9 %psum.29 = f32[256,42]{0,1:T(8,128)} all-reduce(f32[256,42]{0,1:T(8,128)} %psum.28), channel_id=1, replica_groups=mesh['row'=4,'col_0'=4,'col_1'=4,'col_2'=2] {'col_0'}, use_global_device_ids=true, to_apply=%region_2.3 | all-reduce | flops 10752 | bytes 86016 | tf_op jit(solution)/shard_map/psum | solution.py:83
  373.7 14.3 %psum.30 = f32[256,42]{0,1:T(8,128)} all-reduce(f32[256,42]{0,1:T(8,128)} %psum.29), channel_id=1, replica_groups=mesh['row'=4,'col_0'=4,'col_1'=4,'col_2'=2] {'col_1'}, use_global_device_ids=true, to_apply=%region_3.4 | all-reduce | flops 10752 | bytes 86016 | tf_op jit(solution)/shard_map/psum | solution.py:83
  388.0 16.2 %psum.31 = f32[256,42]{0,1:T(8,128)} all-reduce(f32[256,42]{0,1:T(8,128)} %psum.30), channel_id=1, replica_groups=mesh['row'=4,'col_0'=4,'col_1'=4,'col_2'=2] {'col_2'}, use_global_device_ids=true, to_apply=%region_4.5 | all-reduce | flops 10752 | bytes 86016 | tf_op jit(solution)/shard_map/psum | solution.py:83
  412.7 6.0 %fusion = f32[48,1,3072]{2,1,0:T(1,128)S(1)} fusion(f32[48,6,1]{1,2,0:T(1,128)S(1)} %bitcast.456, f32[6,48,3072]{2,1,0:T(8,128)S(1)} %get-tuple-element.38), kind=kOutput, calls=%fused_computation.2 | convolution fusion | flops 10616832 | bytes 4129920 | tf_op jit(solution)/shard_map/aep,ea->ep/dot_general | solution.py:244
  421.7 17.3 %collective-permute-done.6 = f32[64,3072]{1,0:T(8,128)S(1)} collective-permute-done((f32[64,3072]{1,0:T(8,128)S(1)}, f32[64,3072]{1,0:T(8,128)S(1)}, u32[]{:S(2)}, u32[]{:S(2)}) %collective-permute-start.6) | collective-permute-done | bytes 786464 | tf_op jit(solution)/shard_map/ppermute | solution.py:55
  443.0 5.0 %all-to-all-start.3 = ((f32[32,2,3072]{2,1,0:T(2,128)}), f32[32,2,3072]{2,1,0:T(2,128)S(1)}, u32[]{:S(2)}, u32[]{:S(2)}) async-start(f32[32,2,3072]{2,1,0:T(2,128)} %reshape.5250), calls=%async_computation.3 | async-start | bytes 1572864 | tf_op jit(solution)/shard_map/all_to_all | solution.py:66
  448.8 13.5 %all-to-all-done.3 = f32[32,2,3072]{2,1,0:T(2,128)S(1)} async-done(((f32[32,2,3072]{2,1,0:T(2,128)}), f32[32,2,3072]{2,1,0:T(2,128)S(1)}, u32[]{:S(2)}, u32[]{:S(2)}) %all-to-all-start.3) | async-done | bytes 786464 | tf_op jit(solution)/shard_map/all_to_all | solution.py:66
  (146 shorter events, 101.0 us)
Async XLA Ops:
  0.6 56.5 %copy-start.10 = (f32[2,2,24,3072]{3,2,1,0:T(8,128)S(1)}, f32[2,2,24,3072]{3,2,1,0:T(8,128)}, u32[]{:S(2)}) copy-start(f32[2,2,24,3072]{3,2,1,0:T(8,128)} %param.10) | copy-start | bytes 3538948
  2.6 51.7 %all-to-all-start = ((f32[32,2,3072]{2,1,0:T(2,128)}), f32[32,2,3072]{2,1,0:T(2,128)S(1)}, u32[]{:S(2)}, u32[]{:S(2)}) async-start(f32[32,2,3072]{2,1,0:T(2,128)} %broadcast_in_dim.30), calls=%async_computation | async-start | bytes 1572864 | tf_op jit(solution)/shard_map/all_to_all | solution.py:21
  11.9 44.6 %copy-start.27 = (s32[48]{0:T(128)}, s32[48]{0:T(128)S(1)}, u32[]{:S(2)}) copy-start(s32[48]{0:T(128)S(1)} %reshape.5242) | copy-start | bytes 580
  52.9 20.9 %copy-start.28 = (s32[48]{0:T(128)}, s32[48]{0:T(128)S(1)}, u32[]{:S(2)}) copy-start(s32[48]{0:T(128)S(1)} %fusion.146) | copy-start | bytes 580
  54.8 19.0 %collective-permute-start.1 = (f32[1,64,3072]{2,1,0:T(8,128)S(1)}, f32[1,64,3072]{2,1,0:T(8,128)S(1)}, u32[]{:S(2)}, u32[]{:S(2)}) collective-permute-start(f32[1,64,3072]{2,1,0:T(8,128)S(1)} %broadcast_in_dim_reshape.7), channel_id=1, source_target_pairs={{32,0},{64,32},{96,64},{0,96},{33,1},{65,33},{97,65},{1,97},{34,2}... | collective-permute-start | bytes 2359304 | tf_op jit(solution)/shard_map/ppermute | solution.py:46
  56.6 19.9 %collective-permute-start = (f32[1,64,3072]{2,1,0:T(8,128)S(1)}, f32[1,64,3072]{2,1,0:T(8,128)S(1)}, u32[]{:S(2)}, u32[]{:S(2)}) collective-permute-start(f32[1,64,3072]{2,1,0:T(8,128)S(1)} %broadcast_in_dim_reshape.7), channel_id=1, source_target_pairs={{0,32},{32,64},{64,96},{96,0},{1,33},{33,65},{65,97},{97,1},{2,34}... | collective-permute-start | bytes 2359304 | tf_op jit(solution)/shard_map/ppermute | solution.py:44
  92.2 36.2 %collective-permute-start.3 = (f32[64,2,3072]{2,1,0:T(2,128)}, f32[64,2,3072]{2,1,0:T(2,128)}, u32[]{:S(2)}, u32[]{:S(2)}) collective-permute-start(f32[64,2,3072]{2,1,0:T(2,128)} %squeeze.110), channel_id=1, source_target_pairs={{0,32},{32,64},{64,96},{96,0},{1,33},{33,65},{65,97},{97,1},{2,34}... | collective-permute-start | bytes 4718600 | tf_op jit(solution)/shard_map/ppermute | solution.py:55
  92.2 36.2 %collective-permute-start.2 = (f32[64,2,3072]{2,1,0:T(2,128)}, f32[64,2,3072]{2,1,0:T(2,128)}, u32[]{:S(2)}, u32[]{:S(2)}) collective-permute-start(f32[64,2,3072]{2,1,0:T(2,128)} %squeeze.109), channel_id=1, source_target_pairs={{0,96},{32,0},{64,32},{96,64},{1,97},{33,1},{65,33},{97,65},{2,98}... | collective-permute-start | bytes 4718600 | tf_op jit(solution)/shard_map/ppermute | solution.py:55
  132.2 28.3 %all-to-all-start.1 = ((f32[32,2,2,3072]{3,2,1,0:T(2,128)}), f32[32,2,2,3072]{3,2,1,0:T(2,128)S(1)}, u32[]{:S(2)}, u32[]{:S(2)}) async-start(f32[32,2,2,3072]{3,2,1,0:T(2,128)} %bitcast.445), calls=%async_computation.1 | async-start | bytes 3145728 | tf_op jit(solution)/shard_map/all_to_all | solution.py:66
  163.1 32.2 %copy-start.20 = (f32[48]{0:T(128)S(1)}, f32[48]{0:T(128)}, u32[]{:S(2)}) copy-start(f32[48]{0:T(128)} %get-tuple-element.70) | copy-start | bytes 580
  163.1 32.2 %copy-start.24 = (f32[48]{0:T(128)S(1)}, f32[48]{0:T(128)}, u32[]{:S(2)}) copy-start(f32[48]{0:T(128)} %get-tuple-element.71) | copy-start | bytes 580
  163.1 33.4 %copy-start.4 = (f32[1,2,24,3072]{3,2,1,0:T(8,128)S(1)}, f32[1,2,24,3072]{3,2,1,0:T(8,128)}, u32[]{:S(2)}) copy-start(f32[1,2,24,3072]{3,2,1,0:T(8,128)} %get-tuple-element.50) | copy-start | bytes 1769476
  163.1 33.4 %copy-start.5 = (f32[1,2,24,3072]{3,2,1,0:T(8,128)S(1)}, f32[1,2,24,3072]{3,2,1,0:T(8,128)}, u32[]{:S(2)}) copy-start(f32[1,2,24,3072]{3,2,1,0:T(8,128)} %get-tuple-element.51) | copy-start | bytes 1769476
  163.1 33.4 %copy-start.22 = (f32[48]{0:T(128)S(1)}, f32[48]{0:T(128)}, u32[]{:S(2)}) copy-start(f32[48]{0:T(128)} %get-tuple-element.69) | copy-start | bytes 580
  163.1 28.1 %all-to-all-start.2 = ((f32[32,2,2,3072]{3,2,1,0:T(2,128)}), f32[32,2,2,3072]{3,2,1,0:T(2,128)S(1)}, u32[]{:S(2)}, u32[]{:S(2)}) async-start(f32[32,2,2,3072]{3,2,1,0:T(2,128)} %broadcast_in_dim.37), calls=%async_computation.2 | async-start | bytes 3145728 | tf_op jit(solution)/shard_map/all_to_all | solution.py:21
  191.2 34.7 %collective-permute-start.5 = (f32[1,64,2,3072]{3,2,1,0:T(2,128)S(1)}, f32[1,64,2,3072]{3,2,1,0:T(2,128)S(1)}, u32[]{:S(2)}, u32[]{:S(2)}) collective-permute-start(f32[1,64,2,3072]{3,2,1,0:T(2,128)S(1)} %bitcast.441), channel_id=1, source_target_pairs={{32,0},{64,32},{96,64},{0,96},{33,1},{65,33},{97,65},{1,97},{34,2}... | collective-permute-start | bytes 4718600 | tf_op jit(solution)/shard_map/ppermute | solution.py:46
  194.0 35.3 %collective-permute-start.4 = (f32[1,64,2,3072]{3,2,1,0:T(2,128)S(1)}, f32[1,64,2,3072]{3,2,1,0:T(2,128)S(1)}, u32[]{:S(2)}, u32[]{:S(2)}) collective-permute-start(f32[1,64,2,3072]{3,2,1,0:T(2,128)S(1)} %bitcast.442), channel_id=1, source_target_pairs={{0,32},{32,64},{64,96},{96,0},{1,33},{33,65},{65,97},{97,1},{2,34}... | collective-permute-start | bytes 4718600 | tf_op jit(solution)/shard_map/ppermute | solution.py:44
  339.1 79.6 %copy-start.26 = (s32[48]{0:T(128)S(1)}, s32[48]{0:T(128)}, u32[]{:S(2)}) copy-start(s32[48]{0:T(128)} %get-tuple-element.42) | copy-start | bytes 580
  420.0 19.0 %collective-permute-start.6 = (f32[64,3072]{1,0:T(8,128)S(1)}, f32[64,3072]{1,0:T(8,128)S(1)}, u32[]{:S(2)}, u32[]{:S(2)}) collective-permute-start(f32[64,3072]{1,0:T(8,128)S(1)} %get-tuple-element.46), channel_id=1, source_target_pairs={{0,96},{32,0},{64,32},{96,64},{1,97},{33,1},{65,33},{97,65},{2,98}... | collective-permute-start | bytes 2359304 | tf_op jit(solution)/shard_map/ppermute | solution.py:55
  421.7 40.8 %copy-start.12 = (f32[2,1,3072]{2,1,0:T(1,128)S(1)}, f32[2,1,3072]{2,1,0:T(1,128)}, u32[]{:S(2)}) copy-start(f32[2,1,3072]{2,1,0:T(1,128)} %copy-done.11) | copy-start | bytes 73732
  421.7 40.8 %copy-start.14 = (f32[2,1,3072]{2,1,0:T(1,128)S(1)}, f32[2,1,3072]{2,1,0:T(1,128)}, u32[]{:S(2)}) copy-start(f32[2,1,3072]{2,1,0:T(1,128)} %copy-done.13) | copy-start | bytes 73732
  421.7 40.9 %copy-start.15 = (f32[2,3072]{1,0:T(2,128)S(1)}, f32[2,3072]{1,0:T(2,128)}, u32[]{:S(2)}) copy-start(f32[2,3072]{1,0:T(2,128)} %param.6) | copy-start | bytes 73732
  421.7 19.9 %collective-permute-start.7 = (f32[64,3072]{1,0:T(8,128)S(1)}, f32[64,3072]{1,0:T(8,128)S(1)}, u32[]{:S(2)}, u32[]{:S(2)}) collective-permute-start(f32[64,3072]{1,0:T(8,128)S(1)} %get-tuple-element.47), channel_id=1, source_target_pairs={{0,32},{32,64},{64,96},{96,0},{1,33},{33,65},{65,97},{97,1},{2,34}... | collective-permute-start | bytes 2359304 | tf_op jit(solution)/shard_map/ppermute | solution.py:55
  443.0 19.3 %all-to-all-start.3 = ((f32[32,2,3072]{2,1,0:T(2,128)}), f32[32,2,3072]{2,1,0:T(2,128)S(1)}, u32[]{:S(2)}, u32[]{:S(2)}) async-start(f32[32,2,3072]{2,1,0:T(2,128)} %reshape.5250), calls=%async_computation.3 | async-start | bytes 1572864 | tf_op jit(solution)/shard_map/all_to_all | solution.py:66
  (17 other events, 213.3 us)
where the time goes:
time: 473 us; the launch traced here: 464 us
  waiting for transfers between devices  145 us (31%)
  matrix products  101 us (21%)
  blocking collectives  96.5 us (20%)
  other arithmetic  43.8 us (9%)
  local copies, waits for them, and re-layouts  41.3 us (9%)
  starting transfers between devices  35 us (7%)
    psum x4, blocking collectives, one_axis_at_a_time(): shard = lax.psum(shard, axis)  58.6 us
    ppermute x4, waiting for transfers between devices, from_behind(): lax.ppermute(shard, axis, [(i, (i + by) % devices) for i in range(devices)])  47.1 us
    ppermute x2, waiting for transfers between devices, with_halo(): lax.ppermute(head, axis, [((i + 1) % count, i) for i in range(count)])  41.5 us
    all_gather x1, blocking collectives, gather_turned(): result, at, outs = (lax.all_gather(both, axis, axis=0, tiled=True), 0, [])  37.9 us
    all_to_all x2, waiting for transfers between devices, sent_and_summed(): lax.all_to_all(split_up(shard, dim, devices), axis, 0, 0, tiled=True)  32.3 us
    dot_general x1, matrix products, edge_terms(): jnp.einsum('aep,bep->eab', scaled_v, jac_v, precision=PRECISE)  18.1 us
    all_to_all x2, waiting for transfers between devices, copy_for_each(): lax.all_to_all(jnp.broadcast_to(shard[None], (devices, *shard.shape)), ax...  17.5 us
    dot_general x1, matrix products, edge_terms(): jnp.einsum('aep,bep->eab', scaled_u, jac_u, precision=PRECISE)  16.7 us
  transfers between devices with their start and end apart: 12, of which 10 were waited for; matrix products, arithmetic and copies ran while one was open for 6% of the time, Pallas kernels for 0%

commit v1 on v0

v1 whole, which is shorter than its diff:
```python
import functools

import jax
import jax.numpy as jnp
from jax import lax
from jax.experimental import pallas as pl
from jax.experimental.pallas import tpu as pltpu
from jax.sharding import PartitionSpec as P

F32 = jnp.float32
BF16 = jnp.bfloat16
NDEV = 128
PX = 24
GROUPS = 16
LANES = 384
MESH = pl.DeviceIdType.MESH
PAIRS = [(a, b) for a in (0, 1, 2, 5) for b in (0, 1, 2, 5) if a <= b]
K_ROWS = [*PAIRS, *[(3, b) for b in range(6)], *[(4, b) for b in (0, 1, 2, 4, 5)]]
K_INDEX = {}
for _n, (_a, _b) in enumerate(K_ROWS):
    K_INDEX[_a, _b] = _n
    K_INDEX[_b, _a] = _n
H_ROW = 21


def lane_iota(shape=(8, 128)):
    return lax.broadcasted_iota(jnp.int32, shape, 1)


def pack_kernel(flow_ref, weight_ref, depth_ref, extra_ref, out_ref, low, high):
    turn = lax.axis_index("col") % 8

    def put(ref, block, value):
        at = pl.multiple_of(((3 * turn + block) % 8) * 16, 16)
        ref[pl.ds(at, 16), :] = value

    for n in range(3):
        put(low, n, flow_ref[0, 16 * n : 16 * n + 16, :])
        put(low, 3 + n, flow_ref[1, 16 * n : 16 * n + 16, :])
        put(high, 1 + n, weight_ref[1, 16 * n : 16 * n + 16, :])
        put(high, 4 + n, jnp.zeros((16, LANES), F32))
    put(low, 6, weight_ref[0, 0:16, :])
    put(low, 7, weight_ref[0, 16:32, :])
    put(high, 0, weight_ref[0, 32:48, :])
    dep = depth_ref[...]
    put(high, 7, jnp.concatenate([dep, dep], 0))
    low_t = low[...].T
    high_t = high[...].T
    where_at = (lane_iota() - 48 * turn + 384) % 128
    extra = pltpu.roll(extra_ref[...], 48 * turn, 1)
    for d in range(16):
        base = 24 * d
        for j in range(3):
            out_ref[d, 8 * j : 8 * j + 8, :] = low_t[base + 8 * j : base + 8 * j + 8]
        u0 = high_t[base : base + 8]
        u1 = high_t[base + 8 : base + 16]
        u2 = high_t[base + 16 : base + 24]
        out_ref[d, 24:32, :] = jnp.where(where_at < 64, u0, pltpu.roll(u1, 64, 1))
        tail = jnp.where(where_at < 114, u0, jnp.where(where_at < 116, u1, u2))
        tail = jnp.where(where_at < 112, extra, tail)
        out_ref[d, 32:40, :] = jnp.where(where_at < 64, u2, tail)


def pack(flow, weight, depth8, extra):
    return pl.pallas_call(
        pack_kernel,
        grid=(8,),
        in_specs=[
            pl.BlockSpec((2, 48, LANES), lambda i: (0, 0, i)),
            pl.BlockSpec((2, 48, LANES), lambda i: (0, 0, i)),
            pl.BlockSpec((8, LANES), lambda i: (0, i)),
            pl.BlockSpec((8, 128), lambda i: (0, 0)),
        ],
        out_specs=pl.BlockSpec((16, 40, 128), lambda i: (i, 0, 0)),
        out_shape=jax.ShapeDtypeStruct((NDEV, 40, 128), F32),
        scratch_shapes=[pltpu.VMEM((128, LANES), F32), pltpu.VMEM((128, LANES), F32)],
        name="pack",
    )(flow, weight, depth8, extra)


def strip(tiles, lane, offset, width):
    out = []
    for t in range(3):
        acc = None
        for i in range(8):
            start = 48 * i + offset
            for wrap in (0, 384, 768):
                a = max(start - wrap, 128 * t) - 128 * t
                b = min(start + width - wrap, 128 * t + 128) - 128 * t
                if a < b:
                    if acc is None:
                        acc = tiles[i]
                    else:
                        acc = jnp.where((lane >= a) & (lane < b), tiles[i], acc)
        out.append(acc)
    return out


def shifted(tiles, lane, shift):
    whole, part = divmod(shift % 384, 128)
    if part == 0:
        return [tiles[(t - whole) % 3] for t in range(3)]
    rolled = [pltpu.roll(t, part, 1) for t in tiles]
    return [
        jnp.where(lane < part, rolled[(t - whole - 1) % 3], rolled[(t - whole) % 3])
        for t in range(3)
    ]


def split3(x):
    top = x.astype(BF16).astype(F32)
    rest = x - top
    mid = rest.astype(BF16).astype(F32)
    return jnp.concatenate([top, mid, rest - mid], 0).astype(BF16)


def join3(y):
    n = y.shape[0] // 3
    return y[:n] + y[n : 2 * n] + y[2 * n :]


def gathered(table, hot):
    return join3(jnp.dot(split3(table), hot, preferred_element_type=F32))


def summed(values, hot):
    return join3(
        lax.dot_general(
            split3(values), hot, (((1,), (1,)), ((), ())), preferred_element_type=F32
        )
    )


def unpack_group(g, recv, comps, extras, table):
    lane = lane_iota()
    block_lane = [(lane + 128 * t) % 48 for t in range(3)]
    srcs = [8 * g + i for i in range(8)]
    tile3 = [recv[s, 24:32, :] for s in srcs]
    tile4 = [recv[s, 32:40, :] for s in srcs]
    for j in range(3):
        low = [recv[s, 8 * j : 8 * j + 8, :] for s in srcs]
        high = (tile3, tile3, tile4)[j]
        at = (0, 64, 0)[j]
        first = shifted(strip(low, lane, 96, 32), lane, -96)
        second = shifted(strip(high, lane, at, 16), lane, 32 - at)
        parts = [
            strip(low, lane, 0, 48),
            shifted(strip(low, lane, 48, 48), lane, -48),
            [jnp.where(b < 32, f, s) for b, f, s in zip(block_lane, first, second)],
            shifted(strip(high, lane, at + 16, 48), lane, -16 - at),
        ]
        for c, tiles in enumerate(parts):
            for t in range(3):
                comps[g, 24 * c + 8 * j : 24 * c + 8 * j + 8, 128 * t : 128 * t + 128] = tiles[t]
    for t, tile in enumerate(shifted(strip(tile4, lane, 64, 48), lane, -64)):
        extras[g, :, 128 * t : 128 * t + 128] = tile
    for f in range(2):
        for j in range(4):
            offset = 112 + 2 * j + f if j < 3 else 64 + 24 * f
            acc = jnp.zeros((8, 128), F32)
            for i in range(8):
                moved = pltpu.roll(tile4[i], (i - 48 * i - offset) % 128, 1)
                acc = jnp.where(lane == i, moved, acc)
            acc = pltpu.roll(acc, 8 * g, 1)
            rows, cols = slice(8 * j, 8 * j + 8), slice(128 * f, 128 * f + 128)
            table[rows, cols] = jnp.where(lane // 8 == g, acc, table[rows, cols])


def pixel_xy(me, j):
    p = me * PX + 8 * j + lax.broadcasted_iota(jnp.int32, (8, 128), 0)
    x = ((p % 64).astype(F32) + 0.5) / 64 - 0.5
    y = ((p // 64).astype(F32) + 0.5 - 24.0) / 64
    return x, y


def first_pass(g, me, comps, extras, table, hot, geom, rel, both, sums):
    target = extras[g, 0:1, :]
    rows = lax.broadcasted_iota(jnp.int32, (256, LANES), 0).astype(F32)
    hot[g] = jnp.where(rows == target, 1.0, 0.0).astype(BF16)
    near = gathered(table[...], hot[g])
    rel[g] = extras[g] - near[24:32]
    for j in range(3):
        x, y = pixel_xy(me, j)
        for t in range(3):
            cols = slice(128 * t, 128 * t + 128)
            w0, w1, w2, m0, m1, m2 = [rel[g, 1 + k : 2 + k, cols] for k in range(6)]
            at = [slice(24 * c + 8 * j, 24 * c + 8 * j + 8) for c in range(4)]
            d = near[8 * j : 8 * j + 8, cols]
            x0 = x + w1 - w2 * y + m0 * d
            x1 = y + w2 * x - w0 + m1 * d
            x2 = 1.0 + w0 * y - w1 * x + m2 * d
            q = 1.0 / x2
            u = x0 * q
            v = x1 * q
            ru = comps[g, at[0], cols] - (u - x)
            rv = comps[g, at[1], cols] - (v - y)
            du = q * (m0 - u * m2)
            dv = q * (m1 - v * m2)
            eu = comps[g, at[2], cols] * du
            ev = comps[g, at[3], cols] * dv
            comps[g, at[0], cols] = ru
            comps[g, at[1], cols] = rv
            geom[g, at[0], cols] = d
            geom[g, at[1], cols] = q
            geom[g, at[2], cols] = u
            geom[g, at[3], cols] = v
            both[8 * j : 8 * j + 8, cols] = eu * ru + ev * rv
            both[24 + 8 * j : 32 + 8 * j, cols] = eu * du + ev * dv
    sums[...] += summed(both[...], hot[g])


def source_hot(g):
    rows = lax.broadcasted_iota(jnp.int32, (256, LANES), 0)
    lanes = lax.broadcasted_iota(jnp.int32, (256, LANES), 1)
    frame = lanes // 24
    col = (frame % 2) * 128 + 8 * g + frame // 2
    return jnp.where(rows == col, 1.0, 0.0).astype(BF16)


def second_pass(g, me, comps, geom, rel, hot, inverse, trio, rows_kh, total):
    near = gathered(inverse[...], hot[g])
    for t in range(3):
        cols = slice(128 * t, 128 * t + 128)
        acc = [None] * 27
        m0, m1, m2 = [rel[g, 4 + k : 5 + k, cols] for k in range(3)]

        def add(row, value):
            acc[row] = value if acc[row] is None else acc[row] + value

        for j in range(3):
            x, y = pixel_xy(me, j)
            at = [slice(24 * c + 8 * j, 24 * c + 8 * j + 8) for c in range(4)]
            d, q, u, v = [geom[g, at[c], cols] for c in range(4)]
            ru, rv, cu, cv = [comps[g, at[c], cols] for c in range(4)]
            ci = near[8 * j : 8 * j + 8, cols]
            gi = near[24 + 8 * j : 32 + 8 * j, cols]
            du = q * (m0 - u * m2)
            dv = q * (m1 - v * m2)
            eu = cu * du
            ev = cv * dv
            a1 = eu * q
            a2 = ev * q
            trio[g, at[0], cols] = a1
            trio[g, at[1], cols] = a2
            trio[g, at[2], cols] = a1 * u + a2 * v
            qq = q * q
            iu = ci * eu
            alpha = (cu - iu * eu) * qq
            gamma = (iu * ev) * qq
            beta = (cv - ci * ev * ev) * qq
            hu = (cu * ru - eu * gi) * q
            hv = (cv * rv - ev * gi) * q
            nd = -d
            ju = {0: -(u * y), 1: 1.0 + u * x, 2: -y, 5: u * nd}
            jv = {0: -1.0 - v * y, 1: v * x, 2: x, 5: v * nd}
            gd = gamma * d
            pp = {b: alpha * ju[b] - gamma * jv[b] for b in ju}
            qb = {b: beta * jv[b] - gamma * ju[b] for b in ju}
            pp[3], pp[4] = alpha * d, -gd
            qb[4] = beta * d
            for a, b in PAIRS:
                add(K_INDEX[a, b], ju[a] * pp[b] + jv[a] * qb[b])
            for b in range(6):
                add(K_INDEX[3, b], d * pp[b])
            for b in (0, 1, 2, 4, 5):
                add(K_INDEX[4, b], d * qb[b])
            for b in ju:
                add(H_ROW + b, ju[b] * hu + jv[b] * hv)
            add(H_ROW + 3, d * hu)
            add(H_ROW + 4, d * hv)
        for row in range(27):
            rows_kh[row : row + 1, cols] = jnp.sum(acc[row], axis=0, keepdims=True)
    src = source_hot(g)
    values = rows_kh[...]
    plus = summed(values, src + hot[g])
    minus = summed(values, src - hot[g])
    kind = lax.broadcasted_iota(jnp.int32, (32, 256), 0)
    total[...] += jnp.where(kind < H_ROW, plus, minus)


def third_pass(g, me, geom, trio, hot, steps, corr, fix):
    motion = gathered(steps[...], source_hot(g) - hot[g])
    for j in range(3):
        x, y = pixel_xy(me, j)
        for t in range(3):
            cols = slice(128 * t, 128 * t + 128)
            at = [slice(24 * c + 8 * j, 24 * c + 8 * j + 8) for c in range(3)]
            n0, n1, n2, n3, n4, n5 = [motion[k : k + 1, cols] for k in range(6)]
            d = geom[g, at[0], cols]
            a1, a2, a3 = [trio[g, at[c], cols] for c in range(3)]
            corr[8 * j : 8 * j + 8, cols] = (
                a1 * (n1 - y * n2 + d * n3)
                + a2 * (x * n2 - n0 + d * n4)
                - a3 * (y * n0 - x * n1 + d * n5)
            )
    fix[...] += summed(corr[...], hot[g])


def solve(matrix, right):
    factor = {}
    for i in range(6):
        for j in range(i + 1):
            e = matrix(i, j)
            if i == j:
                e = e * 1.1 + 0.001
            for k in range(j):
                e = e - factor[i, k] * factor[j, k]
            factor[i, j] = jnp.sqrt(e) if i == j else e / factor[j, j]
    forward = []
    for i in range(6):
        e = right(i)
        for k in range(i):
            e = e - factor[i, k] * forward[k]
        forward.append(e / factor[i, i])
    z = [None] * 6
    for i in reversed(range(6)):
        e = forward[i]
        for k in range(i + 1, 6):
            e = e - factor[k, i] * z[k]
        z[i] = e / factor[i, i]
    return z


def partner(k):
    row, col = lax.axis_index("row"), lax.axis_index("col")
    z = (row + k // 32) % 4
    y = (col // 8 + (k // 8) % 4) % 4
    x = ((col // 2) % 4 + (k // 2) % 4) % 4
    c = (col + k) % 2
    return z, y * 8 + x * 2 + c


def send_all(copy_to):
    def step(n, carry):
        copy_to(*partner((n * 37) % 128)).start()
        return carry

    lax.fori_loop(1, NDEV, step, 0)


def rows_exchange(send, recv, slot, send_sem, recv_sem):
    def copy_to(row, col):
        d = row * 32 + col
        return pltpu.make_async_remote_copy(
            src_ref=send.at[pl.ds(d, 1), :],
            dst_ref=recv.at[pl.ds(slot, 1), :],
            send_sem=send_sem,
            recv_sem=recv_sem,
            device_id=(row, col),
            device_id_type=MESH,
        )

    send_all(copy_to)


def rows_wait(buf, sem):
    ref = buf.at[pl.ds(0, NDEV - 1), :]
    pltpu.make_async_copy(ref, ref, sem).wait()


def main_kernel(
    packed, out_ref, pose_ref,
    recv, comps, extras, table, hot, geom, rel, both, sums, inverse, trio,
    rows_kh, total, steps, corr, fix,
    send_d, recv_d, send_e, recv_e, send_f, recv_f,
    big_send, big_recv, own_sem, small_send, small_recv,
):
    row, col = lax.axis_index("row"), lax.axis_index("col")
    me = row * 32 + col
    lane = lane_iota()

    def chunk_to(r, c):
        return pltpu.make_async_remote_copy(
            src_ref=packed.at[r * 32 + c],
            dst_ref=recv.at[me],
            send_sem=big_send,
            recv_sem=big_recv.at[me],
            device_id=(r, c),
            device_id_type=MESH,
        )

    own = pltpu.make_async_copy(packed.at[me], recv.at[me], big_recv.at[me])
    own.start()
    send_all(chunk_to)
    table[...] = jnp.zeros_like(table)
    sums[...] = jnp.zeros_like(sums)
    total[...] = jnp.zeros_like(total)
    fix[...] = jnp.zeros_like(fix)
    rows_kh[...] = jnp.zeros_like(rows_kh)

    def loop(body):
        def step(g, carry):
            body(g)
            return carry

        lax.fori_loop(0, GROUPS, step, 0)

    def arrive(g):
        for i in range(8):
            s = 8 * g + i
            pltpu.make_async_copy(packed.at[s], recv.at[s], big_recv.at[s]).wait()
        unpack_group(g, recv, comps, extras, table)

    loop(arrive)
    loop(lambda g: first_pass(g, me, comps, extras, table, hot, geom, rel, both, sums))
    ci = 1.0 / (0.1 + sums[24:48])
    inverse[0:24] = ci
    inverse[24:48] = sums[0:24] * ci
    loop(lambda g: second_pass(g, me, comps, geom, rel, hot, inverse, trio, rows_kh, total))

    send_d[...] = jnp.concatenate(
        [total[:, 0:128], total[:, 128:256], jnp.zeros((64, 128), F32)], 0
    ).T
    recv_d[pl.ds(me, 1), :] = send_d[pl.ds(me, 1), :]
    rows_exchange(send_d, recv_d, me, small_send.at[0], small_recv.at[0])
    rows_wait(recv_d, small_recv.at[0])
    line = jnp.sum(recv_d[...], axis=0, keepdims=True)
    sub = lax.broadcasted_iota(jnp.int32, (8, 128), 0)
    lines = jnp.broadcast_to(line, (8, 128))
    lines = jnp.where(sub == 1, pltpu.roll(lines, 96, 1), lines)
    full = jnp.concatenate([lines, jnp.zeros((120, 128), F32)], 0).T
    z = solve(
        lambda i, j: full[K_INDEX[i, j] : K_INDEX[i, j] + 1, :],
        lambda i: full[H_ROW + i : H_ROW + i + 1, :],
    )
    zs = jnp.concatenate([*z, jnp.zeros((122, 128), F32)], 0)
    pose_ref[...] = zs[0:6, 0:2]
    turned = zs.T
    mine = turned[0:1] + pltpu.roll(turned[0:8], 8, 1)[1:2]
    send_e[...] = jnp.broadcast_to(mine, (8, 128))
    recv_e[pl.ds(me, 1), :] = mine

    def step_to(r, c):
        return pltpu.make_async_remote_copy(
            src_ref=send_e.at[pl.ds(0, 1), :],
            dst_ref=recv_e.at[pl.ds(me, 1), :],
            send_sem=small_send.at[1],
            recv_sem=small_recv.at[1],
            device_id=(r, c),
            device_id_type=MESH,
        )

    send_all(step_to)
    rows_wait(recv_e, small_recv.at[1])
    every = recv_e[...].T
    steps[:, 0:128] = every[0:8]
    steps[:, 128:256] = every[8:16]
    loop(lambda g: third_pass(g, me, geom, trio, hot, steps, corr, fix))
    grad = sums[0:24]
    new = table[0:24] + (grad - fix[...]) * inverse[0:24]
    zero8 = jnp.zeros((8, 128), F32)
    send_f[...] = jnp.concatenate(
        [new[:, 0:128], zero8, new[:, 128:256], zero8, jnp.zeros((64, 128), F32)], 0
    ).T
    slot = (me % 16) * 8 + me // 16
    recv_f[pl.ds(slot, 1), :] = send_f[pl.ds(me, 1), :]
    rows_exchange(send_f, recv_f, slot, small_send.at[2], small_recv.at[2])
    rows_wait(recv_f, small_recv.at[2])
    for f in range(2):
        tiles = [None] * 3
        for i in range(16):
            piece = recv_f[8 * i : 8 * i + 8, :]
            first = 24 * i
            moved = pltpu.roll(piece, (first - 32 * f) % 128, 1)
            for t in range(3):
                a, b = max(first - 128 * t, 0), min(first + 24 - 128 * t, 128)
                if a < b:
                    if tiles[t] is None:
                        tiles[t] = moved
                    else:
                        tiles[t] = jnp.where((lane >= a) & (lane < b), moved, tiles[t])
        for g in range(8):
            for t in range(3):
                at = 384 * g + 128 * t
                out_ref[f : f + 1, at : at + 128] = tiles[t][g : g + 1]

    ref = packed.at[pl.ds(0, NDEV - 1)]
    pltpu.make_async_copy(ref, ref, big_send).wait()
    rows_wait(recv_d, small_send.at[0])
    rows_wait(recv_e, small_send.at[1])
    rows_wait(recv_f, small_send.at[2])


def run_main(packed):
    v = pltpu.VMEM
    return pl.pallas_call(
        main_kernel,
        in_specs=[pl.BlockSpec(memory_space=pl.ANY)],
        out_specs=[pl.BlockSpec(memory_space=pltpu.VMEM)] * 2,
        out_shape=[
            jax.ShapeDtypeStruct((2, PX * NDEV), F32),
            jax.ShapeDtypeStruct((6, 2), F32),
        ],
        scratch_shapes=[
            v((NDEV, 40, 128), F32),
            v((GROUPS, 96, LANES), F32),
            v((GROUPS, 8, LANES), F32),
            v((32, 256), F32),
            v((GROUPS, 256, LANES), BF16),
            v((GROUPS, 96, LANES), F32),
            v((GROUPS, 8, LANES), F32),
            v((48, LANES), F32),
            v((48, 256), F32),
            v((48, 256), F32),
            v((GROUPS, 72, LANES), F32),
            v((32, LANES), F32),
            v((32, 256), F32),
            v((8, 256), F32),
            v((24, LANES), F32),
            v((24, 256), F32),
            v((128, 128), F32),
            v((128, 128), F32),
            v((8, 128), F32),
            v((128, 128), F32),
            v((128, 128), F32),
            v((128, 128), F32),
            pltpu.SemaphoreType.DMA,
            pltpu.SemaphoreType.DMA((NDEV,)),
            pltpu.SemaphoreType.DMA,
            pltpu.SemaphoreType.DMA((3,)),
            pltpu.SemaphoreType.DMA((3,)),
        ],
        compiler_params=pltpu.CompilerParams(
            has_side_effects=True, vmem_limit_bytes=48 * 1024 * 1024
        ),
        name="step",
    )(packed)


def shards(inv_depth, rotation, translation, edge_target, flow_obs, weight):
    pixels = inv_depth.shape[1]
    flow = flow_obs.reshape(2, 48, pixels)
    wts = weight.reshape(2, 48, pixels)
    target = edge_target.reshape(1, 48)
    target = ((target % 2) * 128 + target // 2).astype(F32)
    pose = jnp.repeat(jnp.concatenate([rotation, translation], 0), 24, axis=1)
    extra = jnp.pad(jnp.concatenate([target, pose], 0), ((0, 1), (64, 16)))
    depth8 = jnp.tile(inv_depth, (4, 1))
    return run_main(pack(flow, wts, depth8, extra))


def solution(mesh):
    in_specs = (
        P(("row", "col"), None),
        P(None, ("row", "col")),
        P(None, ("row", "col")),
        P(("row", "col"), None),
        P(None, ("row", "col"), None, None),
        P(None, ("row", "col"), None, None),
    )
    out_specs = (P(("row", "col"), None), P(None, ("row", "col")))
    return jax.shard_map(
        shards, mesh=mesh, in_specs=in_specs, out_specs=out_specs, check_vma=False
    )
```

time: 473 us -> 117 us (0.25); the launches traced: 464 us -> 117 us
  waiting for transfers between devices: 145 us -> 0 us
  Pallas kernels: 0 us -> 109 us
  matrix products: 101 us -> 0 us
  blocking collectives: 96.5 us -> 0 us
  other arithmetic: 43.8 us -> 1.46 us
  local copies, waits for them, and re-layouts: 41.3 us -> 5.47 us
  starting transfers between devices: 35 us -> 0 us
    pallas_call x0 -> x2, Pallas kernels: none -> 109 us  [the longest x1 102 us: run_main(): pl.pallas_call(main_kernel, in_specs=[pl.BlockSpec(memory_space=pl.ANY)],...]
    dot_general x13 -> x0, matrix products: 101 us -> none  [the longest x1 18.1 us: edge_terms(): jnp.einsum('aep,bep->eab', scaled_v, jac_v, precision=PRECISE)]
    ppermute x8 -> x0, waiting for transfers between devices: 94.7 us -> none  [the longest x4 47.1 us: from_behind(): lax.ppermute(shard, axis, [(i, (i + by) % devices) for i in range(devices)])]
    psum x4 -> x0, blocking collectives: 58.6 us -> none  [one_axis_at_a_time(): shard = lax.psum(shard, axis)]
    all_to_all x4 -> x0, waiting for transfers between devices: 49.8 us -> none  [the longest x2 32.3 us: sent_and_summed(): lax.all_to_all(split_up(shard, dim, devices), axis, 0, 0, tiled=True)]
    all_gather x1 -> x0, blocking collectives: 37.9 us -> none  [gather_turned(): result, at, outs = (lax.all_gather(both, axis, axis=0, tiled=True), 0, [])]
    all_to_all x4 -> x0, starting transfers between devices: 25.4 us -> none  [the longest x2 14.3 us: copy_for_each(): lax.all_to_all(jnp.broadcast_to(shard[None], (devices, *shard.shape)), ax...]
    unnamed x9 -> x0, other arithmetic: 10.3 us -> none
  transfers between devices with their start and end apart: 12 -> 0, of which waited for: 10 -> 0; matrix products, arithmetic and copies ran while one was open for 6% -> 0% of each run, Pallas kernels for 0% -> 0%
where the time goes in v1:
time: 117 us
  Pallas kernels  109 us (93%)
  local copies, waits for them, and re-layouts  5.47 us (5%)
  other arithmetic  1.46 us (1%)
    pallas_call x1, Pallas kernels, run_main(): pl.pallas_call(main_kernel, in_specs=[pl.BlockSpec(memory_space=pl.ANY)],...  102 us
    pallas_call x1, Pallas kernels, pack(): pl.pallas_call(pack_kernel, grid=(8,), in_specs=[pl.BlockSpec((2, 48, LAN...  6.92 us
    unnamed x3, local copies, waits for them, and re-layouts  2.35 us

profile of v1, /device:TPU:1, one launch (start us, length us, event | category | flops | bytes accessed | tf_op | source)
XLA Modules:
  0.0 116.9 jit_solution(21696911613744322)
XLA Ops:
  0.6 0.8 reshape.168
  1.4 0.8 pad_maximum_fusion
  2.2 0.1 copy.8
  2.3 0.1 broadcast_in_dim.3
  2.3 0.1 reshape.169
  2.4 0.7 select_maximum_fusion.extra_ref
  3.1 0.8 tile.4
  3.9 0.7 tile.10.depth_ref
  4.6 6.9 %pack.1.packed = f32[128,40,128]{2,1,0:T(8,128)} custom-call(f32[2,48,3072]{2,1,0:T(8,128)} %bitcast.2, f32[2,48,3072]{2,1,0:T(8,128)} %bitcast.3, f32[8,3072]{1,0:T(8,128)} %tile.10.depth_ref, f32[8,128]{1,0:T(8,128)} %select_maximum_fusion.extra_ref), custom_call_target="tpu_custom_call" | custom-call | tf_op jit(solution)/shard_map/pack/pallas_call | solution.py:65
  11.5 0.0 copy-start
  11.5 1.7 %copy-done = f32[128,40,128]{2,1,0:T(8,128)S(1)} copy-done((f32[128,40,128]{2,1,0:T(8,128)S(1)}, f32[128,40,128]{2,1,0:T(8,128)}, u32[]{:S(2)}) %copy-start) | copy-done | bytes 2621464
  13.2 102.5 %step.1 = (f32[2,3072]{1,0:T(2,128)S(1)}, f32[6,2]{1,0:T(8,128)S(1)}) custom-call(f32[128,40,128]{2,1,0:T(8,128)S(1)} %copy-done), custom_call_target="tpu_custom_call" | custom-call | tf_op jit(solution)/shard_map/step/pallas_call | solution.py:486
  115.7 0.6 copy.9
  116.3 0.6 copy.11
  (1 shorter events, 0.0 us)
Async XLA Ops:
  11.5 1.7 %copy-start = (f32[128,40,128]{2,1,0:T(8,128)S(1)}, f32[128,40,128]{2,1,0:T(8,128)}, u32[]{:S(2)}) copy-start(f32[128,40,128]{2,1,0:T(8,128)} %pack.1.packed) | copy-start | bytes 7864324

commit v2 on v1

v2 whole, which is shorter than its diff:
```python
import contextlib

import jax
import jax.numpy as jnp
from jax import lax
from jax.experimental import pallas as pl
from jax.experimental.pallas import tpu as pltpu
from jax.sharding import PartitionSpec as P

F32 = jnp.float32
BF16 = jnp.bfloat16
NDEV = 128
PX = 24
GROUPS = 16
LANES = 384
MESH = pl.DeviceIdType.MESH
PAIRS = [(a, b) for a in (0, 1, 2, 5) for b in (0, 1, 2, 5) if a <= b]
K_ROWS = [*PAIRS, *[(3, b) for b in range(6)], *[(4, b) for b in (0, 1, 2, 4, 5)]]
K_INDEX = {}
for _n, (_a, _b) in enumerate(K_ROWS):
    K_INDEX[_a, _b] = _n
    K_INDEX[_b, _a] = _n
H_ROW = 21


def lane_iota(shape=(8, 128)):
    return lax.broadcasted_iota(jnp.int32, shape, 1)


def pack_block(n, turn, flow, weight, depth, extra, low, high, out):
    cols = pl.ds(pl.multiple_of(n * LANES, 128), LANES)

    def put(ref, block, value):
        at = pl.multiple_of(((3 * turn + block) % 8) * 16, 16)
        ref[pl.ds(at, 16), :] = value

    for k in range(3):
        put(low, k, flow[0, 16 * k : 16 * k + 16, cols])
        put(low, 3 + k, flow[1, 16 * k : 16 * k + 16, cols])
        put(high, 1 + k, weight[1, 16 * k : 16 * k + 16, cols])
    put(low, 6, weight[0, 0:16, cols])
    put(low, 7, weight[0, 16:32, cols])
    put(high, 0, weight[0, 32:48, cols])
    low_t = low[...].T
    high_t = high[...].T
    where_at = (lane_iota() - 48 * turn + 384) % 128
    for d in range(16):
        base = 24 * d
        to = 16 * n + d
        for j in range(3):
            out[to, 8 * j : 8 * j + 8, :] = low_t[base + 8 * j : base + 8 * j + 8]
        u0 = high_t[base : base + 8]
        u1 = high_t[base + 8 : base + 16]
        u2 = high_t[base + 16 : base + 24]
        out[to, 24:32, :] = jnp.where(where_at < 64, u0, pltpu.roll(u1, 64, 1))
        out[to, 32:40, :] = jnp.where(where_at < 64, u2, extra)


def own_edges(target_ref, rotation_ref, translation_ref, ints, floats):
    lane = lane_iota()
    sub = lax.broadcasted_iota(jnp.int32, (8, 128), 0)
    ints[...] = jnp.zeros_like(ints)
    ints[0:2, 0:24] = target_ref[...]
    both = ints[...]
    target = jnp.where(lane < 24, both[0:1], pltpu.roll(both, 24, 1)[1:2])
    target = ((target % 2) * 128 + target // 2).astype(F32)
    floats[...] = jnp.zeros_like(floats)
    floats[0, 0:2, 0:3] = rotation_ref[...]
    floats[1, 0:2, 0:3] = translation_ref[...]
    pose = floats[0] + pltpu.roll(floats[1], 3, 1)
    column = jnp.concatenate([pose, jnp.zeros((120, 128), F32)], 0).T[0:8]
    spread = jnp.where(lane < 24, column[:, 0:1], column[:, 1:2])
    return jnp.where(sub == 6, target, spread), pose


def pack_tables(depth_ref, pose, unfold, send):
    lane = lane_iota()
    poses = pltpu.roll(pose, 48, 1)[0:1] + pltpu.roll(pose, 56, 1)[1:2]
    for f in range(2):
        for g in range(8):
            unfold[f, g : g + 1, :] = depth_ref[f : f + 1, LANES * g : LANES * g + LANES]
    for i in range(16):
        acc = jnp.broadcast_to(poses, (8, 128))
        for f in range(2):
            for t in range(3):
                a, b = max(24 * i - 128 * t, 0), min(24 * i + 24 - 128 * t, 128)
                if a < b:
                    shift = 24 * f - (24 * i - 128 * t)
                    moved = pltpu.roll(unfold[f, :, 128 * t : 128 * t + 128], shift % 128, 1)
                    acc = jnp.where((lane >= a + shift) & (lane < b + shift), moved, acc)
        send[8 * i : 8 * i + 8, :] = acc


def strip(tiles, lane, offset, width):
    out = []
    for t in range(3):
        acc = None
        for i in range(8):
            start = 48 * i + offset
            for wrap in (0, 384, 768):
                a = max(start - wrap, 128 * t) - 128 * t
                b = min(start + width - wrap, 128 * t + 128) - 128 * t
                if a < b:
                    if acc is None:
                        acc = tiles[i]
                    else:
                        acc = jnp.where((lane >= a) & (lane < b), tiles[i], acc)
        out.append(acc)
    return out


def shifted(tiles, lane, shift):
    whole, part = divmod(shift % 384, 128)
    if part == 0:
        return [tiles[(t - whole) % 3] for t in range(3)]
    rolled = [pltpu.roll(t, part, 1) for t in tiles]
    return [
        jnp.where(lane < part, rolled[(t - whole - 1) % 3], rolled[(t - whole) % 3])
        for t in range(3)
    ]


def split3(x):
    top = x.astype(BF16).astype(F32)
    rest = x - top
    mid = rest.astype(BF16).astype(F32)
    return jnp.concatenate([top, mid, rest - mid], 0).astype(BF16)


def join3(y):
    n = y.shape[0] // 3
    return y[:n] + y[n : 2 * n] + y[2 * n :]


def gathered(table, hot):
    return join3(jnp.dot(split3(table), hot, preferred_element_type=F32))


def summed(values, hot):
    return join3(
        lax.dot_general(
            split3(values), hot, (((1,), (1,)), ((), ())), preferred_element_type=F32
        )
    )


def unpack_group(g, recv, comps, extras):
    lane = lane_iota()
    block_lane = [(lane + 128 * t) % 48 for t in range(3)]
    srcs = [8 * g + i for i in range(8)]
    tile3 = [recv[s, 24:32, :] for s in srcs]
    tile4 = [recv[s, 32:40, :] for s in srcs]
    for j in range(3):
        low = [recv[s, 8 * j : 8 * j + 8, :] for s in srcs]
        high = (tile3, tile3, tile4)[j]
        at = (0, 64, 0)[j]
        first = shifted(strip(low, lane, 96, 32), lane, -96)
        second = shifted(strip(high, lane, at, 16), lane, 32 - at)
        parts = [
            strip(low, lane, 0, 48),
            shifted(strip(low, lane, 48, 48), lane, -48),
            [jnp.where(b < 32, f, s) for b, f, s in zip(block_lane, first, second)],
            shifted(strip(high, lane, at + 16, 48), lane, -16 - at),
        ]
        for c, tiles in enumerate(parts):
            for t in range(3):
                comps[g, 24 * c + 8 * j : 24 * c + 8 * j + 8, 128 * t : 128 * t + 128] = tiles[t]
    for t, tile in enumerate(shifted(strip(tile4, lane, 64, 48), lane, -64)):
        extras[g, :, 128 * t : 128 * t + 128] = tile


def pixel_xy(me, j):
    p = me * PX + 8 * j + lax.broadcasted_iota(jnp.int32, (8, 128), 0)
    x = ((p % 64).astype(F32) + 0.5) / 64 - 0.5
    y = ((p // 64).astype(F32) + 0.5 - 24.0) / 64
    return x, y


def first_pass(g, me, comps, extras, table, hot, geom, rel, both, sums):
    target = extras[g, 6:7, :]
    rows = lax.broadcasted_iota(jnp.int32, (256, LANES), 0).astype(F32)
    hot[g] = jnp.where(rows == target, 1.0, 0.0).astype(BF16)
    near = gathered(table[...], hot[g])
    rel[g] = extras[g] - near[24:32]
    for j in range(3):
        x, y = pixel_xy(me, j)
        for t in range(3):
            cols = slice(128 * t, 128 * t + 128)
            w0, w1, w2, m0, m1, m2 = [rel[g, k : 1 + k, cols] for k in range(6)]
            at = [slice(24 * c + 8 * j, 24 * c + 8 * j + 8) for c in range(4)]
            d = near[8 * j : 8 * j + 8, cols]
            x0 = x + w1 - w2 * y + m0 * d
            x1 = y + w2 * x - w0 + m1 * d
            x2 = 1.0 + w0 * y - w1 * x + m2 * d
            q = 1.0 / x2
            u = x0 * q
            v = x1 * q
            ru = comps[g, at[0], cols] - (u - x)
            rv = comps[g, at[1], cols] - (v - y)
            du = q * (m0 - u * m2)
            dv = q * (m1 - v * m2)
            eu = comps[g, at[2], cols] * du
            ev = comps[g, at[3], cols] * dv
            comps[g, at[0], cols] = ru
            comps[g, at[1], cols] = rv
            geom[g, at[0], cols] = d
            geom[g, at[1], cols] = q
            geom[g, at[2], cols] = u
            geom[g, at[3], cols] = v
            both[8 * j : 8 * j + 8, cols] = eu * ru + ev * rv
            both[24 + 8 * j : 32 + 8 * j, cols] = eu * du + ev * dv
    sums[...] += summed(both[...], hot[g])


def source_columns():
    rows = lax.broadcasted_iota(jnp.int32, (128, LANES), 0)
    frame = lax.broadcasted_iota(jnp.int32, (1, LANES), 1) // 24
    return jnp.where(rows == (frame % 2) * 8 + frame // 2, 1.0, 0.0).astype(BF16)


def second_pass(g, me, comps, geom, rel, hot, own, inverse, trio, rows_kh, total_s, total_t):
    near = gathered(inverse[...], hot[g])
    for t in range(3):
        cols = slice(128 * t, 128 * t + 128)
        acc = [None] * 27
        m0, m1, m2 = [rel[g, 3 + k : 4 + k, cols] for k in range(3)]

        def add(row, value):
            acc[row] = value if acc[row] is None else acc[row] + value

        for j in range(3):
            x, y = pixel_xy(me, j)
            at = [slice(24 * c + 8 * j, 24 * c + 8 * j + 8) for c in range(4)]
            d, q, u, v = [geom[g, at[c], cols] for c in range(4)]
            ru, rv, cu, cv = [comps[g, at[c], cols] for c in range(4)]
            ci = near[8 * j : 8 * j + 8, cols]
            gi = near[24 + 8 * j : 32 + 8 * j, cols]
            du = q * (m0 - u * m2)
            dv = q * (m1 - v * m2)
            eu = cu * du
            ev = cv * dv
            a1 = eu * q
            a2 = ev * q
            trio[g, at[0], cols] = a1
            trio[g, at[1], cols] = a2
            trio[g, at[2], cols] = a1 * u + a2 * v
            qq = q * q
            iu = ci * eu
            alpha = (cu - iu * eu) * qq
            gamma = (iu * ev) * qq
            beta = (cv - ci * ev * ev) * qq
            hu = (cu * ru - eu * gi) * q
            hv = (cv * rv - ev * gi) * q
            nd = -d
            ju = {0: -(u * y), 1: 1.0 + u * x, 2: -y, 5: u * nd}
            jv = {0: -1.0 - v * y, 1: v * x, 2: x, 5: v * nd}
            gd = gamma * d
            pp = {b: alpha * ju[b] - gamma * jv[b] for b in ju}
            qb = {b: beta * jv[b] - gamma * ju[b] for b in ju}
            pp[3], pp[4] = alpha * d, -gd
            qb[4] = beta * d
            for a, b in PAIRS:
                add(K_INDEX[a, b], ju[a] * pp[b] + jv[a] * qb[b])
            for b in range(6):
                add(K_INDEX[3, b], d * pp[b])
            for b in (0, 1, 2, 4, 5):
                add(K_INDEX[4, b], d * qb[b])
            for b in ju:
                add(H_ROW + b, ju[b] * hu + jv[b] * hv)
            add(H_ROW + 3, d * hu)
            add(H_ROW + 4, d * hv)
        for row in range(27):
            rows_kh[row : row + 1, cols] = jnp.sum(acc[row], axis=0, keepdims=True)
    values = rows_kh[...]
    total_t[...] += summed(values, hot[g])
    by_source = summed(values, own[...])
    lane = lane_iota((32, 128))
    for f in range(2):
        at = slice(128 * f, 128 * f + 128)
        moved = pltpu.roll(by_source, (8 * g - 8 * f + 128) % 128, 1)
        total_s[:, at] = jnp.where(lane // 8 == g, moved, total_s[:, at])


def third_pass(g, me, geom, trio, hot, own, steps, corr, fix):
    lane = lane_iota()
    mine = jnp.where(
        lane < 8,
        pltpu.roll(steps[:, 0:128], (128 - 8 * g) % 128, 1),
        pltpu.roll(steps[:, 128:256], (136 - 8 * g) % 128, 1),
    )
    motion = gathered(mine, own[...]) - gathered(steps[...], hot[g])
    for j in range(3):
        x, y = pixel_xy(me, j)
        for t in range(3):
            cols = slice(128 * t, 128 * t + 128)
            at = [slice(24 * c + 8 * j, 24 * c + 8 * j + 8) for c in range(3)]
            n0, n1, n2, n3, n4, n5 = [motion[k : k + 1, cols] for k in range(6)]
            d = geom[g, at[0], cols]
            a1, a2, a3 = [trio[g, at[c], cols] for c in range(3)]
            corr[8 * j : 8 * j + 8, cols] = (
                a1 * (n1 - y * n2 + d * n3)
                + a2 * (x * n2 - n0 + d * n4)
                - a3 * (y * n0 - x * n1 + d * n5)
            )
    fix[...] += summed(corr[...], hot[g])


def solve(matrix, right):
    factor = {}
    for i in range(6):
        for j in range(i + 1):
            e = matrix(i, j)
            if i == j:
                e = e * 1.1 + 0.001
            for k in range(j):
                e = e - factor[i, k] * factor[j, k]
            factor[i, j] = jnp.sqrt(e) if i == j else e / factor[j, j]
    forward = []
    for i in range(6):
        e = right(i)
        for k in range(i):
            e = e - factor[i, k] * forward[k]
        forward.append(e / factor[i, i])
    z = [None] * 6
    for i in reversed(range(6)):
        e = forward[i]
        for k in range(i + 1, 6):
            e = e - factor[k, i] * z[k]
        z[i] = e / factor[i, i]
    return z


def ring_steps(d):
    return min(d, 4 - d)


def far_first():
    offsets = [
        (dz, dy, dx, dc)
        for dz in range(4)
        for dy in range(4)
        for dx in range(4)
        for dc in range(2)
        if (dz, dy, dx, dc) != (0, 0, 0, 0)
    ]
    return sorted(offsets, key=lambda o: -(ring_steps(o[0]) + ring_steps(o[1]) + ring_steps(o[2])))


def group_offset(n):
    return (n // 4 + n) % 4, n % 4


def by_group():
    return [
        (*group_offset(n), dx, dc)
        for n in range(GROUPS)
        for dx in range(4)
        for dc in range(2)
        if (n, dx, dc) != (0, 0, 0)
    ]


def to_all(order, act):
    row, col = lax.axis_index("row"), lax.axis_index("col")
    zs = [((row + d) % 4) * 32 for d in range(4)]
    ys = [((col // 8 + d) % 4) * 8 for d in range(4)]
    xs = [((col // 2 + d) % 4) * 2 for d in range(4)]
    cs = [(col + d) % 2 for d in range(2)]
    for dz, dy, dx, dc in order:
        act(zs[dz] + ys[dy] + xs[dx] + cs[dc])


def slot_of(d):
    return (d % 16) * 8 + d // 16


def rows_exchange(send, recv, source, slot, send_sem, recv_sem):
    def act(d):
        pltpu.make_async_remote_copy(
            src_ref=send.at[pl.ds(source(d), 1), :],
            dst_ref=recv.at[pl.ds(slot, 1), :],
            send_sem=send_sem,
            recv_sem=recv_sem,
            device_id=d,
            device_id_type=pl.DeviceIdType.LOGICAL,
        ).start()

    to_all(far_first(), act)


def rows_wait(buf, sem):
    ref = buf.at[pl.ds(0, NDEV - 1), :]
    pltpu.make_async_copy(ref, ref, sem).wait()


def scope(name):
    return contextlib.nullcontext()


def loop(body):
    def step(g, carry):
        body(g)
        return carry

    lax.fori_loop(0, GROUPS, step, 0)


def main_kernel(
    flow_hbm, weight_hbm, depth_ref, target_ref, rotation_ref, translation_ref,
    out_ref, pose_ref,
    flow, weight, low, high, chunks, ints, floats, unfold,
    recv, comps, extras, table, hot, own, geom, rel, both, sums, inverse, trio,
    rows_kh, total_s, total_t, steps, corr, fix,
    send_t, recv_t, send_d, recv_d, send_e, recv_e, send_f, recv_f,
    in_sem, own_sem, big_send, big_recv, small_send, small_recv,
):
    row, col = lax.axis_index("row"), lax.axis_index("col")
    me = row * 32 + col
    lane = lane_iota()
    barrier = pltpu.get_barrier_semaphore()

    loads = [
        pltpu.make_async_copy(flow_hbm, flow, in_sem.at[0]),
        pltpu.make_async_copy(weight_hbm, weight, in_sem.at[1]),
    ]
    for load in loads:
        load.start()

    def greet(d):
        pl.semaphore_signal(
            barrier, inc=1, device_id=d, device_id_type=pl.DeviceIdType.LOGICAL
        )

    with scope("sc_greet"):
        to_all(far_first(), greet)

    with scope("sc_tables"):
        table[...] = jnp.zeros_like(table)
        sums[...] = jnp.zeros_like(sums)
        total_t[...] = jnp.zeros_like(total_t)
        total_s[...] = jnp.zeros_like(total_s)
        fix[...] = jnp.zeros_like(fix)
        rows_kh[...] = jnp.zeros_like(rows_kh)
        own[...] = source_columns()
        high[...] = jnp.zeros_like(high)
        extra, pose = own_edges(target_ref, rotation_ref, translation_ref, ints, floats)
        pack_tables(depth_ref, pose, unfold, send_t)
        recv_t[pl.ds(me, 1), :] = send_t[pl.ds(slot_of(me), 1), :]
        turn = col % 8
        extra = pltpu.roll(extra, (64 + 48 * turn) % 128, 1)
        for load in loads:
            load.wait()

    def pack(n, carry):
        pack_block(n, turn, flow, weight, depth_ref, extra, low, high, chunks)
        return carry

    with scope("sc_pack"):
        lax.fori_loop(0, 8, pack, 0)
    with scope("sc_barrier"):
        pl.semaphore_wait(barrier, NDEV - 1)

    with scope("sc_sends"):
        rows_exchange(send_t, recv_t, slot_of, me, small_send.at[3], small_recv.at[3])

        def send_chunk(d):
            pltpu.make_async_remote_copy(
                src_ref=chunks.at[d],
                dst_ref=recv.at[me],
                send_sem=big_send,
                recv_sem=big_recv.at[me],
                device_id=d,
                device_id_type=pl.DeviceIdType.LOGICAL,
            ).start()

        to_all(by_group(), send_chunk)
        recv[me] = chunks[me]

    with scope("sc_waitt"):
        rows_wait(recv_t, small_recv.at[3])
        known = recv_t[...].T
        for f in range(2):
            at = slice(128 * f, 128 * f + 128)
            table[0:24, at] = known[24 * f : 24 * f + 24]
            table[24:32, at] = known[48 + 8 * f : 56 + 8 * f]

    def arrive(n):
        dz, dy = group_offset(n)
        g = ((row + 4 - dz) % 4) * 4 + (col // 8 + 4 - dy) % 4
        for i in range(8):
            s = 8 * g + i

            @pl.when(s != me)
            def _():
                pltpu.make_async_copy(chunks.at[s], recv.at[s], big_recv.at[s]).wait()

        unpack_group(g, recv, comps, extras)
        first_pass(g, me, comps, extras, table, hot, geom, rel, both, sums)

    with scope("sc_arrive"):
        loop(arrive)
    with scope("sc_second"):
        ci = 1.0 / (0.1 + sums[24:48])
        inverse[0:24] = ci
        inverse[24:48] = sums[0:24] * ci
        loop(
            lambda g: second_pass(
                g, me, comps, geom, rel, hot, own, inverse, trio, rows_kh, total_s, total_t
            )
        )

    with scope("sc_sendd"):
        kind = lax.broadcasted_iota(jnp.int32, (32, 256), 0)
        total = total_s[...] + jnp.where(kind < H_ROW, total_t[...], -total_t[...])
        send_d[...] = jnp.concatenate(
            [total[:, 0:128], total[:, 128:256], jnp.zeros((64, 128), F32)], 0
        ).T
        recv_d[pl.ds(me, 1), :] = send_d[pl.ds(me, 1), :]
        rows_exchange(send_d, recv_d, lambda d: d, me, small_send.at[0], small_recv.at[0])
    with scope("sc_waitd"):
        rows_wait(recv_d, small_recv.at[0])
    with scope("sc_solve"):
        line = jnp.sum(recv_d[...], axis=0, keepdims=True)
        sub = lax.broadcasted_iota(jnp.int32, (8, 128), 0)
        lines = jnp.broadcast_to(line, (8, 128))
        lines = jnp.where(sub == 1, pltpu.roll(lines, 96, 1), lines)
        full = jnp.concatenate([lines, jnp.zeros((120, 128), F32)], 0).T
        z = solve(
            lambda i, j: full[K_INDEX[i, j] : K_INDEX[i, j] + 1, :],
            lambda i: full[H_ROW + i : H_ROW + i + 1, :],
        )
        zs = jnp.concatenate([*z, jnp.zeros((122, 128), F32)], 0)
        turned = zs.T
        pose_ref[...] = turned[0:2, 0:6]
        mine = turned[0:1] + pltpu.roll(turned[0:8], 8, 1)[1:2]
        send_e[...] = jnp.broadcast_to(mine, (8, 128))
        recv_e[pl.ds(me, 1), :] = mine
    with scope("sc_sende"):
        rows_exchange(send_e, recv_e, lambda d: 0, me, small_send.at[1], small_recv.at[1])
    with scope("sc_waite"):
        rows_wait(recv_e, small_recv.at[1])
    with scope("sc_third"):
        every = recv_e[...].T
        steps[:, 0:128] = every[0:8]
        steps[:, 128:256] = every[8:16]
        loop(lambda g: third_pass(g, me, geom, trio, hot, own, steps, corr, fix))
    with scope("sc_sendf"):
        grad = sums[0:24]
        new = table[0:24] + (grad - fix[...]) * inverse[0:24]
        zero8 = jnp.zeros((8, 128), F32)
        send_f[...] = jnp.concatenate(
            [new[:, 0:128], zero8, new[:, 128:256], zero8, jnp.zeros((64, 128), F32)], 0
        ).T
        slot = slot_of(me)
        recv_f[pl.ds(slot, 1), :] = send_f[pl.ds(me, 1), :]
        rows_exchange(send_f, recv_f, lambda d: d, slot, small_send.at[2], small_recv.at[2])
    with scope("sc_waitf"):
        rows_wait(recv_f, small_recv.at[2])
    for f in range(2):
        tiles = [None] * 3
        for i in range(16):
            piece = recv_f[8 * i : 8 * i + 8, :]
            first = 24 * i
            moved = pltpu.roll(piece, (first - 32 * f) % 128, 1)
            for t in range(3):
                a, b = max(first - 128 * t, 0), min(first + 24 - 128 * t, 128)
                if a < b:
                    if tiles[t] is None:
                        tiles[t] = moved
                    else:
                        tiles[t] = jnp.where((lane >= a) & (lane < b), moved, tiles[t])
        for g in range(8):
            for t in range(3):
                at = 384 * g + 128 * t
                out_ref[f : f + 1, at : at + 128] = tiles[t][g : g + 1]

    ref = chunks.at[pl.ds(0, NDEV - 1)]
    pltpu.make_async_copy(ref, ref, big_send).wait()
    rows_wait(recv_t, small_send.at[3])
    rows_wait(recv_d, small_send.at[0])
    rows_wait(recv_e, small_send.at[1])
    rows_wait(recv_f, small_send.at[2])


def run_main(flow, weight, inv_depth, edge_target, rotation, translation):
    v = pltpu.VMEM
    vmem = pl.BlockSpec(memory_space=pltpu.VMEM)
    hbm = pl.BlockSpec(memory_space=pl.ANY)
    return pl.pallas_call(
        main_kernel,
        in_specs=[hbm, hbm, vmem, vmem, vmem, vmem],
        out_specs=[vmem] * 2,
        out_shape=[
            jax.ShapeDtypeStruct((2, PX * NDEV), F32),
            jax.ShapeDtypeStruct((2, 6), F32),
        ],
        scratch_shapes=[
            v((2, 48, PX * NDEV), F32),
            v((2, 48, PX * NDEV), F32),
            v((128, LANES), F32),
            v((128, LANES), F32),
            v((NDEV, 40, 128), F32),
            v((8, 128), jnp.int32),
            v((2, 8, 128), F32),
            v((2, 8, LANES), F32),
            v((NDEV, 40, 128), F32),
            v((GROUPS, 96, LANES), F32),
            v((GROUPS, 8, LANES), F32),
            v((32, 256), F32),
            v((GROUPS, 256, LANES), BF16),
            v((128, LANES), BF16),
            v((GROUPS, 96, LANES), F32),
            v((GROUPS, 8, LANES), F32),
            v((48, LANES), F32),
            v((48, 256), F32),
            v((48, 256), F32),
            v((GROUPS, 72, LANES), F32),
            v((32, LANES), F32),
            v((32, 256), F32),
            v((32, 256), F32),
            v((8, 256), F32),
            v((24, LANES), F32),
            v((24, 256), F32),
            v((128, 128), F32),
            v((128, 128), F32),
            v((128, 128), F32),
            v((128, 128), F32),
            v((8, 128), F32),
            v((128, 128), F32),
            v((128, 128), F32),
            v((128, 128), F32),
            pltpu.SemaphoreType.DMA((2,)),
            pltpu.SemaphoreType.DMA,
            pltpu.SemaphoreType.DMA,
            pltpu.SemaphoreType.DMA((NDEV,)),
            pltpu.SemaphoreType.DMA((4,)),
            pltpu.SemaphoreType.DMA((4,)),
        ],
        compiler_params=pltpu.CompilerParams(
            collective_id=0, has_side_effects=True, vmem_limit_bytes=56 * 1024 * 1024
        ),
        name="step",
    )(flow, weight, inv_depth, edge_target, rotation, translation)


def shards(inv_depth, rotation, translation, edge_target, flow_obs, weight):
    pixels = inv_depth.shape[1]
    flow = flow_obs.reshape(2, 48, pixels)
    wts = weight.reshape(2, 48, pixels)
    depth, pose = run_main(flow, wts, inv_depth, edge_target, rotation.T, translation.T)
    return depth, pose.T


def solution(mesh):
    in_specs = (
        P(("row", "col"), None),
        P(None, ("row", "col")),
        P(None, ("row", "col")),
        P(("row", "col"), None),
        P(None, ("row", "col"), None, None),
        P(None, ("row", "col"), None, None),
    )
    out_specs = (P(("row", "col"), None), P(None, ("row", "col")))
    return jax.shard_map(
        shards, mesh=mesh, in_specs=in_specs, out_specs=out_specs, check_vma=False
    )
```

time: 117 us -> 91.6 us (0.78)
  Pallas kernels: 109 us -> 88.1 us
  local copies, waits for them, and re-layouts: 5.47 us -> 2.58 us
  other arithmetic: 1.46 us -> 0 us
    pallas_call x2 -> x1, Pallas kernels: 109 us -> 88.1 us  [run_main(): pl.pallas_call(main_kernel, in_specs=[hbm, hbm, vmem, vmem, vmem, vmem],...]
    another operation x2 -> x0, local copies, waits for them, and re-layouts: 1.46 us -> none  [shards(): depth8 = jnp.tile(inv_depth, (4, 1))]
    concatenate x2 -> x0, other arithmetic: 1.44 us -> none  [the longest x1 0.77 us: shards(): pose = jnp.repeat(jnp.concatenate([rotation, translation], 0), 24, axis=1)]
    unnamed x3 -> x2, local copies, waits for them, and re-layouts: 2.35 us -> 2.58 us
where the time goes in v2:
time: 91.6 us; the launch traced here: 91.3 us
  Pallas kernels  88.1 us (96%)
  local copies, waits for them, and re-layouts  2.58 us (3%)
    pallas_call x1, Pallas kernels, run_main(): pl.pallas_call(main_kernel, in_specs=[hbm, hbm, vmem, vmem, vmem, vmem],...  88.1 us
    unnamed x2, local copies, waits for them, and re-layouts  2.58 us

profile of v2, /device:TPU:1, one launch (start us, length us, event | category | flops | bytes accessed | tf_op | source)
XLA Modules:
  0.0 91.3 jit_solution(239160070672087485)
XLA Ops:
  0.6 88.1 %step.1 = (f32[2,3072]{1,0:T(2,128)}, f32[2,6]{1,0:T(2,128)}) custom-call(f32[2,48,3072]{2,1,0:T(8,128)} %bitcast.5, f32[2,48,3072]{2,1,0:T(8,128)} %bitcast.6, f32[2,3072]{1,0:T(2,128)} %depth_ref.1, s32[2,24]{1,0:T(2,128)} %target_ref.1, f32[2,3]{1,0:T(2,128)} %bitcast.7, f32[2,3]{1,0:T(2,128)} %bitcast.8), custom_call_target="tpu_custom_call" | custom-call | tf_op jit(solution)/shard_map/step/pallas_call | solution.py:589
  88.8 1.3 %copy.10 = f32[2,3072]{1,0:T(2,128)} copy(f32[2,3072]{1,0:T(2,128)} %get-tuple-element.8) | data formatting | bytes 49152
  90.1 1.2 %copy.11 = f32[6,2]{0,1:T(2,128)} copy(f32[6,2]{0,1:T(2,128)} %bitcast.9) | data formatting | bytes 96

commit v3 on v2

v3 whole, which is shorter than its diff:
```python
import contextlib

import jax
import jax.numpy as jnp
from jax import lax
from jax.experimental import pallas as pl
from jax.experimental.pallas import tpu as pltpu
from jax.sharding import PartitionSpec as P

F32 = jnp.float32
BF16 = jnp.bfloat16
NDEV = 128
PX = 24
GROUPS = 16
LANES = 384
MESH = pl.DeviceIdType.MESH
K_PAIRS = [((a, b), n) for n, (a, b) in enumerate((a, b) for a in range(6) for b in range(a, 6))]
K_INDEX = {**dict(K_PAIRS), **{(b, a): n for (a, b), n in K_PAIRS}}
H_ROW = 21


def lane_iota(shape=(8, 128)):
    return lax.broadcasted_iota(jnp.int32, shape, 1)


def pack_block(n, turn, flow, weight, low, high, out):
    cols = pl.ds(pl.multiple_of(n * LANES, 128), LANES)

    def put(ref, block, value):
        at = pl.multiple_of(((3 * turn + block) % 8) * 16, 16)
        ref[pl.ds(at, 16), :] = value

    for k in range(3):
        put(low, k, flow[0, 16 * k : 16 * k + 16, cols])
        put(low, 3 + k, flow[1, 16 * k : 16 * k + 16, cols])
        put(high, 1 + k, weight[1, 16 * k : 16 * k + 16, cols])
    put(low, 6, weight[0, 0:16, cols])
    put(low, 7, weight[0, 16:32, cols])
    put(high, 0, weight[0, 32:48, cols])
    low_t = low[...].T
    high_t = high[...].T
    where_at = (lane_iota() - 48 * turn + 384) % 128
    for d in range(16):
        base = 24 * d
        to = 16 * n + d
        for j in range(3):
            out[to, 8 * j : 8 * j + 8, :] = low_t[base + 8 * j : base + 8 * j + 8]
        u0 = high_t[base : base + 8]
        u1 = high_t[base + 8 : base + 16]
        u2 = high_t[base + 16 : base + 24]
        out[to, 24:32, :] = jnp.where(where_at < 64, u0, pltpu.roll(u1, 64, 1))
        last = jnp.where(where_at < 64, u2, pltpu.roll(pltpu.roll(u2, 64, 1), 4, 0))
        out[to, 32:36, :] = last[0:4]


def own_edges(target_ref, rotation_ref, translation_ref, ints, floats):
    lane = lane_iota()
    ints[...] = jnp.zeros_like(ints)
    ints[0:2, 0:24] = target_ref[...]
    both = ints[...]
    target = jnp.where(lane < 24, both[0:1], pltpu.roll(both, 24, 1)[1:2])
    x, y, z = (target >> 2) & 3, (target >> 4) & 3, target >> 6
    group = (((z - x) & 3) << 2) + ((y - x) & 3)
    column = ((target & 1) << 7) + (group << 3) + ((target >> 1) & 7)
    floats[...] = jnp.zeros_like(floats)
    floats[0, 0:2, 0:3] = rotation_ref[...]
    floats[1, 0:2, 0:3] = translation_ref[...]
    return column.astype(F32), floats[0] + pltpu.roll(floats[1], 3, 1)


def pack_tables(depth_ref, column, pose, unfold, send):
    lane = lane_iota()
    poses = pltpu.roll(pose, 48, 1)[0:1] + pltpu.roll(pose, 56, 1)[1:2]
    known = jnp.where(lane < 64, poses, pltpu.roll(column, 64, 1)[0:1])
    for f in range(2):
        for g in range(8):
            unfold[f, g : g + 1, :] = depth_ref[f : f + 1, LANES * g : LANES * g + LANES]
    for i in range(16):
        acc = known
        for f in range(2):
            for t in range(3):
                a, b = max(24 * i - 128 * t, 0), min(24 * i + 24 - 128 * t, 128)
                if a < b:
                    shift = 24 * f - (24 * i - 128 * t)
                    moved = pltpu.roll(unfold[f, :, 128 * t : 128 * t + 128], shift % 128, 1)
                    acc = jnp.where((lane >= a + shift) & (lane < b + shift), moved, acc)
        send[8 * i : 8 * i + 8, :] = acc


def strip(tiles, lane, offset, width):
    out = []
    for t in range(3):
        acc = None
        for i in range(8):
            start = 48 * i + offset
            for wrap in (0, 384, 768):
                a = max(start - wrap, 128 * t) - 128 * t
                b = min(start + width - wrap, 128 * t + 128) - 128 * t
                if a < b:
                    if acc is None:
                        acc = tiles[i]
                    else:
                        acc = jnp.where((lane >= a) & (lane < b), tiles[i], acc)
        out.append(acc)
    return out


def shifted(tiles, lane, shift):
    whole, part = divmod(shift % 384, 128)
    if part == 0:
        return [tiles[(t - whole) % 3] for t in range(3)]
    rolled = [pltpu.roll(t, part, 1) for t in tiles]
    return [
        jnp.where(lane < part, rolled[(t - whole - 1) % 3], rolled[(t - whole) % 3])
        for t in range(3)
    ]


def split3(x):
    top = x.astype(BF16).astype(F32)
    rest = x - top
    mid = rest.astype(BF16).astype(F32)
    return jnp.concatenate([top, mid, rest - mid], 0).astype(BF16)


def join3(y):
    n = y.shape[0] // 3
    return y[:n] + y[n : 2 * n] + y[2 * n :]


def gathered(table, hot):
    return join3(jnp.dot(split3(table), hot, preferred_element_type=F32))


def summed(values, hot):
    return join3(
        lax.dot_general(
            split3(values), hot, (((1,), (1,)), ((), ())), preferred_element_type=F32
        )
    )


def unpack_group(g, recv, comps):
    lane = lane_iota()
    upper = lax.broadcasted_iota(jnp.int32, (8, 128), 0) >= 4
    block_lane = [(lane + 128 * t) % 48 for t in range(3)]
    srcs = [8 * g + i for i in range(8)]
    tile3 = [recv[s, 24:32, :] for s in srcs]
    tile4 = [recv[s, 32:40, :] for s in srcs]

    def piece(j, offset, width, to):
        def at(tiles, start):
            return shifted(strip(tiles, lane, start, width), lane, to - start)

        if j < 2:
            return at(tile3, offset + 64 * j)
        first, second = at(tile4, offset), at(tile4, offset + 64)
        return [jnp.where(upper, pltpu.roll(b, 4, 0), a) for a, b in zip(first, second)]

    for j in range(3):
        low = [recv[s, 8 * j : 8 * j + 8, :] for s in srcs]
        first = shifted(strip(low, lane, 96, 32), lane, -96)
        second = piece(j, 0, 16, 32)
        parts = [
            strip(low, lane, 0, 48),
            shifted(strip(low, lane, 48, 48), lane, -48),
            [jnp.where(b < 32, f, s) for b, f, s in zip(block_lane, first, second)],
            piece(j, 16, 48, 0),
        ]
        for c, tiles in enumerate(parts):
            for t in range(3):
                comps[24 * c + 8 * j : 24 * c + 8 * j + 8, 128 * t : 128 * t + 128] = tiles[t]


def group_targets(g, recv_t):
    lane = lane_iota()
    sub = lax.broadcasted_iota(jnp.int32, (8, 128), 0)
    tile = recv_t[pl.ds(pl.multiple_of(8 * g, 8), 8), :]
    out = [jnp.zeros((8, 128), F32)] * 3
    for i in range(8):
        moved = pltpu.roll(tile, (48 * i - 64) % 128, 1)
        for t in range(3):
            a, b = max(48 * i - 128 * t, 0), min(48 * i + 48 - 128 * t, 128)
            if a < b:
                out[t] = jnp.where((sub == i) & (lane >= a) & (lane < b), moved, out[t])
    return jnp.concatenate([jnp.sum(x, axis=0, keepdims=True) for x in out], 1)


def merge(items):
    sub = lax.broadcasted_iota(jnp.int32, (8, 128), 0)
    items = items[::-1]
    for bit in (0, 1, 2):
        step = 1 << bit
        here = (sub & step) != 0
        items = [
            jnp.where(here, a, b) + pltpu.roll(jnp.where(here, b, a), step, 0)
            for a, b in zip(items[0::2], items[1::2])
        ]
    return items[0]


def merged_rows(rows):
    rows = rows + [jnp.zeros((8, 128), F32)] * (32 - len(rows))
    return jnp.concatenate([merge(rows[k : k + 8]) for k in range(0, 32, 8)], 0)


def pixel_xy(me, j):
    p = me * PX + 8 * j + lax.broadcasted_iota(jnp.int32, (8, 128), 0)
    x = ((p % 64).astype(F32) + 0.5) / 64 - 0.5
    y = ((p // 64).astype(F32) + 0.5 - 24.0) / 64
    return x, y


def expanded(rows, g, own):
    lane = lane_iota()
    mine = jnp.where(
        lane < 8,
        pltpu.roll(rows[:, 0:128], (128 - 8 * g) % 128, 1),
        pltpu.roll(rows[:, 128:256], (136 - 8 * g) % 128, 1),
    )
    return gathered(mine, own[...])


def add_up(values, g, hot, own, total_s, total_t):
    total_t[...] += summed(values, hot[g])
    by_source = summed(values, own[...])
    lane = lane_iota((32, 128))
    for f in range(2):
        at = slice(128 * f, 128 * f + 128)
        moved = pltpu.roll(by_source, (8 * g - 8 * f + 128) % 128, 1)
        total_s[:, at] += jnp.where(lane // 8 == g, moved, 0.0)


def first_pass(g, me, comps, recv_t, table, hot, own, coup, sums, total_s, total_t):
    rows = lax.broadcasted_iota(jnp.int32, (256, LANES), 0).astype(F32)
    hot[g] = jnp.where(rows == group_targets(g, recv_t), 1.0, 0.0).astype(BF16)
    near = gathered(table[...], hot[g])
    rel = expanded(table[24:32, :], g, own) - near[24:32]
    grads, curvs, blocks = [], [], []
    for t in range(3):
        cols = slice(128 * t, 128 * t + 128)
        w0, w1, w2, m0, m1, m2 = [rel[k : 1 + k, cols] for k in range(6)]
        acc = [None] * 27
        gs, cs = [], []

        def add(row, value):
            acc[row] = value if acc[row] is None else acc[row] + value

        for j in range(3):
            x, y = pixel_xy(me, j)
            fu, fv, cu, cv = [comps[24 * c + 8 * j : 24 * c + 8 * j + 8, cols] for c in range(4)]
            d = near[8 * j : 8 * j + 8, cols]
            x0 = x + w1 - w2 * y + m0 * d
            x1 = y + w2 * x - w0 + m1 * d
            x2 = 1.0 + w0 * y - w1 * x + m2 * d
            q = 1.0 / x2
            u = x0 * q
            v = x1 * q
            ru = fu - (u - x)
            rv = fv - (v - y)
            du = q * (m0 - u * m2)
            dv = q * (m1 - v * m2)
            eu = cu * du
            ev = cv * dv
            gs.append(eu * ru + ev * rv)
            cs.append(eu * du + ev * dv)
            dq = d * q
            ju = {0: -(u * y) * q, 1: (1.0 + u * x) * q, 2: -y * q, 3: dq, 5: -u * dq}
            jv = {0: (-1.0 - v * y) * q, 1: v * x * q, 2: x * q, 4: dq, 5: -v * dq}
            for a in range(6):
                if a in ju and a in jv:
                    e = ju[a] * eu + jv[a] * ev
                else:
                    e = ju[a] * eu if a in ju else jv[a] * ev
                coup[g, 24 * a + 8 * j : 24 * a + 8 * j + 8, cols] = e
            su = {a: cu * ju[a] for a in ju}
            sv = {a: cv * jv[a] for a in jv}
            for (a, b), row in K_PAIRS:
                if a in ju and b in ju:
                    add(row, su[a] * ju[b])
                if a in jv and b in jv:
                    add(row, sv[a] * jv[b])
            for a in range(6):
                if a in ju:
                    add(H_ROW + a, su[a] * ru)
                if a in jv:
                    add(H_ROW + a, sv[a] * rv)
        acc = [jnp.zeros((8, 128), F32) if x is None else x for x in acc]
        grads.append(jnp.concatenate(gs, 0))
        curvs.append(jnp.concatenate(cs, 0))
        blocks.append(merged_rows(acc))
    both = jnp.concatenate([jnp.concatenate(grads, 1), jnp.concatenate(curvs, 1)], 0)
    sums[...] += summed(both, hot[g])
    add_up(jnp.concatenate(blocks, 1), g, hot, own, total_s, total_t)


def source_columns():
    rows = lax.broadcasted_iota(jnp.int32, (128, LANES), 0)
    frame = lax.broadcasted_iota(jnp.int32, (1, LANES), 1) // 24
    return jnp.where(rows == (frame % 2) * 8 + frame // 2, 1.0, 0.0).astype(BF16)


def second_pass(g, hot, own, coup, inverse, total_s, total_t):
    near = gathered(inverse[...], hot[g])
    blocks = []
    for t in range(3):
        cols = slice(128 * t, 128 * t + 128)
        acc = [None] * 27
        for j in range(3):
            ci = near[8 * j : 8 * j + 8, cols]
            gi = near[24 + 8 * j : 32 + 8 * j, cols]
            e = [coup[g, 24 * a + 8 * j : 24 * a + 8 * j + 8, cols] for a in range(6)]
            for a in range(6):
                scaled = e[a] * ci
                new = [(row, scaled * e[b]) for (k, b), row in K_PAIRS if k == a]
                for row, value in [*new, (H_ROW + a, e[a] * gi)]:
                    acc[row] = value if acc[row] is None else acc[row] + value
        blocks.append(-merged_rows(acc))
    add_up(jnp.concatenate(blocks, 1), g, hot, own, total_s, total_t)


def third_pass(g, hot, own, coup, steps, fix):
    motion = expanded(steps[...], g, own) - gathered(steps[...], hot[g])
    parts = []
    for t in range(3):
        cols = slice(128 * t, 128 * t + 128)
        column = []
        for j in range(3):
            at = [slice(24 * a + 8 * j, 24 * a + 8 * j + 8) for a in range(6)]
            terms = [coup[g, at[a], cols] * motion[a : a + 1, cols] for a in range(6)]
            column.append(((terms[0] + terms[1]) + (terms[2] + terms[3])) + (terms[4] + terms[5]))
        parts.append(jnp.concatenate(column, 0))
    fix[...] += summed(jnp.concatenate(parts, 1), hot[g])


def solve(matrix, right):
    factor = {}
    for i in range(6):
        for j in range(i + 1):
            e = matrix(i, j)
            if i == j:
                e = e * 1.1 + 0.001
            for k in range(j):
                e = e - factor[i, k] * factor[j, k]
            factor[i, j] = jnp.sqrt(e) if i == j else e / factor[j, j]
    forward = []
    for i in range(6):
        e = right(i)
        for k in range(i):
            e = e - factor[i, k] * forward[k]
        forward.append(e / factor[i, i])
    z = [None] * 6
    for i in reversed(range(6)):
        e = forward[i]
        for k in range(i + 1, 6):
            e = e - factor[k, i] * z[k]
        z[i] = e / factor[i, i]
    return z


def ring_steps(d):
    return min(d, 4 - d)


def far_first():
    offsets = [
        (dz, dy, dx, dc)
        for dz in range(4)
        for dy in range(4)
        for dx in range(4)
        for dc in range(2)
        if (dz, dy, dx, dc) != (0, 0, 0, 0)
    ]
    return sorted(offsets, key=lambda o: -(ring_steps(o[0]) + ring_steps(o[1]) + ring_steps(o[2])))


def group_offset(n):
    return (n // 4 + n) % 4, n % 4


def by_group():
    order = []
    for n in range(GROUPS):
        oz, oy = group_offset(n)
        for dx in range(4):
            for dc in range(2):
                order.append(((oz + dx) % 4, (oy + dx) % 4, dx, dc))
    return order[1:]


def to_all(order, act):
    row, col = lax.axis_index("row"), lax.axis_index("col")
    y, x = col // 8, (col // 2) % 4
    zs = [((row + d) % 4) * 32 for d in range(4)]
    ys = [((y + d) % 4) * 8 for d in range(4)]
    xs = [((x + d) % 4) * 2 for d in range(4)]
    cs = [(col + d) % 2 for d in range(2)]
    gz = [((row + 4 - x + d) % 4) * 32 for d in range(4)]
    gy = [((y + 4 - x + d) % 4) * 8 for d in range(4)]
    for dz, dy, dx, dc in order:
        last = xs[dx] + cs[dc]
        act(zs[dz] + ys[dy] + last, gz[(dz - dx) % 4] + gy[(dy - dx) % 4] + last)


def slot_of(d):
    return (d % 16) * 8 + d // 16


def rows_exchange(send, recv, source, slot, send_sem, recv_sem):
    def act(d, place):
        pltpu.make_async_remote_copy(
            src_ref=send.at[pl.ds(source(d, place), 1), :],
            dst_ref=recv.at[pl.ds(slot, 1), :],
            send_sem=send_sem,
            recv_sem=recv_sem,
            device_id=d,
            device_id_type=pl.DeviceIdType.LOGICAL,
        ).start()

    to_all(far_first(), act)


def rows_wait(buf, sem):
    ref = buf.at[pl.ds(0, NDEV - 1), :]
    pltpu.make_async_copy(ref, ref, sem).wait()


def scope(name):
    return contextlib.nullcontext()


def loop(body, times):
    def step(n, carry):
        for k in range(times):
            body(times * n + k)
        return carry

    lax.fori_loop(0, GROUPS // times, step, 0)


def main_kernel(
    flow_hbm, weight_hbm, depth_ref, target_ref, rotation_ref, translation_ref,
    out_ref, pose_ref,
    flow, weight, low, high, chunks, ints, floats, unfold,
    recv, comps, table, hot, own, coup, sums, inverse, total_s, total_t, steps, fix,
    send_t, recv_t, send_d, recv_d, send_e, recv_e, send_f, recv_f,
    in_sem, big_send, big_recv, small_send, small_recv,
):
    row, col = lax.axis_index("row"), lax.axis_index("col")
    me = row * 32 + col
    y, x = col // 8, (col // 2) % 4
    my_gz, my_gy = (row + 4 - x) % 4, (y + 4 - x) % 4
    mine_at = (my_gz * 4 + my_gy) * 8 + col % 8
    lane = lane_iota()
    barrier = pltpu.get_barrier_semaphore()

    loads = [
        pltpu.make_async_copy(flow_hbm, flow, in_sem.at[0]),
        pltpu.make_async_copy(weight_hbm, weight, in_sem.at[1]),
    ]
    for load in loads:
        load.start()

    def greet(d, _):
        pl.semaphore_signal(
            barrier, inc=1, device_id=d, device_id_type=pl.DeviceIdType.LOGICAL
        )

    with scope("sc_greet"):
        to_all(far_first(), greet)

    with scope("sc_tables"):
        table[...] = jnp.zeros_like(table)
        sums[...] = jnp.zeros_like(sums)
        total_t[...] = jnp.zeros_like(total_t)
        total_s[...] = jnp.zeros_like(total_s)
        fix[...] = jnp.zeros_like(fix)
        own[...] = source_columns()
        high[...] = jnp.zeros_like(high)
        column, pose = own_edges(target_ref, rotation_ref, translation_ref, ints, floats)
        pack_tables(depth_ref, column, pose, unfold, send_t)
        recv_t[pl.ds(mine_at, 1), :] = send_t[pl.ds(slot_of(me), 1), :]
        turn = col % 8
        for load in loads:
            load.wait()

    def pack(n, carry):
        pack_block(n, turn, flow, weight, low, high, chunks)
        return carry

    with scope("sc_pack"):
        lax.fori_loop(0, 8, pack, 0)
    with scope("sc_barrier"):
        pl.semaphore_wait(barrier, NDEV - 1)

    with scope("sc_sends"):
        rows_exchange(
            send_t, recv_t, lambda d, _: slot_of(d), mine_at, small_send.at[3], small_recv.at[3]
        )

        def send_chunk(d, _):
            pltpu.make_async_remote_copy(
                src_ref=chunks.at[d, pl.ds(0, 36), :],
                dst_ref=recv.at[mine_at, pl.ds(0, 36), :],
                send_sem=big_send,
                recv_sem=big_recv.at[mine_at],
                device_id=d,
                device_id_type=pl.DeviceIdType.LOGICAL,
            ).start()

        to_all(by_group(), send_chunk)
        recv[mine_at, 0:36, :] = chunks[me, 0:36, :]

    with scope("sc_waitt"):
        rows_wait(recv_t, small_recv.at[3])
        known = recv_t[...].T
        for f in range(2):
            at = slice(128 * f, 128 * f + 128)
            table[0:24, at] = known[24 * f : 24 * f + 24]
            table[24:32, at] = known[48 + 8 * f : 56 + 8 * f]

    def arrive(n):
        oz, oy = group_offset(n)
        g = ((my_gz + 4 - oz) % 4) * 4 + (my_gy + 4 - oy) % 4
        for i in range(8):
            s = 8 * g + i

            @pl.when(s != mine_at)
            def _():
                ref = recv.at[s, pl.ds(0, 36), :]
                pltpu.make_async_copy(ref, ref, big_recv.at[s]).wait()

        unpack_group(g, recv, comps)
        first_pass(g, me, comps, recv_t, table, hot, own, coup, sums, total_s, total_t)

    with scope("sc_arrive"):
        loop(arrive, 1)
    with scope("sc_second"):
        ci = 1.0 / (0.1 + sums[24:48])
        inverse[0:24] = ci
        inverse[24:48] = sums[0:24] * ci
        loop(lambda g: second_pass(g, hot, own, coup, inverse, total_s, total_t), 2)

    with scope("sc_sendd"):
        kind = lax.broadcasted_iota(jnp.int32, (32, 256), 0)
        total = total_s[...] + jnp.where(kind < H_ROW, total_t[...], -total_t[...])
        send_d[...] = jnp.concatenate(
            [total[:, 0:128], total[:, 128:256], jnp.zeros((64, 128), F32)], 0
        ).T
        recv_d[pl.ds(mine_at, 1), :] = send_d[pl.ds(mine_at, 1), :]
        rows_exchange(
            send_d, recv_d, lambda _, place: place, mine_at, small_send.at[0], small_recv.at[0]
        )
    with scope("sc_waitd"):
        rows_wait(recv_d, small_recv.at[0])
    with scope("sc_solve"):
        line = jnp.sum(recv_d[...], axis=0, keepdims=True)
        sub = lax.broadcasted_iota(jnp.int32, (8, 128), 0)
        lines = jnp.broadcast_to(line, (8, 128))
        lines = jnp.where(sub == 1, pltpu.roll(lines, 96, 1), lines)
        full = jnp.concatenate([lines, jnp.zeros((120, 128), F32)], 0).T
        z = solve(
            lambda i, j: full[K_INDEX[i, j] : K_INDEX[i, j] + 1, :],
            lambda i: full[H_ROW + i : H_ROW + i + 1, :],
        )
        zs = jnp.concatenate([*z, jnp.zeros((122, 128), F32)], 0)
        turned = zs.T
        pose_ref[...] = turned[0:2, 0:6]
        mine = turned[0:1] + pltpu.roll(turned[0:8], 8, 1)[1:2]
        send_e[...] = jnp.broadcast_to(mine, (8, 128))
        recv_e[pl.ds(mine_at, 1), :] = mine
    with scope("sc_sende"):
        rows_exchange(
            send_e, recv_e, lambda d, _: 0, mine_at, small_send.at[1], small_recv.at[1]
        )
    with scope("sc_waite"):
        rows_wait(recv_e, small_recv.at[1])
    with scope("sc_third"):
        every = recv_e[...].T
        steps[:, 0:128] = every[0:8]
        steps[:, 128:256] = every[8:16]
        loop(lambda g: third_pass(g, hot, own, coup, steps, fix), 4)
    with scope("sc_sendf"):
        grad = sums[0:24]
        new = table[0:24] + (grad - fix[...]) * inverse[0:24]
        zero8 = jnp.zeros((8, 128), F32)
        send_f[...] = jnp.concatenate(
            [new[:, 0:128], zero8, new[:, 128:256], zero8, jnp.zeros((64, 128), F32)], 0
        ).T
        slot = slot_of(me)
        recv_f[pl.ds(slot, 1), :] = send_f[pl.ds(mine_at, 1), :]
        rows_exchange(
            send_f, recv_f, lambda _, place: place, slot, small_send.at[2], small_recv.at[2]
        )
    with scope("sc_waitf"):
        rows_wait(recv_f, small_recv.at[2])
    for f in range(2):
        tiles = [None] * 3
        for i in range(16):
            piece = recv_f[8 * i : 8 * i + 8, :]
            first = 24 * i
            moved = pltpu.roll(piece, (first - 32 * f) % 128, 1)
            for t in range(3):
                a, b = max(first - 128 * t, 0), min(first + 24 - 128 * t, 128)
                if a < b:
                    if tiles[t] is None:
                        tiles[t] = moved
                    else:
                        tiles[t] = jnp.where((lane >= a) & (lane < b), moved, tiles[t])
        for g in range(8):
            for t in range(3):
                at = 384 * g + 128 * t
                out_ref[f : f + 1, at : at + 128] = tiles[t][g : g + 1]

    ref = chunks.at[pl.ds(0, NDEV - 1), pl.ds(0, 36), :]
    pltpu.make_async_copy(ref, ref, big_send).wait()
    rows_wait(recv_t, small_send.at[3])
    rows_wait(recv_d, small_send.at[0])
    rows_wait(recv_e, small_send.at[1])
    rows_wait(recv_f, small_send.at[2])


def run_main(flow, weight, inv_depth, edge_target, rotation, translation):
    v = pltpu.VMEM
    vmem = pl.BlockSpec(memory_space=pltpu.VMEM)
    hbm = pl.BlockSpec(memory_space=pl.ANY)
    return pl.pallas_call(
        main_kernel,
        in_specs=[hbm, hbm, vmem, vmem, vmem, vmem],
        out_specs=[vmem] * 2,
        out_shape=[
            jax.ShapeDtypeStruct((2, PX * NDEV), F32),
            jax.ShapeDtypeStruct((2, 6), F32),
        ],
        scratch_shapes=[
            v((2, 48, PX * NDEV), F32),
            v((2, 48, PX * NDEV), F32),
            v((128, LANES), F32),
            v((128, LANES), F32),
            v((NDEV, 40, 128), F32),
            v((8, 128), jnp.int32),
            v((2, 8, 128), F32),
            v((2, 8, LANES), F32),
            v((NDEV, 40, 128), F32),
            v((96, LANES), F32),
            v((32, 256), F32),
            v((GROUPS, 256, LANES), BF16),
            v((128, LANES), BF16),
            v((GROUPS, 144, LANES), F32),
            v((48, 256), F32),
            v((48, 256), F32),
            v((32, 256), F32),
            v((32, 256), F32),
            v((8, 256), F32),
            v((24, 256), F32),
            v((128, 128), F32),
            v((128, 128), F32),
            v((128, 128), F32),
            v((128, 128), F32),
            v((8, 128), F32),
            v((128, 128), F32),
            v((128, 128), F32),
            v((128, 128), F32),
            pltpu.SemaphoreType.DMA((2,)),
            pltpu.SemaphoreType.DMA,
            pltpu.SemaphoreType.DMA((NDEV,)),
            pltpu.SemaphoreType.DMA((4,)),
            pltpu.SemaphoreType.DMA((4,)),
        ],
        compiler_params=pltpu.CompilerParams(
            collective_id=0, has_side_effects=True, vmem_limit_bytes=56 * 1024 * 1024
        ),
        name="step",
    )(flow, weight, inv_depth, edge_target, rotation, translation)


def shards(inv_depth, rotation, translation, edge_target, flow_obs, weight):
    pixels = inv_depth.shape[1]
    flow = flow_obs.reshape(2, 48, pixels)
    wts = weight.reshape(2, 48, pixels)
    depth, pose = run_main(flow, wts, inv_depth, edge_target, rotation.T, translation.T)
    return depth, pose.T


def solution(mesh):
    in_specs = (
        P(("row", "col"), None),
        P(None, ("row", "col")),
        P(None, ("row", "col")),
        P(("row", "col"), None),
        P(None, ("row", "col"), None, None),
        P(None, ("row", "col"), None, None),
    )
    out_specs = (P(("row", "col"), None), P(None, ("row", "col")))
    return jax.shard_map(
        shards, mesh=mesh, in_specs=in_specs, out_specs=out_specs, check_vma=False
    )
```

time: 91.6 us -> 76.9 us (0.84)
  Pallas kernels: 88.1 us -> 73.4 us
    pallas_call x1, Pallas kernels: 88.1 us -> 73.4 us  [run_main(): pl.pallas_call(main_kernel, in_specs=[hbm, hbm, vmem, vmem, vmem, vmem],...]
where the time goes in v3:
time: 76.9 us; the launch traced here: 76.6 us
  Pallas kernels  73.4 us (95%)
  local copies, waits for them, and re-layouts  2.58 us (3%)
    pallas_call x1, Pallas kernels, run_main(): pl.pallas_call(main_kernel, in_specs=[hbm, hbm, vmem, vmem, vmem, vmem],...  73.4 us
    unnamed x2, local copies, waits for them, and re-layouts  2.58 us

profile of v3, /device:TPU:1, one launch (start us, length us, event | category | flops | bytes accessed | tf_op | source)
XLA Modules:
  0.0 76.6 jit_solution(10130828188535940852)
XLA Ops:
  0.6 73.4 %step.1 = (f32[2,3072]{1,0:T(2,128)}, f32[2,6]{1,0:T(2,128)}) custom-call(f32[2,48,3072]{2,1,0:T(8,128)} %bitcast.5, f32[2,48,3072]{2,1,0:T(8,128)} %bitcast.6, f32[2,3072]{1,0:T(2,128)} %depth_ref.1, s32[2,24]{1,0:T(2,128)} %target_ref.1, f32[2,3]{1,0:T(2,128)} %bitcast.7, f32[2,3]{1,0:T(2,128)} %bitcast.8), custom_call_target="tpu_custom_call" | custom-call | tf_op jit(solution)/shard_map/step/pallas_call | solution.py:627
  74.0 1.3 %copy.10 = f32[2,3072]{1,0:T(2,128)} copy(f32[2,3072]{1,0:T(2,128)} %get-tuple-element.8) | data formatting | bytes 49152
  75.4 1.2 %copy.11 = f32[6,2]{0,1:T(2,128)} copy(f32[6,2]{0,1:T(2,128)} %bitcast.9) | data formatting | bytes 96

commit v4 on v3

--- a/solution.py
+++ b/solution.py
@@ -1,4 +1,5 @@
 import contextlib
+import functools
 
 import jax
 import jax.numpy as jnp
@@ -17,6 +18,7 @@
 K_PAIRS = [((a, b), n) for n, (a, b) in enumerate((a, b) for a in range(6) for b in range(a, 6))]
 K_INDEX = {**dict(K_PAIRS), **{(b, a): n for (a, b), n in K_PAIRS}}
 H_ROW = 21
+ARRIVE, LAST, THIRD = 2, 4, 8
 
 
 def lane_iota(shape=(8, 128)):
@@ -41,16 +43,12 @@
     high_t = high[...].T
     where_at = (lane_iota() - 48 * turn + 384) % 128
     for d in range(16):
-        base = 24 * d
-        to = 16 * n + d
         for j in range(3):
-            out[to, 8 * j : 8 * j + 8, :] = low_t[base + 8 * j : base + 8 * j + 8]
-        u0 = high_t[base : base + 8]
-        u1 = high_t[base + 8 : base + 16]
-        u2 = high_t[base + 16 : base + 24]
-        out[to, 24:32, :] = jnp.where(where_at < 64, u0, pltpu.roll(u1, 64, 1))
-        last = jnp.where(where_at < 64, u2, pltpu.roll(pltpu.roll(u2, 64, 1), 4, 0))
-        out[to, 32:36, :] = last[0:4]
+            at = 24 * d + 8 * j
+            out[16 * n + d, j, 0:8, :] = low_t[at : at + 8]
+            rest = high_t[at : at + 8]
+            turned = pltpu.roll(pltpu.roll(rest, 64, 1), 4, 0)
+            out[16 * n + d, j, 8:12, :] = jnp.where(where_at < 64, rest, turned)[0:4]
 
 
 def own_edges(target_ref, rotation_ref, translation_ref, ints, floats):
@@ -132,44 +130,31 @@
     return join3(jnp.dot(split3(table), hot, preferred_element_type=F32))
 
 
-def summed(values, hot):
-    return join3(
-        lax.dot_general(
-            split3(values), hot, (((1,), (1,)), ((), ())), preferred_element_type=F32
-        )
-    )
-
-
-def unpack_group(g, recv, comps):
+def summed(values, hot_t):
+    return join3(jnp.dot(split3(values), hot_t, preferred_element_type=F32))
+
+
+def unpack_group(g, j, recv):
     lane = lane_iota()
     upper = lax.broadcasted_iota(jnp.int32, (8, 128), 0) >= 4
     block_lane = [(lane + 128 * t) % 48 for t in range(3)]
-    srcs = [8 * g + i for i in range(8)]
-    tile3 = [recv[s, 24:32, :] for s in srcs]
-    tile4 = [recv[s, 32:40, :] for s in srcs]
-
-    def piece(j, offset, width, to):
-        def at(tiles, start):
-            return shifted(strip(tiles, lane, start, width), lane, to - start)
-
-        if j < 2:
-            return at(tile3, offset + 64 * j)
-        first, second = at(tile4, offset), at(tile4, offset + 64)
+    low = [recv[8 * g + i, j, 0:8, :] for i in range(8)]
+    high = [recv[8 * g + i, j, 8:16, :] for i in range(8)]
+
+    def at(tiles, start, width, to):
+        return shifted(strip(tiles, lane, start, width), lane, to - start)
+
+    def piece(offset, width, to):
+        first, second = at(high, offset, width, to), at(high, offset + 64, width, to)
         return [jnp.where(upper, pltpu.roll(b, 4, 0), a) for a, b in zip(first, second)]
 
-    for j in range(3):
-        low = [recv[s, 8 * j : 8 * j + 8, :] for s in srcs]
-        first = shifted(strip(low, lane, 96, 32), lane, -96)
-        second = piece(j, 0, 16, 32)
-        parts = [
-            strip(low, lane, 0, 48),
-            shifted(strip(low, lane, 48, 48), lane, -48),
-            [jnp.where(b < 32, f, s) for b, f, s in zip(block_lane, first, second)],
-            piece(j, 16, 48, 0),
-        ]
-        for c, tiles in enumerate(parts):
-            for t in range(3):
-                comps[24 * c + 8 * j : 24 * c + 8 * j + 8, 128 * t : 128 * t + 128] = tiles[t]
+    first, second = at(low, 96, 32, 0), piece(0, 16, 32)
+    return [
+        at(low, 0, 48, 0),
+        at(low, 48, 48, 0),
+        [jnp.where(b < 32, f, s) for b, f, s in zip(block_lane, first, second)],
+        piece(16, 48, 0),
+    ]
 
 
 def group_targets(g, recv_t):
@@ -211,19 +196,26 @@
     return x, y
 
 
-def expanded(rows, g, own):
+def expand(rows, own, out):
     lane = lane_iota()
-    mine = jnp.where(
-        lane < 8,
-        pltpu.roll(rows[:, 0:128], (128 - 8 * g) % 128, 1),
-        pltpu.roll(rows[:, 128:256], (136 - 8 * g) % 128, 1),
-    )
-    return gathered(mine, own[...])
-
-
-def add_up(values, g, hot, own, total_s, total_t):
-    total_t[...] += summed(values, hot[g])
-    by_source = summed(values, own[...])
+    mine = [
+        jnp.where(
+            lane < 8,
+            pltpu.roll(rows[:, 0:128], (128 - 8 * g) % 128, 1),
+            pltpu.roll(rows[:, 128:256], (136 - 8 * g) % 128, 1),
+        )
+        for g in range(GROUPS)
+    ]
+    out[...] = gathered(jnp.concatenate(mine, 0), own[...])
+
+
+def rows_of(ref, g):
+    return ref[pl.ds(pl.multiple_of(8 * g, 8), 8), :]
+
+
+def add_up(values, g, hot_t, own_t, total_s, total_t):
+    total_t[...] += summed(values, hot_t[g])
+    by_source = summed(values, own_t[...])
     lane = lane_iota((32, 128))
     for f in range(2):
         at = slice(128 * f, 128 * f + 128)
@@ -231,67 +223,111 @@
         total_s[:, at] += jnp.where(lane // 8 == g, moved, 0.0)
 
 
-def first_pass(g, me, comps, recv_t, table, hot, own, coup, sums, total_s, total_t):
-    rows = lax.broadcasted_iota(jnp.int32, (256, LANES), 0).astype(F32)
-    hot[g] = jnp.where(rows == group_targets(g, recv_t), 1.0, 0.0).astype(BF16)
-    near = gathered(table[...], hot[g])
-    rel = expanded(table[24:32, :], g, own) - near[24:32]
+def edge_rows(a, j):
+    return slice(24 * a + 8 * j, 24 * a + 8 * j + 8)
+
+
+def add_block(acc, row, value):
+    acc[row] = value if acc[row] is None else acc[row] + value
+
+
+def source_columns_t():
+    frame = lax.broadcasted_iota(jnp.int32, (LANES, 1), 0) // 24
+    lanes = lax.broadcasted_iota(jnp.int32, (LANES, 128), 1)
+    return jnp.where(lanes == (frame % 2) * 8 + frame // 2, 1.0, 0.0).astype(BF16)
+
+
+def build_terms(acc, cols, inputs, d, rel, xy, coup, g, j):
+    x, y = xy
+    fu, fv, cu, cv = inputs
+    w0, w1, w2, m0, m1, m2 = [rel[k : 1 + k, cols] for k in range(6)]
+    x0 = x + w1 - w2 * y + m0 * d
+    x1 = y + w2 * x - w0 + m1 * d
+    x2 = 1.0 + w0 * y - w1 * x + m2 * d
+    q = 1.0 / x2
+    u = x0 * q
+    v = x1 * q
+    ru = fu - (u - x)
+    rv = fv - (v - y)
+    du = q * (m0 - u * m2)
+    dv = q * (m1 - v * m2)
+    eu = cu * du
+    ev = cv * dv
+    dq = d * q
+    ju = {0: -(u * y) * q, 1: (1.0 + u * x) * q, 2: -y * q, 3: dq, 5: -u * dq}
+    jv = {0: (-1.0 - v * y) * q, 1: v * x * q, 2: x * q, 4: dq, 5: -v * dq}
+    for a in range(6):
+        if a in ju and a in jv:
+            e = ju[a] * eu + jv[a] * ev
+        else:
+            e = ju[a] * eu if a in ju else jv[a] * ev
+        coup[g, edge_rows(a, j), cols] = e
+    su = {a: cu * ju[a] for a in ju}
+    sv = {a: cv * jv[a] for a in jv}
+    for (a, b), row in K_PAIRS:
+        if a in ju and b in ju:
+            add_block(acc, row, su[a] * ju[b])
+        if a in jv and b in jv:
+            add_block(acc, row, sv[a] * jv[b])
+    for a in range(6):
+        if a in ju:
+            add_block(acc, H_ROW + a, su[a] * ru)
+        if a in jv:
+            add_block(acc, H_ROW + a, sv[a] * rv)
+    return eu * ru + ev * rv, eu * du + ev * dv
+
+
+def take_terms(acc, cols, near, coup, g, j):
+    ci, gi = -near[0:8, cols], -near[8:16, cols]
+    e = [coup[g, edge_rows(a, j), cols] for a in range(6)]
+    for a in range(6):
+        scaled = e[a] * ci
+        for (k, b), row in K_PAIRS:
+            if k == a:
+                add_block(acc, row, scaled * e[b])
+        add_block(acc, H_ROW + a, e[a] * gi)
+
+
+def filled(acc):
+    return [jnp.zeros((8, 128), F32) if x is None else x for x in acc]
+
+
+def phase_pass(g, j, me, recv, recv_t, table, hot, hot_t, from_pose, dep, rel, coup, sums, inverse, kh):
+    if j == 0:
+        rows = lax.broadcasted_iota(jnp.int32, (256, LANES), 0).astype(F32)
+        targets = group_targets(g, recv_t)
+        hot[g] = jnp.where(rows == targets, 1.0, 0.0).astype(BF16)
+        lanes = lane_iota((128, 256)).astype(F32)
+        for t in range(3):
+            at = slice(128 * t, 128 * t + 128)
+            column = jnp.broadcast_to(targets[:, at], (128, 128)).T
+            column = jnp.concatenate([column, column], 1)
+            hot_t[g, at, :] = jnp.where(lanes == column, 1.0, 0.0).astype(BF16)
+        near = gathered(table[...], hot[g])
+        dep[g] = near[0:24]
+        relative = rows_of(from_pose, g) - near[24:32]
+        rel[g] = relative
+    else:
+        relative = rel[g]
+        back = gathered(inverse[j - 1], hot[g])
+    parts = unpack_group(g, j, recv)
     grads, curvs, blocks = [], [], []
+    xy = pixel_xy(me, j)
     for t in range(3):
         cols = slice(128 * t, 128 * t + 128)
-        w0, w1, w2, m0, m1, m2 = [rel[k : 1 + k, cols] for k in range(6)]
         acc = [None] * 27
-        gs, cs = [], []
-
-        def add(row, value):
-            acc[row] = value if acc[row] is None else acc[row] + value
-
-        for j in range(3):
-            x, y = pixel_xy(me, j)
-            fu, fv, cu, cv = [comps[24 * c + 8 * j : 24 * c + 8 * j + 8, cols] for c in range(4)]
-            d = near[8 * j : 8 * j + 8, cols]
-            x0 = x + w1 - w2 * y + m0 * d
-            x1 = y + w2 * x - w0 + m1 * d
-            x2 = 1.0 + w0 * y - w1 * x + m2 * d
-            q = 1.0 / x2
-            u = x0 * q
-            v = x1 * q
-            ru = fu - (u - x)
-            rv = fv - (v - y)
-            du = q * (m0 - u * m2)
-            dv = q * (m1 - v * m2)
-            eu = cu * du
-            ev = cv * dv
-            gs.append(eu * ru + ev * rv)
-            cs.append(eu * du + ev * dv)
-            dq = d * q
-            ju = {0: -(u * y) * q, 1: (1.0 + u * x) * q, 2: -y * q, 3: dq, 5: -u * dq}
-            jv = {0: (-1.0 - v * y) * q, 1: v * x * q, 2: x * q, 4: dq, 5: -v * dq}
-            for a in range(6):
-                if a in ju and a in jv:
-                    e = ju[a] * eu + jv[a] * ev
-                else:
-                    e = ju[a] * eu if a in ju else jv[a] * ev
-                coup[g, 24 * a + 8 * j : 24 * a + 8 * j + 8, cols] = e
-            su = {a: cu * ju[a] for a in ju}
-            sv = {a: cv * jv[a] for a in jv}
-            for (a, b), row in K_PAIRS:
-                if a in ju and b in ju:
-                    add(row, su[a] * ju[b])
-                if a in jv and b in jv:
-                    add(row, sv[a] * jv[b])
-            for a in range(6):
-                if a in ju:
-                    add(H_ROW + a, su[a] * ru)
-                if a in jv:
-                    add(H_ROW + a, sv[a] * rv)
-        acc = [jnp.zeros((8, 128), F32) if x is None else x for x in acc]
-        grads.append(jnp.concatenate(gs, 0))
-        curvs.append(jnp.concatenate(cs, 0))
-        blocks.append(merged_rows(acc))
+        d = dep[g, 8 * j : 8 * j + 8, cols]
+        tiles = [part[t] for part in parts]
+        gd, cd = build_terms(acc, cols, tiles, d, relative, xy, coup, g, j)
+        grads.append(gd)
+        curvs.append(cd)
+        if j > 0:
+            take_terms(acc, cols, back, coup, g, j - 1)
+        blocks.append(merged_rows(filled(acc)))
     both = jnp.concatenate([jnp.concatenate(grads, 1), jnp.concatenate(curvs, 1)], 0)
-    sums[...] += summed(both, hot[g])
-    add_up(jnp.concatenate(blocks, 1), g, hot, own, total_s, total_t)
+    sums[j] += summed(both, hot_t[g])
+    block = jnp.concatenate(blocks, 1)
+    kh[g] = block if j == 0 else kh[g] + block
 
 
 def source_columns():
@@ -300,37 +336,27 @@
     return jnp.where(rows == (frame % 2) * 8 + frame // 2, 1.0, 0.0).astype(BF16)
 
 
-def second_pass(g, hot, own, coup, inverse, total_s, total_t):
-    near = gathered(inverse[...], hot[g])
+def last_pass(g, hot, hot_t, own_t, coup, inverse, kh, total_s, total_t):
+    near = gathered(inverse[2], hot[g])
     blocks = []
     for t in range(3):
-        cols = slice(128 * t, 128 * t + 128)
         acc = [None] * 27
-        for j in range(3):
-            ci = near[8 * j : 8 * j + 8, cols]
-            gi = near[24 + 8 * j : 32 + 8 * j, cols]
-            e = [coup[g, 24 * a + 8 * j : 24 * a + 8 * j + 8, cols] for a in range(6)]
-            for a in range(6):
-                scaled = e[a] * ci
-                new = [(row, scaled * e[b]) for (k, b), row in K_PAIRS if k == a]
-                for row, value in [*new, (H_ROW + a, e[a] * gi)]:
-                    acc[row] = value if acc[row] is None else acc[row] + value
-        blocks.append(-merged_rows(acc))
-    add_up(jnp.concatenate(blocks, 1), g, hot, own, total_s, total_t)
-
-
-def third_pass(g, hot, own, coup, steps, fix):
-    motion = expanded(steps[...], g, own) - gathered(steps[...], hot[g])
+        take_terms(acc, slice(128 * t, 128 * t + 128), near, coup, g, 2)
+        blocks.append(merged_rows(acc))
+    add_up(kh[g] + jnp.concatenate(blocks, 1), g, hot_t, own_t, total_s, total_t)
+
+
+def third_pass(g, hot_t, coup, from_steps, fix):
+    motion = rows_of(from_steps, g)
     parts = []
     for t in range(3):
         cols = slice(128 * t, 128 * t + 128)
         column = []
         for j in range(3):
-            at = [slice(24 * a + 8 * j, 24 * a + 8 * j + 8) for a in range(6)]
-            terms = [coup[g, at[a], cols] * motion[a : a + 1, cols] for a in range(6)]
+            terms = [coup[g, edge_rows(a, j), cols] * motion[a : a + 1, cols] for a in range(6)]
             column.append(((terms[0] + terms[1]) + (terms[2] + terms[3])) + (terms[4] + terms[5]))
         parts.append(jnp.concatenate(column, 0))
-    fix[...] += summed(jnp.concatenate(parts, 1), hot[g])
+    fix[...] += summed(jnp.concatenate(parts, 1), hot_t[g])
 
 
 def solve(matrix, right):
@@ -439,10 +465,11 @@
 
 
 def main_kernel(
-    flow_hbm, weight_hbm, depth_ref, target_ref, rotation_ref, translation_ref,
+    flow_hbm, weight_hbm, depth_hbm, target_hbm, rotation_hbm, translation_hbm,
     out_ref, pose_ref,
-    flow, weight, low, high, chunks, ints, floats, unfold,
-    recv, comps, table, hot, own, coup, sums, inverse, total_s, total_t, steps, fix,
+    flow, weight, depth_ref, target_ref, rotation_ref, translation_ref, low, high, chunks, ints, floats, unfold,
+    recv, table, hot, hot_t, own, own_t, from_pose, dep, rel, coup, sums, inverse, kh,
+    total_s, total_t, at_target, steps, from_steps, fix,
     send_t, recv_t, send_d, recv_d, send_e, recv_e, send_f, recv_f,
     in_sem, big_send, big_recv, small_send, small_recv,
 ):
@@ -450,16 +477,22 @@
     me = row * 32 + col
     y, x = col // 8, (col // 2) % 4
     my_gz, my_gy = (row + 4 - x) % 4, (y + 4 - x) % 4
-    mine_at = (my_gz * 4 + my_gy) * 8 + col % 8
+    my_group = my_gz * 4 + my_gy
+    mine_at = my_group * 8 + col % 8
     lane = lane_iota()
     barrier = pltpu.get_barrier_semaphore()
 
+    inputs = [
+        (depth_hbm, depth_ref),
+        (target_hbm, target_ref),
+        (rotation_hbm, rotation_ref),
+        (translation_hbm, translation_ref),
+        (flow_hbm, flow),
+        (weight_hbm, weight),
+    ]
     loads = [
-        pltpu.make_async_copy(flow_hbm, flow, in_sem.at[0]),
-        pltpu.make_async_copy(weight_hbm, weight, in_sem.at[1]),
+        pltpu.make_async_copy(source, to, in_sem.at[k]) for k, (source, to) in enumerate(inputs)
     ]
-    for load in loads:
-        load.start()
 
     def greet(d, _):
         pl.semaphore_signal(
@@ -467,6 +500,8 @@
         )
 
     with scope("sc_greet"):
+        for load in loads:
+            load.start()
         to_all(far_first(), greet)
 
     with scope("sc_tables"):
@@ -475,13 +510,17 @@
         total_t[...] = jnp.zeros_like(total_t)
         total_s[...] = jnp.zeros_like(total_s)
         fix[...] = jnp.zeros_like(fix)
+        at_target[...] = jnp.zeros_like(at_target)
         own[...] = source_columns()
+        own_t[...] = source_columns_t()
         high[...] = jnp.zeros_like(high)
+        for load in loads[:4]:
+            load.wait()
         column, pose = own_edges(target_ref, rotation_ref, translation_ref, ints, floats)
         pack_tables(depth_ref, column, pose, unfold, send_t)
         recv_t[pl.ds(mine_at, 1), :] = send_t[pl.ds(slot_of(me), 1), :]
         turn = col % 8
-        for load in loads:
+        for load in loads[4:]:
             load.wait()
 
     def pack(n, carry):
@@ -498,18 +537,20 @@
             send_t, recv_t, lambda d, _: slot_of(d), mine_at, small_send.at[3], small_recv.at[3]
         )
 
-        def send_chunk(d, _):
-            pltpu.make_async_remote_copy(
-                src_ref=chunks.at[d, pl.ds(0, 36), :],
-                dst_ref=recv.at[mine_at, pl.ds(0, 36), :],
-                send_sem=big_send,
-                recv_sem=big_recv.at[mine_at],
-                device_id=d,
-                device_id_type=pl.DeviceIdType.LOGICAL,
-            ).start()
-
-        to_all(by_group(), send_chunk)
-        recv[mine_at, 0:36, :] = chunks[me, 0:36, :]
+        for j in range(3):
+
+            def send_chunk(d, _):
+                pltpu.make_async_remote_copy(
+                    src_ref=chunks.at[d, j, pl.ds(0, 12), :],
+                    dst_ref=recv.at[mine_at, j, pl.ds(0, 12), :],
+                    send_sem=big_send,
+                    recv_sem=big_recv.at[j, my_group],
+                    device_id=d,
+                    device_id_type=pl.DeviceIdType.LOGICAL,
+                ).start()
+
+            to_all(by_group(), send_chunk)
+        recv[mine_at, :, 0:12, :] = chunks[me, :, 0:12, :]
 
     with scope("sc_waitt"):
         rows_wait(recv_t, small_recv.at[3])
@@ -518,28 +559,34 @@
             at = slice(128 * f, 128 * f + 128)
             table[0:24, at] = known[24 * f : 24 * f + 24]
             table[24:32, at] = known[48 + 8 * f : 56 + 8 * f]
-
-    def arrive(n):
+        expand(table[24:32, :], own, from_pose)
+
+    def arrive(n, j):
         oz, oy = group_offset(n)
         g = ((my_gz + 4 - oz) % 4) * 4 + (my_gy + 4 - oy) % 4
-        for i in range(8):
-            s = 8 * g + i
-
-            @pl.when(s != mine_at)
-            def _():
-                ref = recv.at[s, pl.ds(0, 36), :]
-                pltpu.make_async_copy(ref, ref, big_recv.at[s]).wait()
-
-        unpack_group(g, recv, comps)
-        first_pass(g, me, comps, recv_t, table, hot, own, coup, sums, total_s, total_t)
-
-    with scope("sc_arrive"):
-        loop(arrive, 1)
-    with scope("sc_second"):
-        ci = 1.0 / (0.1 + sums[24:48])
-        inverse[0:24] = ci
-        inverse[24:48] = sums[0:24] * ci
-        loop(lambda g: second_pass(g, hot, own, coup, inverse, total_s, total_t), 2)
+
+        def landed(count):
+            ref = recv.at[pl.ds(8 * g, count), j, pl.ds(0, 12), :]
+            pltpu.make_async_copy(ref, ref, big_recv.at[j, g]).wait()
+
+        pl.when(n == 0)(lambda: landed(7))
+        pl.when(n != 0)(lambda: landed(8))
+
+        phase_pass(
+            g, j, me, recv, recv_t, table, hot, hot_t, from_pose, dep, rel, coup, sums,
+            inverse, kh,
+        )
+
+    for j in range(3):
+        with scope(f"sc_arrive{j}"):
+            loop(functools.partial(arrive, j=j), ARRIVE)
+            ci = 1.0 / (0.1 + sums[j, 8:16])
+            inverse[j, 0:8] = ci
+            inverse[j, 8:16] = sums[j, 0:8] * ci
+    with scope("sc_last"):
+        loop(
+            lambda g: last_pass(g, hot, hot_t, own_t, coup, inverse, kh, total_s, total_t), LAST
+        )
 
     with scope("sc_sendd"):
         kind = lax.broadcasted_iota(jnp.int32, (32, 256), 0)
@@ -551,6 +598,12 @@
         rows_exchange(
             send_d, recv_d, lambda _, place: place, mine_at, small_send.at[0], small_recv.at[0]
         )
+    with scope("sc_target"):
+
+        def couple(g):
+            at_target[...] += summed(coup[g], hot_t[g])
+
+        loop(couple, 2)
     with scope("sc_waitd"):
         rows_wait(recv_d, small_recv.at[0])
     with scope("sc_solve"):
@@ -579,10 +632,15 @@
         every = recv_e[...].T
         steps[:, 0:128] = every[0:8]
         steps[:, 128:256] = every[8:16]
-        loop(lambda g: third_pass(g, hot, own, coup, steps, fix), 4)
+        expand(steps[...], own, from_steps)
+        loop(lambda g: third_pass(g, hot_t, coup, from_steps, fix), THIRD)
     with scope("sc_sendf"):
-        grad = sums[0:24]
-        new = table[0:24] + (grad - fix[...]) * inverse[0:24]
+        back = at_target[0:24] * steps[0:1]
+        for a in range(1, 6):
+            back += at_target[24 * a : 24 * a + 24] * steps[a : a + 1]
+        grad = jnp.concatenate([sums[j, 0:8] for j in range(3)], 0)
+        ci = jnp.concatenate([inverse[j, 0:8] for j in range(3)], 0)
+        new = table[0:24] + (grad - (fix[...] - back)) * ci
         zero8 = jnp.zeros((8, 128), F32)
         send_f[...] = jnp.concatenate(
             [new[:, 0:128], zero8, new[:, 128:256], zero8, jnp.zeros((64, 128), F32)], 0
@@ -612,7 +670,7 @@
                 at = 384 * g + 128 * t
                 out_ref[f : f + 1, at : at + 128] = tiles[t][g : g + 1]
 
-    ref = chunks.at[pl.ds(0, NDEV - 1), pl.ds(0, 36), :]
+    ref = chunks.at[pl.ds(0, NDEV - 1), :, pl.ds(0, 12), :]
     pltpu.make_async_copy(ref, ref, big_send).wait()
     rows_wait(recv_t, small_send.at[3])
     rows_wait(recv_d, small_send.at[0])
@@ -626,7 +684,7 @@
     hbm = pl.BlockSpec(memory_space=pl.ANY)
     return pl.pallas_call(
         main_kernel,
-        in_specs=[hbm, hbm, vmem, vmem, vmem, vmem],
+        in_specs=[hbm] * 6,
         out_specs=[vmem] * 2,
         out_shape=[
             jax.ShapeDtypeStruct((2, PX * NDEV), F32),
@@ -635,23 +693,34 @@
         scratch_shapes=[
             v((2, 48, PX * NDEV), F32),
             v((2, 48, PX * NDEV), F32),
+            v((2, PX * NDEV), F32),
+            v((2, 24), jnp.int32),
+            v((2, 3), F32),
+            v((2, 3), F32),
             v((128, LANES), F32),
             v((128, LANES), F32),
-            v((NDEV, 40, 128), F32),
+            v((NDEV, 3, 16, 128), F32),
             v((8, 128), jnp.int32),
             v((2, 8, 128), F32),
             v((2, 8, LANES), F32),
-            v((NDEV, 40, 128), F32),
-            v((96, LANES), F32),
+            v((NDEV, 3, 16, 128), F32),
             v((32, 256), F32),
             v((GROUPS, 256, LANES), BF16),
+            v((GROUPS, LANES, 256), BF16),
             v((128, LANES), BF16),
+            v((LANES, 128), BF16),
+            v((128, LANES), F32),
+            v((GROUPS, 24, LANES), F32),
+            v((GROUPS, 8, LANES), F32),
             v((GROUPS, 144, LANES), F32),
-            v((48, 256), F32),
-            v((48, 256), F32),
+            v((3, 16, 256), F32),
+            v((3, 16, 256), F32),
+            v((GROUPS, 32, LANES), F32),
             v((32, 256), F32),
             v((32, 256), F32),
+            v((144, 256), F32),
             v((8, 256), F32),
+            v((128, LANES), F32),
             v((24, 256), F32),
             v((128, 128), F32),
             v((128, 128), F32),
@@ -661,9 +730,9 @@
             v((128, 128), F32),
             v((128, 128), F32),
             v((128, 128), F32),
-            pltpu.SemaphoreType.DMA((2,)),
+            pltpu.SemaphoreType.DMA((6,)),
             pltpu.SemaphoreType.DMA,
-            pltpu.SemaphoreType.DMA((NDEV,)),
+            pltpu.SemaphoreType.DMA((3, GROUPS)),
             pltpu.SemaphoreType.DMA((4,)),
             pltpu.SemaphoreType.DMA((4,)),
         ],

time: 76.9 us -> 69.9 us (0.909)
  Pallas kernels: 73.4 us -> 66.5 us
    pallas_call x1, Pallas kernels: 73.4 us -> 66.5 us  [run_main(): pl.pallas_call(main_kernel, in_specs=[hbm] * 6, out_specs=[vmem] * 2, out...]
where the time goes in v4:
time: 69.9 us; the launch traced here: 69.7 us
  Pallas kernels  66.5 us (95%)
  local copies, waits for them, and re-layouts  2.58 us (4%)
    pallas_call x1, Pallas kernels, run_main(): pl.pallas_call(main_kernel, in_specs=[hbm] * 6, out_specs=[vmem] * 2, out...  66.5 us
    unnamed x2, local copies, waits for them, and re-layouts  2.58 us

profile of v4, /device:TPU:1, one launch (start us, length us, event | category | flops | bytes accessed | tf_op | source)
XLA Modules:
  0.0 69.7 jit_solution(2887102060620387190)
XLA Ops:
  0.6 66.5 %step.1 = (f32[2,3072]{1,0:T(2,128)}, f32[2,6]{1,0:T(2,128)}) custom-call(f32[2,48,3072]{2,1,0:T(8,128)} %bitcast.5, f32[2,48,3072]{2,1,0:T(8,128)} %bitcast.6, f32[2,3072]{1,0:T(2,128)} %depth_hbm.1, s32[2,24]{1,0:T(2,128)} %target_hbm.1, f32[2,3]{1,0:T(2,128)} %bitcast.7, f32[2,3]{1,0:T(2,128)} %bitcast.8), custom_call_target="tpu_custom_call" | custom-call | tf_op jit(solution)/shard_map/step/pallas_call | solution.py:685
  67.1 1.3 %copy.10 = f32[2,3072]{1,0:T(2,128)} copy(f32[2,3072]{1,0:T(2,128)} %get-tuple-element.8) | data formatting | bytes 49152
  68.5 1.2 %copy.11 = f32[6,2]{0,1:T(2,128)} copy(f32[6,2]{0,1:T(2,128)} %bitcast.9) | data formatting | bytes 96

commit v5 on v4

--- a/solution.py
+++ b/solution.py
@@ -18,7 +18,6 @@
 K_PAIRS = [((a, b), n) for n, (a, b) in enumerate((a, b) for a in range(6) for b in range(a, 6))]
 K_INDEX = {**dict(K_PAIRS), **{(b, a): n for (a, b), n in K_PAIRS}}
 H_ROW = 21
-ARRIVE, LAST, THIRD = 2, 4, 8
 
 
 def lane_iota(shape=(8, 128)):
@@ -126,8 +125,8 @@
     return y[:n] + y[n : 2 * n] + y[2 * n :]
 
 
-def gathered(table, hot):
-    return join3(jnp.dot(split3(table), hot, preferred_element_type=F32))
+def gathered(parts, hot):
+    return join3(jnp.dot(parts, hot, preferred_element_type=F32))
 
 
 def summed(values, hot_t):
@@ -206,23 +205,13 @@
         )
         for g in range(GROUPS)
     ]
-    out[...] = gathered(jnp.concatenate(mine, 0), own[...])
+    out[...] = gathered(split3(jnp.concatenate(mine, 0)), own[...])
 
 
 def rows_of(ref, g):
     return ref[pl.ds(pl.multiple_of(8 * g, 8), 8), :]
 
 
-def add_up(values, g, hot_t, own_t, total_s, total_t):
-    total_t[...] += summed(values, hot_t[g])
-    by_source = summed(values, own_t[...])
-    lane = lane_iota((32, 128))
-    for f in range(2):
-        at = slice(128 * f, 128 * f + 128)
-        moved = pltpu.roll(by_source, (8 * g - 8 * f + 128) % 128, 1)
-        total_s[:, at] += jnp.where(lane // 8 == g, moved, 0.0)
-
-
 def edge_rows(a, j):
     return slice(24 * a + 8 * j, 24 * a + 8 * j + 8)
 
@@ -231,13 +220,21 @@
     acc[row] = value if acc[row] is None else acc[row] + value
 
 
+def source_columns():
+    rows = lax.broadcasted_iota(jnp.int32, (128, LANES), 0)
+    frame = lax.broadcasted_iota(jnp.int32, (1, LANES), 1) // 24
+    return jnp.where(rows == (frame % 2) * 8 + frame // 2, 1.0, 0.0).astype(BF16)
+
+
 def source_columns_t():
-    frame = lax.broadcasted_iota(jnp.int32, (LANES, 1), 0) // 24
-    lanes = lax.broadcasted_iota(jnp.int32, (LANES, 128), 1)
-    return jnp.where(lanes == (frame % 2) * 8 + frame // 2, 1.0, 0.0).astype(BF16)
-
-
-def build_terms(acc, cols, inputs, d, rel, xy, coup, g, j):
+    edge = lax.broadcasted_iota(jnp.int32, (8 * LANES, 1), 0)
+    frame = (edge % LANES) // 24
+    lanes = lax.broadcasted_iota(jnp.int32, (8 * LANES, 128), 1)
+    at = (edge // LANES) * 16 + (frame % 2) * 8 + frame // 2
+    return jnp.where(lanes == at, 1.0, 0.0).astype(BF16)
+
+
+def build_terms(acc, cols, inputs, d, rel, xy, coup, m, j):
     x, y = xy
     fu, fv, cu, cv = inputs
     w0, w1, w2, m0, m1, m2 = [rel[k : 1 + k, cols] for k in range(6)]
@@ -261,7 +258,7 @@
             e = ju[a] * eu + jv[a] * ev
         else:
             e = ju[a] * eu if a in ju else jv[a] * ev
-        coup[g, edge_rows(a, j), cols] = e
+        coup[m, edge_rows(a, j), cols] = e
     su = {a: cu * ju[a] for a in ju}
     sv = {a: cv * jv[a] for a in jv}
     for (a, b), row in K_PAIRS:
@@ -277,9 +274,9 @@
     return eu * ru + ev * rv, eu * du + ev * dv
 
 
-def take_terms(acc, cols, near, coup, g, j):
-    ci, gi = -near[0:8, cols], -near[8:16, cols]
-    e = [coup[g, edge_rows(a, j), cols] for a in range(6)]
+def take_terms(acc, cols, near, coup, m, j):
+    ci, gi = -near[0], -near[1]
+    e = [coup[m, edge_rows(a, j), cols] for a in range(6)]
     for a in range(6):
         scaled = e[a] * ci
         for (k, b), row in K_PAIRS:
@@ -292,71 +289,85 @@
     return [jnp.zeros((8, 128), F32) if x is None else x for x in acc]
 
 
-def phase_pass(g, j, me, recv, recv_t, table, hot, hot_t, from_pose, dep, rel, coup, sums, inverse, kh):
+def tile_cols(t):
+    return slice(128 * t, 128 * t + 128)
+
+
+def pair_at(m, count=1):
+    size = 2 * LANES * count
+    return pl.ds(pl.multiple_of(size * m, 128), size)
+
+
+def phase_pass(
+    m, j, gs, me, recv, recv_t, table3, hot, hot_t, from_pose, dep, rel, coup, sums, inverse3, kh
+):
+    at = pair_at(m)
     if j == 0:
-        rows = lax.broadcasted_iota(jnp.int32, (256, LANES), 0).astype(F32)
-        targets = group_targets(g, recv_t)
-        hot[g] = jnp.where(rows == targets, 1.0, 0.0).astype(BF16)
+        rows = lax.broadcasted_iota(jnp.int32, (256, 2 * LANES), 0).astype(F32)
+        targets = jnp.concatenate([group_targets(g, recv_t) for g in gs], 1)
+        hot[:, at] = jnp.where(rows == targets, 1.0, 0.0).astype(BF16)
         lanes = lane_iota((128, 256)).astype(F32)
-        for t in range(3):
-            at = slice(128 * t, 128 * t + 128)
-            column = jnp.broadcast_to(targets[:, at], (128, 128)).T
+        for t in range(6):
+            column = jnp.broadcast_to(targets[:, tile_cols(t)], (128, 128)).T
             column = jnp.concatenate([column, column], 1)
-            hot_t[g, at, :] = jnp.where(lanes == column, 1.0, 0.0).astype(BF16)
-        near = gathered(table[...], hot[g])
-        dep[g] = near[0:24]
-        relative = rows_of(from_pose, g) - near[24:32]
-        rel[g] = relative
+            to = pl.ds(pl.multiple_of(2 * LANES * m + 128 * t, 128), 128)
+            hot_t[to, :] = jnp.where(lanes == column, 1.0, 0.0).astype(BF16)
+        near = gathered(table3[...], hot[:, at])
+        dep[m] = near[0:24]
+        relative = jnp.concatenate([rows_of(from_pose, g) for g in gs], 1) - near[24:32]
+        rel[m] = relative
     else:
-        relative = rel[g]
-        back = gathered(inverse[j - 1], hot[g])
-    parts = unpack_group(g, j, recv)
+        relative = rel[m]
+        back = gathered(inverse3[j - 1], hot[:, at])
+    parts = [unpack_group(g, j, recv) for g in gs]
     grads, curvs, blocks = [], [], []
     xy = pixel_xy(me, j)
-    for t in range(3):
-        cols = slice(128 * t, 128 * t + 128)
+    for t in range(6):
+        cols = tile_cols(t)
         acc = [None] * 27
-        d = dep[g, 8 * j : 8 * j + 8, cols]
-        tiles = [part[t] for part in parts]
-        gd, cd = build_terms(acc, cols, tiles, d, relative, xy, coup, g, j)
+        d = dep[m, 8 * j : 8 * j + 8, cols]
+        tiles = [part[t % 3] for part in parts[t // 3]]
+        gd, cd = build_terms(acc, cols, tiles, d, relative, xy, coup, m, j)
         grads.append(gd)
         curvs.append(cd)
         if j > 0:
-            take_terms(acc, cols, back, coup, g, j - 1)
+            take_terms(acc, cols, (back[0:8, cols], back[8:16, cols]), coup, m, j - 1)
         blocks.append(merged_rows(filled(acc)))
     both = jnp.concatenate([jnp.concatenate(grads, 1), jnp.concatenate(curvs, 1)], 0)
-    sums[j] += summed(both, hot_t[g])
+    sums[j] += summed(both, hot_t[at, :])
     block = jnp.concatenate(blocks, 1)
-    kh[g] = block if j == 0 else kh[g] + block
-
-
-def source_columns():
-    rows = lax.broadcasted_iota(jnp.int32, (128, LANES), 0)
-    frame = lax.broadcasted_iota(jnp.int32, (1, LANES), 1) // 24
-    return jnp.where(rows == (frame % 2) * 8 + frame // 2, 1.0, 0.0).astype(BF16)
-
-
-def last_pass(g, hot, hot_t, own_t, coup, inverse, kh, total_s, total_t):
-    near = gathered(inverse[2], hot[g])
+    kh[m] = block if j == 0 else kh[m] + block
+
+
+def last_pass(h, hot, hot_t, own_t, coup, inverse3, kh, total_s, total_t):
+    at = pair_at(h, 4)
+    near = gathered(inverse3[2], hot[:, at])
     blocks = []
-    for t in range(3):
+    for t in range(24):
+        m = 4 * h + t // 6
         acc = [None] * 27
-        take_terms(acc, slice(128 * t, 128 * t + 128), near, coup, g, 2)
-        blocks.append(merged_rows(acc))
-    add_up(kh[g] + jnp.concatenate(blocks, 1), g, hot_t, own_t, total_s, total_t)
-
-
-def third_pass(g, hot_t, coup, from_steps, fix):
-    motion = rows_of(from_steps, g)
+        cols = tile_cols(t)
+        take_terms(acc, tile_cols(t % 6), (near[0:8, cols], near[8:16, cols]), coup, m, 2)
+        blocks.append(kh[m, :, tile_cols(t % 6)] + merged_rows(acc))
+    parts = split3(jnp.concatenate(blocks, 1))
+    total_t[...] += join3(jnp.dot(parts, hot_t[at, :], preferred_element_type=F32))
+    total_s[h] = join3(jnp.dot(parts, own_t[...], preferred_element_type=F32))
+
+
+def third_pass(h, gs, hot_t, coup, from_steps, fix):
     parts = []
-    for t in range(3):
-        cols = slice(128 * t, 128 * t + 128)
+    for t in range(24):
+        m, cols = 4 * h + t // 6, tile_cols(t % 6)
+        motion = rows_of(from_steps, gs[t // 3])
         column = []
         for j in range(3):
-            terms = [coup[g, edge_rows(a, j), cols] * motion[a : a + 1, cols] for a in range(6)]
+            terms = [
+                coup[m, edge_rows(a, j), cols] * motion[a : a + 1, tile_cols(t % 3)]
+                for a in range(6)
+            ]
             column.append(((terms[0] + terms[1]) + (terms[2] + terms[3])) + (terms[4] + terms[5]))
         parts.append(jnp.concatenate(column, 0))
-    fix[...] += summed(jnp.concatenate(parts, 1), hot_t[g])
+    fix[...] += summed(jnp.concatenate(parts, 1), hot_t[pair_at(h, 4), :])
 
 
 def solve(matrix, right):
@@ -455,20 +466,20 @@
     return contextlib.nullcontext()
 
 
-def loop(body, times):
+def loop(body, count):
     def step(n, carry):
-        for k in range(times):
-            body(times * n + k)
+        body(n)
         return carry
 
-    lax.fori_loop(0, GROUPS // times, step, 0)
+    lax.fori_loop(0, count, step, 0)
 
 
 def main_kernel(
     flow_hbm, weight_hbm, depth_hbm, target_hbm, rotation_hbm, translation_hbm,
     out_ref, pose_ref,
     flow, weight, depth_ref, target_ref, rotation_ref, translation_ref, low, high, chunks, ints, floats, unfold,
-    recv, table, hot, hot_t, own, own_t, from_pose, dep, rel, coup, sums, inverse, kh,
+    recv, table, table3, hot, hot_t, own, own_t, from_pose, dep, rel, coup, sums, inverse,
+    inverse3, kh,
     total_s, total_t, at_target, steps, from_steps, fix,
     send_t, recv_t, send_d, recv_d, send_e, recv_e, send_f, recv_f,
     in_sem, big_send, big_recv, small_send, small_recv,
@@ -505,14 +516,6 @@
         to_all(far_first(), greet)
 
     with scope("sc_tables"):
-        table[...] = jnp.zeros_like(table)
-        sums[...] = jnp.zeros_like(sums)
-        total_t[...] = jnp.zeros_like(total_t)
-        total_s[...] = jnp.zeros_like(total_s)
-        fix[...] = jnp.zeros_like(fix)
-        at_target[...] = jnp.zeros_like(at_target)
-        own[...] = source_columns()
-        own_t[...] = source_columns_t()
         high[...] = jnp.zeros_like(high)
         for load in loads[:4]:
             load.wait()
@@ -553,57 +556,70 @@
         recv[mine_at, :, 0:12, :] = chunks[me, :, 0:12, :]
 
     with scope("sc_waitt"):
+        for ref in (sums, total_t, fix, at_target):
+            ref[...] = jnp.zeros_like(ref)
+        own[...] = source_columns()
+        own_t[...] = source_columns_t()
         rows_wait(recv_t, small_recv.at[3])
         known = recv_t[...].T
         for f in range(2):
             at = slice(128 * f, 128 * f + 128)
             table[0:24, at] = known[24 * f : 24 * f + 24]
             table[24:32, at] = known[48 + 8 * f : 56 + 8 * f]
+        table3[...] = split3(table[...])
         expand(table[24:32, :], own, from_pose)
 
-    def arrive(n, j):
+    def group_at(n):
         oz, oy = group_offset(n)
-        g = ((my_gz + 4 - oz) % 4) * 4 + (my_gy + 4 - oy) % 4
-
-        def landed(count):
+        return ((my_gz + 4 - oz) % 4) * 4 + (my_gy + 4 - oy) % 4
+
+    def arrive(m, j):
+        gs = [group_at(2 * m), group_at(2 * m + 1)]
+
+        def landed(g, count):
             ref = recv.at[pl.ds(8 * g, count), j, pl.ds(0, 12), :]
             pltpu.make_async_copy(ref, ref, big_recv.at[j, g]).wait()
 
-        pl.when(n == 0)(lambda: landed(7))
-        pl.when(n != 0)(lambda: landed(8))
-
+        pl.when(m == 0)(lambda: landed(gs[0], 7))
+        pl.when(m != 0)(lambda: landed(gs[0], 8))
+        landed(gs[1], 8)
         phase_pass(
-            g, j, me, recv, recv_t, table, hot, hot_t, from_pose, dep, rel, coup, sums,
-            inverse, kh,
+            m, j, gs, me, recv, recv_t, table3, hot, hot_t, from_pose, dep, rel, coup, sums,
+            inverse3, kh,
         )
 
     for j in range(3):
         with scope(f"sc_arrive{j}"):
-            loop(functools.partial(arrive, j=j), ARRIVE)
+            loop(functools.partial(arrive, j=j), 8)
             ci = 1.0 / (0.1 + sums[j, 8:16])
-            inverse[j, 0:8] = ci
-            inverse[j, 8:16] = sums[j, 0:8] * ci
+            both = jnp.concatenate([ci, sums[j, 0:8] * ci], 0)
+            inverse[j] = both
+            inverse3[j] = split3(both)
     with scope("sc_last"):
-        loop(
-            lambda g: last_pass(g, hot, hot_t, own_t, coup, inverse, kh, total_s, total_t), LAST
-        )
+        loop(lambda h: last_pass(h, hot, hot_t, own_t, coup, inverse3, kh, total_s, total_t), 2)
 
     with scope("sc_sendd"):
         kind = lax.broadcasted_iota(jnp.int32, (32, 256), 0)
-        total = total_s[...] + jnp.where(kind < H_ROW, total_t[...], -total_t[...])
+        total = jnp.where(kind < H_ROW, total_t[...], -total_t[...])
         send_d[...] = jnp.concatenate(
             [total[:, 0:128], total[:, 128:256], jnp.zeros((64, 128), F32)], 0
         ).T
+        for h in range(2):
+            by_source = jnp.concatenate([total_s[h], jnp.zeros((96, 128), F32)], 0).T
+            for k in range(8):
+                to = pl.ds(pl.multiple_of(8 * group_at(8 * h + k), 8), 8)
+                first, second = by_source[16 * k : 16 * k + 8], by_source[16 * k + 8 : 16 * k + 16]
+                send_d[to, :] += first + pltpu.roll(second, 32, 1)
         recv_d[pl.ds(mine_at, 1), :] = send_d[pl.ds(mine_at, 1), :]
         rows_exchange(
             send_d, recv_d, lambda _, place: place, mine_at, small_send.at[0], small_recv.at[0]
         )
     with scope("sc_target"):
 
-        def couple(g):
-            at_target[...] += summed(coup[g], hot_t[g])
-
-        loop(couple, 2)
+        def couple(m):
+            at_target[...] += summed(coup[m], hot_t[pair_at(m), :])
+
+        loop(couple, 8)
     with scope("sc_waitd"):
         rows_wait(recv_d, small_recv.at[0])
     with scope("sc_solve"):
@@ -633,7 +649,12 @@
         steps[:, 0:128] = every[0:8]
         steps[:, 128:256] = every[8:16]
         expand(steps[...], own, from_steps)
-        loop(lambda g: third_pass(g, hot_t, coup, from_steps, fix), THIRD)
+        loop(
+            lambda h: third_pass(
+                h, [group_at(8 * h + k) for k in range(8)], hot_t, coup, from_steps, fix
+            ),
+            2,
+        )
     with scope("sc_sendf"):
         back = at_target[0:24] * steps[0:1]
         for a in range(1, 6):
@@ -681,7 +702,7 @@
 def run_main(flow, weight, inv_depth, edge_target, rotation, translation):
     v = pltpu.VMEM
     vmem = pl.BlockSpec(memory_space=pltpu.VMEM)
-    hbm = pl.BlockSpec(memory_space=pl.ANY)
+    hbm = pl.BlockSpec(memory_space=pltpu.HBM)
     return pl.pallas_call(
         main_kernel,
         in_specs=[hbm] * 6,
@@ -705,18 +726,20 @@
             v((2, 8, LANES), F32),
             v((NDEV, 3, 16, 128), F32),
             v((32, 256), F32),
-            v((GROUPS, 256, LANES), BF16),
-            v((GROUPS, LANES, 256), BF16),
+            v((96, 256), BF16),
+            v((256, GROUPS * LANES), BF16),
+            v((GROUPS * LANES, 256), BF16),
             v((128, LANES), BF16),
-            v((LANES, 128), BF16),
+            v((8 * LANES, 128), BF16),
             v((128, LANES), F32),
-            v((GROUPS, 24, LANES), F32),
-            v((GROUPS, 8, LANES), F32),
-            v((GROUPS, 144, LANES), F32),
+            v((8, 24, 2 * LANES), F32),
+            v((8, 8, 2 * LANES), F32),
+            v((8, 144, 2 * LANES), F32),
             v((3, 16, 256), F32),
             v((3, 16, 256), F32),
-            v((GROUPS, 32, LANES), F32),
-            v((32, 256), F32),
+            v((3, 48, 256), BF16),
+            v((8, 32, 2 * LANES), F32),
+            v((2, 32, 128), F32),
             v((32, 256), F32),
             v((144, 256), F32),
             v((8, 256), F32),

time: 69.9 us -> 67.5 us (0.966)
  Pallas kernels: 66.5 us -> 64.1 us
    pallas_call x1, Pallas kernels: 66.5 us -> 64.1 us  [run_main(): pl.pallas_call(main_kernel, in_specs=[hbm] * 6, out_specs=[vmem] * 2, out...]
where the time goes in v5:
time: 67.5 us; the launch traced here: 67.3 us
  Pallas kernels  64.1 us (95%)
  local copies, waits for them, and re-layouts  2.58 us (4%)
    pallas_call x1, Pallas kernels, run_main(): pl.pallas_call(main_kernel, in_specs=[hbm] * 6, out_specs=[vmem] * 2, out...  64.1 us
    unnamed x2, local copies, waits for them, and re-layouts  2.58 us

profile of v5, /device:TPU:1, one launch (start us, length us, event | category | flops | bytes accessed | tf_op | source)
XLA Modules:
  0.0 67.3 jit_solution(13604226247822554132)
XLA Ops:
  0.6 64.1 %step.1 = (f32[2,3072]{1,0:T(2,128)}, f32[2,6]{1,0:T(2,128)}) custom-call(f32[2,48,3072]{2,1,0:T(8,128)} %bitcast.5, f32[2,48,3072]{2,1,0:T(8,128)} %bitcast.6, f32[2,3072]{1,0:T(2,128)} %depth_hbm.1, s32[2,24]{1,0:T(2,128)} %target_hbm.1, f32[2,3]{1,0:T(2,128)} %bitcast.7, f32[2,3]{1,0:T(2,128)} %bitcast.8), custom_call_target="tpu_custom_call" | custom-call | tf_op jit(solution)/shard_map/step/pallas_call | solution.py:706
  64.7 1.3 %copy.10 = f32[2,3072]{1,0:T(2,128)} copy(f32[2,3072]{1,0:T(2,128)} %get-tuple-element.8) | data formatting | bytes 49152
  66.0 1.2 %copy.11 = f32[6,2]{0,1:T(2,128)} copy(f32[6,2]{0,1:T(2,128)} %bitcast.9) | data formatting | bytes 96

commit v6 on v5

--- a/solution.py
+++ b/solution.py
@@ -399,6 +399,10 @@
     return min(d, 4 - d)
 
 
+def hops(offset):
+    return ring_steps(offset[0]) + ring_steps(offset[1]) + ring_steps(offset[2])
+
+
 def far_first():
     offsets = [
         (dz, dy, dx, dc)
@@ -408,21 +412,22 @@
         for dc in range(2)
         if (dz, dy, dx, dc) != (0, 0, 0, 0)
     ]
-    return sorted(offsets, key=lambda o: -(ring_steps(o[0]) + ring_steps(o[1]) + ring_steps(o[2])))
+    return sorted(offsets, key=lambda o: -hops(o))
 
 
 def group_offset(n):
     return (n // 4 + n) % 4, n % 4
 
 
-def by_group():
+def by_group(far_ahead=False):
     order = []
     for n in range(GROUPS):
         oz, oy = group_offset(n)
-        for dx in range(4):
-            for dc in range(2):
-                order.append(((oz + dx) % 4, (oy + dx) % 4, dx, dc))
-    return order[1:]
+        members = [
+            ((oz + dx) % 4, (oy + dx) % 4, dx, dc) for dx in range(4) for dc in range(2)
+        ]
+        order += sorted(members, key=lambda o: -hops(o)) if far_ahead else members
+    return [o for o in order if o != (0, 0, 0, 0)]
 
 
 def to_all(order, act):
@@ -457,8 +462,22 @@
     to_all(far_first(), act)
 
 
-def rows_wait(buf, sem):
-    ref = buf.at[pl.ds(0, NDEV - 1), :]
+def steps_exchange(order, send, source, recv, slot, send_sem, recv_sem):
+    def act(d, _):
+        pltpu.make_async_remote_copy(
+            src_ref=send.at[pl.ds(source, 1), :],
+            dst_ref=recv.at[pl.ds(slot, 1), :],
+            send_sem=send_sem,
+            recv_sem=recv_sem,
+            device_id=d,
+            device_id_type=pl.DeviceIdType.LOGICAL,
+        ).start()
+
+    to_all(order, act)
+
+
+def rows_wait(buf, sem, count=NDEV - 1):
+    ref = buf.at[pl.ds(0, count), :]
     pltpu.make_async_copy(ref, ref, sem).wait()
 
 
@@ -481,7 +500,7 @@
     recv, table, table3, hot, hot_t, own, own_t, from_pose, dep, rel, coup, sums, inverse,
     inverse3, kh,
     total_s, total_t, at_target, steps, from_steps, fix,
-    send_t, recv_t, send_d, recv_d, send_e, recv_e, send_f, recv_f,
+    send_t, recv_t, sum_d, send_d, recv_d, send_e, recv_e, send_f, recv_f,
     in_sem, big_send, big_recv, small_send, small_recv,
 ):
     row, col = lax.axis_index("row"), lax.axis_index("col")
@@ -490,6 +509,7 @@
     my_gz, my_gy = (row + 4 - x) % 4, (y + 4 - x) % 4
     my_group = my_gz * 4 + my_gy
     mine_at = my_group * 8 + col % 8
+    other_at = my_group * 8 + (col + 4) % 8
     lane = lane_iota()
     barrier = pltpu.get_barrier_semaphore()
 
@@ -552,7 +572,7 @@
                     device_id_type=pl.DeviceIdType.LOGICAL,
                 ).start()
 
-            to_all(by_group(), send_chunk)
+            to_all(by_group(far_ahead=j == 2), send_chunk)
         recv[mine_at, :, 0:12, :] = chunks[me, :, 0:12, :]
 
     with scope("sc_waitt"):
@@ -601,7 +621,7 @@
     with scope("sc_sendd"):
         kind = lax.broadcasted_iota(jnp.int32, (32, 256), 0)
         total = jnp.where(kind < H_ROW, total_t[...], -total_t[...])
-        send_d[...] = jnp.concatenate(
+        by_target = jnp.concatenate(
             [total[:, 0:128], total[:, 128:256], jnp.zeros((64, 128), F32)], 0
         ).T
         for h in range(2):
@@ -609,7 +629,10 @@
             for k in range(8):
                 to = pl.ds(pl.multiple_of(8 * group_at(8 * h + k), 8), 8)
                 first, second = by_source[16 * k : 16 * k + 8], by_source[16 * k + 8 : 16 * k + 16]
-                send_d[to, :] += first + pltpu.roll(second, 32, 1)
+                sum_d[to, :] = first + pltpu.roll(second, 32, 1)
+        rows = by_target + sum_d[...]
+        opposite = [pltpu.roll(rows[8 * g : 8 * g + 8], 4, 0) for g in range(GROUPS)]
+        send_d[...] = rows + pltpu.roll(jnp.concatenate(opposite, 0), 64, 1)
         recv_d[pl.ds(mine_at, 1), :] = send_d[pl.ds(mine_at, 1), :]
         rows_exchange(
             send_d, recv_d, lambda _, place: place, mine_at, small_send.at[0], small_recv.at[0]
@@ -626,7 +649,8 @@
         line = jnp.sum(recv_d[...], axis=0, keepdims=True)
         sub = lax.broadcasted_iota(jnp.int32, (8, 128), 0)
         lines = jnp.broadcast_to(line, (8, 128))
-        lines = jnp.where(sub == 1, pltpu.roll(lines, 96, 1), lines)
+        for f in range(1, 4):
+            lines = jnp.where(sub == f, pltpu.roll(lines, 128 - 32 * f, 1), lines)
         full = jnp.concatenate([lines, jnp.zeros((120, 128), F32)], 0).T
         z = solve(
             lambda i, j: full[K_INDEX[i, j] : K_INDEX[i, j] + 1, :],
@@ -635,15 +659,18 @@
         zs = jnp.concatenate([*z, jnp.zeros((122, 128), F32)], 0)
         turned = zs.T
         pose_ref[...] = turned[0:2, 0:6]
-        mine = turned[0:1] + pltpu.roll(turned[0:8], 8, 1)[1:2]
-        send_e[...] = jnp.broadcast_to(mine, (8, 128))
+        later = pltpu.roll(turned[0:8], 8, 1)
+        mine, other = turned[0:1] + later[1:2], turned[2:3] + later[3:4]
+        send_e[...] = jnp.where(sub == 0, mine, other)
         recv_e[pl.ds(mine_at, 1), :] = mine
+        recv_e[pl.ds(other_at, 1), :] = other
     with scope("sc_sende"):
-        rows_exchange(
-            send_e, recv_e, lambda d, _: 0, mine_at, small_send.at[1], small_recv.at[1]
-        )
+        near = [o for o in far_first() if hops(o) <= 3]
+        steps_exchange(near, send_e, 0, recv_e, mine_at, small_send.at[1], small_recv.at[1])
+        near = [o for o in near if hops(o) <= 2]
+        steps_exchange(near, send_e, 1, recv_e, other_at, small_send.at[1], small_recv.at[1])
     with scope("sc_waite"):
-        rows_wait(recv_e, small_recv.at[1])
+        rows_wait(recv_e, small_recv.at[1], NDEV - 2)
     with scope("sc_third"):
         every = recv_e[...].T
         steps[:, 0:128] = every[0:8]
@@ -695,7 +722,7 @@
     pltpu.make_async_copy(ref, ref, big_send).wait()
     rows_wait(recv_t, small_send.at[3])
     rows_wait(recv_d, small_send.at[0])
-    rows_wait(recv_e, small_send.at[1])
+    rows_wait(recv_e, small_send.at[1], NDEV - 2)
     rows_wait(recv_f, small_send.at[2])
 
 
@@ -749,6 +776,7 @@
             v((128, 128), F32),
             v((128, 128), F32),
             v((128, 128), F32),
+            v((128, 128), F32),
             v((8, 128), F32),
             v((128, 128), F32),
             v((128, 128), F32),
@@ -766,11 +794,29 @@
     )(flow, weight, inv_depth, edge_target, rotation, translation)
 
 
+def hand_over(*results):
+    def kernel(depth, pose, depth_out, pose_out):
+        depth_out[...] = depth[...]
+        pose_out[...] = pose[...]
+
+    vmem = pl.BlockSpec(memory_space=pltpu.VMEM)
+    return pl.pallas_call(
+        kernel,
+        in_specs=[vmem] * 2,
+        out_specs=[vmem] * 2,
+        out_shape=[jax.ShapeDtypeStruct(r.shape, r.dtype) for r in results],
+        compiler_params=pltpu.CompilerParams(vmem_limit_bytes=56 * 1024 * 1024),
+        name="hand_over",
+    )(*results)
+
+
 def shards(inv_depth, rotation, translation, edge_target, flow_obs, weight):
     pixels = inv_depth.shape[1]
     flow = flow_obs.reshape(2, 48, pixels)
     wts = weight.reshape(2, 48, pixels)
-    depth, pose = run_main(flow, wts, inv_depth, edge_target, rotation.T, translation.T)
+    depth, pose = hand_over(
+        *run_main(flow, wts, inv_depth, edge_target, rotation.T, translation.T)
+    )
     return depth, pose.T
 
 

time: 67.5 us -> 65.5 us (0.970)
  local copies, waits for them, and re-layouts: 2.58 us -> 0 us
    unnamed x2 -> x0, local copies, waits for them, and re-layouts: 2.58 us -> none
    pallas_call x0 -> x1, Pallas kernels: none -> 1.35 us  [hand_over(): pl.pallas_call(kernel, in_specs=[vmem] * 2, out_specs=[vmem] * 2, out_sha...]
    pallas_call x1, Pallas kernels: 64.1 us -> 63.3 us  [run_main(): pl.pallas_call(main_kernel, in_specs=[hbm] * 6, out_specs=[vmem] * 2, out...]
where the time goes in v6:
time: 65.5 us; the launch traced here: 65.3 us
  Pallas kernels  64.7 us (99%)
    pallas_call x1, Pallas kernels, run_main(): pl.pallas_call(main_kernel, in_specs=[hbm] * 6, out_specs=[vmem] * 2, out...  63.3 us
    pallas_call x1, Pallas kernels, hand_over(): pl.pallas_call(kernel, in_specs=[vmem] * 2, out_specs=[vmem] * 2, out_sha...  1.35 us

profile of v6, /device:TPU:1, one launch (start us, length us, event | category | flops | bytes accessed | tf_op | source)
XLA Modules:
  0.0 65.3 jit_solution(6410169442675524282)
XLA Ops:
  0.6 63.3 %step.1 = (f32[2,3072]{1,0:T(2,128)}, f32[2,6]{1,0:T(2,128)}) custom-call(f32[2,48,3072]{2,1,0:T(8,128)} %bitcast.5, f32[2,48,3072]{2,1,0:T(8,128)} %bitcast.6, f32[2,3072]{1,0:T(2,128)} %depth_hbm.1, s32[2,24]{1,0:T(2,128)} %target_hbm.1, f32[2,3]{1,0:T(2,128)} %bitcast.7, f32[2,3]{1,0:T(2,128)} %bitcast.8), custom_call_target="tpu_custom_call" | custom-call | tf_op jit(solution)/shard_map/step/pallas_call | solution.py:733
  63.9 1.4 %hand_over.1 = (f32[2,3072]{1,0:T(2,128)}, f32[2,6]{1,0:T(2,128)}) custom-call(f32[2,3072]{1,0:T(2,128)} %get-tuple-element.6.depth, f32[2,6]{1,0:T(2,128)} %get-tuple-element.7.pose), custom_call_target="tpu_custom_call" | custom-call | tf_op jit(solution)/shard_map/hand_over/pallas_call | solution.py:803

commit v7 on v6

--- a/solution.py
+++ b/solution.py
@@ -24,8 +24,8 @@
     return lax.broadcasted_iota(jnp.int32, shape, 1)
 
 
-def pack_block(n, turn, flow, weight, low, high, out):
-    cols = pl.ds(pl.multiple_of(n * LANES, 128), LANES)
+def pack_half(b, j, turn, flow, weight, low, high, out):
+    cols = pl.ds(pl.multiple_of((2 * j + b) * 512, 512), 512)
 
     def put(ref, block, value):
         at = pl.multiple_of(((3 * turn + block) % 8) * 16, 16)
@@ -41,13 +41,11 @@
     low_t = low[...].T
     high_t = high[...].T
     where_at = (lane_iota() - 48 * turn + 384) % 128
-    for d in range(16):
-        for j in range(3):
-            at = 24 * d + 8 * j
-            out[16 * n + d, j, 0:8, :] = low_t[at : at + 8]
-            rest = high_t[at : at + 8]
-            turned = pltpu.roll(pltpu.roll(rest, 64, 1), 4, 0)
-            out[16 * n + d, j, 8:12, :] = jnp.where(where_at < 64, rest, turned)[0:4]
+    for d in range(64):
+        out[64 * b + d, j, 0:8, :] = low_t[8 * d : 8 * d + 8]
+        rest = high_t[8 * d : 8 * d + 8]
+        turned = pltpu.roll(pltpu.roll(rest, 64, 1), 4, 0)
+        out[64 * b + d, j, 8:12, :] = jnp.where(where_at < 64, rest, turned)[0:4]
 
 
 def own_edges(target_ref, rotation_ref, translation_ref, ints, floats):
@@ -70,17 +68,17 @@
     poses = pltpu.roll(pose, 48, 1)[0:1] + pltpu.roll(pose, 56, 1)[1:2]
     known = jnp.where(lane < 64, poses, pltpu.roll(column, 64, 1)[0:1])
     for f in range(2):
-        for g in range(8):
-            unfold[f, g : g + 1, :] = depth_ref[f : f + 1, LANES * g : LANES * g + LANES]
+        for j in range(3):
+            for g in range(8):
+                at = 128 * (8 * j + g)
+                unfold[f, j, g : g + 1, :] = depth_ref[f : f + 1, at : at + 128]
     for i in range(16):
         acc = known
         for f in range(2):
-            for t in range(3):
-                a, b = max(24 * i - 128 * t, 0), min(24 * i + 24 - 128 * t, 128)
-                if a < b:
-                    shift = 24 * f - (24 * i - 128 * t)
-                    moved = pltpu.roll(unfold[f, :, 128 * t : 128 * t + 128], shift % 128, 1)
-                    acc = jnp.where((lane >= a + shift) & (lane < b + shift), moved, acc)
+            for j in range(3):
+                to = 24 * f + 8 * j
+                moved = pltpu.roll(unfold[f, j], (to - 8 * i) % 128, 1)
+                acc = jnp.where((lane >= to) & (lane < to + 8), moved, acc)
         send[8 * i : 8 * i + 8, :] = acc
 
 
@@ -189,7 +187,7 @@
 
 
 def pixel_xy(me, j):
-    p = me * PX + 8 * j + lax.broadcasted_iota(jnp.int32, (8, 128), 0)
+    p = 8 * NDEV * j + 8 * me + lax.broadcasted_iota(jnp.int32, (8, 128), 0)
     x = ((p % 64).astype(F32) + 0.5) / 64 - 0.5
     y = ((p // 64).astype(F32) + 0.5 - 24.0) / 64
     return x, y
@@ -419,9 +417,9 @@
     return (n // 4 + n) % 4, n % 4
 
 
-def by_group(far_ahead=False):
+def pair_order(m, far_ahead):
     order = []
-    for n in range(GROUPS):
+    for n in (2 * m, 2 * m + 1):
         oz, oy = group_offset(n)
         members = [
             ((oz + dx) % 4, (oy + dx) % 4, dx, dc) for dx in range(4) for dc in range(2)
@@ -546,12 +544,15 @@
         for load in loads[4:]:
             load.wait()
 
-    def pack(n, carry):
-        pack_block(n, turn, flow, weight, low, high, chunks)
-        return carry
+    def pack(j):
+        def step(b, carry):
+            pack_half(b, j, turn, flow, weight, low, high, chunks)
+            return carry
+
+        lax.fori_loop(0, 2, step, 0)
 
     with scope("sc_pack"):
-        lax.fori_loop(0, 8, pack, 0)
+        pack(0)
     with scope("sc_barrier"):
         pl.semaphore_wait(barrier, NDEV - 1)
 
@@ -560,19 +561,26 @@
             send_t, recv_t, lambda d, _: slot_of(d), mine_at, small_send.at[3], small_recv.at[3]
         )
 
-        for j in range(3):
-
-            def send_chunk(d, _):
-                pltpu.make_async_remote_copy(
-                    src_ref=chunks.at[d, j, pl.ds(0, 12), :],
-                    dst_ref=recv.at[mine_at, j, pl.ds(0, 12), :],
-                    send_sem=big_send,
-                    recv_sem=big_recv.at[j, my_group],
-                    device_id=d,
-                    device_id_type=pl.DeviceIdType.LOGICAL,
-                ).start()
-
-            to_all(by_group(far_ahead=j == 2), send_chunk)
+        def send_phase(j):
+            for m in range(8):
+
+                def send_chunk(d, _):
+                    pltpu.make_async_remote_copy(
+                        src_ref=chunks.at[d, j, pl.ds(0, 12), :],
+                        dst_ref=recv.at[mine_at, j, pl.ds(0, 12), :],
+                        send_sem=big_send,
+                        recv_sem=big_recv.at[j, m],
+                        device_id=d,
+                        device_id_type=pl.DeviceIdType.LOGICAL,
+                    ).start()
+
+                to_all(pair_order(m, j == 2), send_chunk)
+
+        send_phase(0)
+        pack(1)
+        pack(2)
+        send_phase(1)
+        send_phase(2)
         recv[mine_at, :, 0:12, :] = chunks[me, :, 0:12, :]
 
     with scope("sc_waitt"):
@@ -596,13 +604,12 @@
     def arrive(m, j):
         gs = [group_at(2 * m), group_at(2 * m + 1)]
 
-        def landed(g, count):
-            ref = recv.at[pl.ds(8 * g, count), j, pl.ds(0, 12), :]
-            pltpu.make_async_copy(ref, ref, big_recv.at[j, g]).wait()
-
-        pl.when(m == 0)(lambda: landed(gs[0], 7))
-        pl.when(m != 0)(lambda: landed(gs[0], 8))
-        landed(gs[1], 8)
+        def landed(count):
+            ref = recv.at[pl.ds(0, count), j, pl.ds(0, 12), :]
+            pltpu.make_async_copy(ref, ref, big_recv.at[j, m]).wait()
+
+        pl.when(m == 0)(lambda: landed(15))
+        pl.when(m != 0)(lambda: landed(16))
         phase_pass(
             m, j, gs, me, recv, recv_t, table3, hot, hot_t, from_pose, dep, rel, coup, sums,
             inverse3, kh,
@@ -701,22 +708,15 @@
     with scope("sc_waitf"):
         rows_wait(recv_f, small_recv.at[2])
     for f in range(2):
-        tiles = [None] * 3
-        for i in range(16):
-            piece = recv_f[8 * i : 8 * i + 8, :]
-            first = 24 * i
-            moved = pltpu.roll(piece, (first - 32 * f) % 128, 1)
-            for t in range(3):
-                a, b = max(first - 128 * t, 0), min(first + 24 - 128 * t, 128)
-                if a < b:
-                    if tiles[t] is None:
-                        tiles[t] = moved
-                    else:
-                        tiles[t] = jnp.where((lane >= a) & (lane < b), moved, tiles[t])
-        for g in range(8):
-            for t in range(3):
-                at = 384 * g + 128 * t
-                out_ref[f : f + 1, at : at + 128] = tiles[t][g : g + 1]
+        for j in range(3):
+            tile = None
+            for i in range(16):
+                shift = 8 * i - 32 * f - 8 * j
+                moved = pltpu.roll(recv_f[8 * i : 8 * i + 8, :], shift % 128, 1)
+                tile = moved if i == 0 else jnp.where(lane >= 8 * i, moved, tile)
+            for g in range(8):
+                at = 128 * (8 * j + g)
+                out_ref[f : f + 1, at : at + 128] = tile[g : g + 1]
 
     ref = chunks.at[pl.ds(0, NDEV - 1), :, pl.ds(0, 12), :]
     pltpu.make_async_copy(ref, ref, big_send).wait()
@@ -745,12 +745,12 @@
             v((2, 24), jnp.int32),
             v((2, 3), F32),
             v((2, 3), F32),
-            v((128, LANES), F32),
-            v((128, LANES), F32),
+            v((128, 512), F32),
+            v((128, 512), F32),
             v((NDEV, 3, 16, 128), F32),
             v((8, 128), jnp.int32),
             v((2, 8, 128), F32),
-            v((2, 8, LANES), F32),
+            v((2, 3, 8, 128), F32),
             v((NDEV, 3, 16, 128), F32),
             v((32, 256), F32),
             v((96, 256), BF16),
@@ -783,7 +783,7 @@
             v((128, 128), F32),
             pltpu.SemaphoreType.DMA((6,)),
             pltpu.SemaphoreType.DMA,
-            pltpu.SemaphoreType.DMA((3, GROUPS)),
+            pltpu.SemaphoreType.DMA((3, GROUPS // 2)),
             pltpu.SemaphoreType.DMA((4,)),
             pltpu.SemaphoreType.DMA((4,)),
         ],

time: 65.5 us -> 65.2 us (level)
  no operation moved by 1% of the time
where the time goes in v7:
time: 65.2 us; the launch traced here: 65 us
  Pallas kernels  64.3 us (99%)
    pallas_call x1, Pallas kernels, run_main(): pl.pallas_call(main_kernel, in_specs=[hbm] * 6, out_specs=[vmem] * 2, out...  63 us
    pallas_call x1, Pallas kernels, hand_over(): pl.pallas_call(kernel, in_specs=[vmem] * 2, out_specs=[vmem] * 2, out_sha...  1.35 us

profile of v7, /device:TPU:1, one launch (start us, length us, event | category | flops | bytes accessed | tf_op | source)
XLA Modules:
  0.0 65.0 jit_solution(7025820083317760830)
XLA Ops:
  0.6 63.0 %step.1 = (f32[2,3072]{1,0:T(2,128)}, f32[2,6]{1,0:T(2,128)}) custom-call(f32[2,48,3072]{2,1,0:T(8,128)} %bitcast.5, f32[2,48,3072]{2,1,0:T(8,128)} %bitcast.6, f32[2,3072]{1,0:T(2,128)} %depth_hbm.1, s32[2,24]{1,0:T(2,128)} %target_hbm.1, f32[2,3]{1,0:T(2,128)} %bitcast.7, f32[2,3]{1,0:T(2,128)} %bitcast.8), custom_call_target="tpu_custom_call" | custom-call | tf_op jit(solution)/shard_map/step/pallas_call | solution.py:733
  63.6 1.4 %hand_over.1 = (f32[2,3072]{1,0:T(2,128)}, f32[2,6]{1,0:T(2,128)}) custom-call(f32[2,3072]{1,0:T(2,128)} %get-tuple-element.6.depth, f32[2,6]{1,0:T(2,128)} %get-tuple-element.7.pose), custom_call_target="tpu_custom_call" | custom-call | tf_op jit(solution)/shard_map/hand_over/pallas_call | solution.py:803

commit v8 on v7

--- a/solution.py
+++ b/solution.py
@@ -493,13 +493,13 @@
 
 def main_kernel(
     flow_hbm, weight_hbm, depth_hbm, target_hbm, rotation_hbm, translation_hbm,
-    out_ref, pose_ref,
+    recv_f, pose_hbm,
     flow, weight, depth_ref, target_ref, rotation_ref, translation_ref, low, high, chunks, ints, floats, unfold,
     recv, table, table3, hot, hot_t, own, own_t, from_pose, dep, rel, coup, sums, inverse,
     inverse3, kh,
     total_s, total_t, at_target, steps, from_steps, fix,
-    send_t, recv_t, sum_d, send_d, recv_d, send_e, recv_e, send_f, recv_f,
-    in_sem, big_send, big_recv, small_send, small_recv,
+    send_t, recv_t, sum_d, send_d, recv_d, send_e, recv_e, send_f, pose_ref,
+    in_sem, out_sem, big_send, big_recv, small_send, small_recv,
 ):
     row, col = lax.axis_index("row"), lax.axis_index("col")
     me = row * 32 + col
@@ -666,6 +666,8 @@
         zs = jnp.concatenate([*z, jnp.zeros((122, 128), F32)], 0)
         turned = zs.T
         pose_ref[...] = turned[0:2, 0:6]
+        pose_out = pltpu.make_async_copy(pose_ref, pose_hbm, out_sem.at[0])
+        pose_out.start()
         later = pltpu.roll(turned[0:8], 8, 1)
         mine, other = turned[0:1] + later[1:2], turned[2:3] + later[3:4]
         send_e[...] = jnp.where(sub == 0, mine, other)
@@ -701,23 +703,17 @@
             [new[:, 0:128], zero8, new[:, 128:256], zero8, jnp.zeros((64, 128), F32)], 0
         ).T
         slot = slot_of(me)
-        recv_f[pl.ds(slot, 1), :] = send_f[pl.ds(mine_at, 1), :]
+        own_row = pltpu.make_async_copy(
+            send_f.at[pl.ds(mine_at, 1), :], recv_f.at[pl.ds(slot, 1), :], out_sem.at[1]
+        )
+        own_row.start()
         rows_exchange(
             send_f, recv_f, lambda _, place: place, slot, small_send.at[2], small_recv.at[2]
         )
     with scope("sc_waitf"):
         rows_wait(recv_f, small_recv.at[2])
-    for f in range(2):
-        for j in range(3):
-            tile = None
-            for i in range(16):
-                shift = 8 * i - 32 * f - 8 * j
-                moved = pltpu.roll(recv_f[8 * i : 8 * i + 8, :], shift % 128, 1)
-                tile = moved if i == 0 else jnp.where(lane >= 8 * i, moved, tile)
-            for g in range(8):
-                at = 128 * (8 * j + g)
-                out_ref[f : f + 1, at : at + 128] = tile[g : g + 1]
-
+    own_row.wait()
+    pose_out.wait()
     ref = chunks.at[pl.ds(0, NDEV - 1), :, pl.ds(0, 12), :]
     pltpu.make_async_copy(ref, ref, big_send).wait()
     rows_wait(recv_t, small_send.at[3])
@@ -728,14 +724,13 @@
 
 def run_main(flow, weight, inv_depth, edge_target, rotation, translation):
     v = pltpu.VMEM
-    vmem = pl.BlockSpec(memory_space=pltpu.VMEM)
     hbm = pl.BlockSpec(memory_space=pltpu.HBM)
     return pl.pallas_call(
         main_kernel,
         in_specs=[hbm] * 6,
-        out_specs=[vmem] * 2,
+        out_specs=[hbm] * 2,
         out_shape=[
-            jax.ShapeDtypeStruct((2, PX * NDEV), F32),
+            jax.ShapeDtypeStruct((NDEV, 128), F32),
             jax.ShapeDtypeStruct((2, 6), F32),
         ],
         scratch_shapes=[
@@ -780,8 +775,9 @@
             v((8, 128), F32),
             v((128, 128), F32),
             v((128, 128), F32),
-            v((128, 128), F32),
+            v((2, 6), F32),
             pltpu.SemaphoreType.DMA((6,)),
+            pltpu.SemaphoreType.DMA((2,)),
             pltpu.SemaphoreType.DMA,
             pltpu.SemaphoreType.DMA((3, GROUPS // 2)),
             pltpu.SemaphoreType.DMA((4,)),
@@ -794,20 +790,33 @@
     )(flow, weight, inv_depth, edge_target, rotation, translation)
 
 
-def hand_over(*results):
-    def kernel(depth, pose, depth_out, pose_out):
-        depth_out[...] = depth[...]
-        pose_out[...] = pose[...]
+def hand_over(parts, pose):
+    def kernel(recv_f, pose_ref, out_ref, pose_out):
+        lane = lane_iota()
+        pose_out[...] = pose_ref[...]
+        for f in range(2):
+            for j in range(3):
+                tile = None
+                for i in range(16):
+                    shift = 8 * i - 32 * f - 8 * j
+                    moved = pltpu.roll(recv_f[8 * i : 8 * i + 8, :], shift % 128, 1)
+                    tile = moved if i == 0 else jnp.where(lane >= 8 * i, moved, tile)
+                for g in range(8):
+                    at = 128 * (8 * j + g)
+                    out_ref[f : f + 1, at : at + 128] = tile[g : g + 1]
 
     vmem = pl.BlockSpec(memory_space=pltpu.VMEM)
     return pl.pallas_call(
         kernel,
         in_specs=[vmem] * 2,
         out_specs=[vmem] * 2,
-        out_shape=[jax.ShapeDtypeStruct(r.shape, r.dtype) for r in results],
+        out_shape=[
+            jax.ShapeDtypeStruct((2, PX * NDEV), F32),
+            jax.ShapeDtypeStruct((2, 6), F32),
+        ],
         compiler_params=pltpu.CompilerParams(vmem_limit_bytes=56 * 1024 * 1024),
         name="hand_over",
-    )(*results)
+    )(parts, pose)
 
 
 def shards(inv_depth, rotation, translation, edge_target, flow_obs, weight):

time: 65.2 us -> 64.8 us (level)
  no operation moved by 1% of the time
where the time goes in v8:
time: 64.8 us; the launch traced here: 64.6 us
  Pallas kernels  63.9 us (99%)
    pallas_call x1, Pallas kernels, run_main(): pl.pallas_call(main_kernel, in_specs=[hbm] * 6, out_specs=[hbm] * 2, out_...  62.3 us
    pallas_call x1, Pallas kernels, hand_over(): pl.pallas_call(kernel, in_specs=[vmem] * 2, out_specs=[vmem] * 2, out_sha...  1.62 us

profile of v8, /device:TPU:1, one launch (start us, length us, event | category | flops | bytes accessed | tf_op | source)
XLA Modules:
  0.0 64.6 jit_solution(4574690396496796487)
XLA Ops:
  0.6 62.3 %step.1 = (f32[128,128]{1,0:T(8,128)}, f32[2,6]{1,0:T(2,128)}) custom-call(f32[2,48,3072]{2,1,0:T(8,128)} %bitcast.5, f32[2,48,3072]{2,1,0:T(8,128)} %bitcast.6, f32[2,3072]{1,0:T(2,128)} %depth_hbm.1, s32[2,24]{1,0:T(2,128)} %target_hbm.1, f32[2,3]{1,0:T(2,128)} %bitcast.7, f32[2,3]{1,0:T(2,128)} %bitcast.8), custom_call_target="tpu_custom_call" | custom-call | tf_op jit(solution)/shard_map/step/pallas_call | solution.py:728
  62.9 1.6 %hand_over.1 = (f32[2,3072]{1,0:T(2,128)}, f32[2,6]{1,0:T(2,128)}) custom-call(f32[128,128]{1,0:T(8,128)} %get-tuple-element.6.recv_f, f32[2,6]{1,0:T(2,128)} %get-tuple-element.7.pose_ref), custom_call_target="tpu_custom_call" | custom-call | tf_op jit(solution)/shard_map/hand_over/pallas_call | solution.py:809

commit v9 on v8

--- a/solution.py
+++ b/solution.py
@@ -369,7 +369,7 @@
 
 
 def solve(matrix, right):
-    factor = {}
+    factor, scale = {}, {}
     for i in range(6):
         for j in range(i + 1):
             e = matrix(i, j)
@@ -377,19 +377,22 @@
                 e = e * 1.1 + 0.001
             for k in range(j):
                 e = e - factor[i, k] * factor[j, k]
-            factor[i, j] = jnp.sqrt(e) if i == j else e / factor[j, j]
+            if i == j:
+                scale[i] = 1.0 / jnp.sqrt(e)
+            else:
+                factor[i, j] = e * scale[j]
     forward = []
     for i in range(6):
         e = right(i)
         for k in range(i):
             e = e - factor[i, k] * forward[k]
-        forward.append(e / factor[i, i])
+        forward.append(e * scale[i])
     z = [None] * 6
     for i in reversed(range(6)):
         e = forward[i]
         for k in range(i + 1, 6):
             e = e - factor[k, i] * z[k]
-        z[i] = e / factor[i, i]
+        z[i] = e * scale[i]
     return z
 
 

time: 64.8 us -> 64.8 us (level)
  no operation moved by 1% of the time
where the time goes in v9:
time: 64.8 us; the launch traced here: 64.6 us
  Pallas kernels  63.9 us (99%)
    pallas_call x1, Pallas kernels, run_main(): pl.pallas_call(main_kernel, in_specs=[hbm] * 6, out_specs=[hbm] * 2, out_...  62.3 us
    pallas_call x1, Pallas kernels, hand_over(): pl.pallas_call(kernel, in_specs=[vmem] * 2, out_specs=[vmem] * 2, out_sha...  1.62 us

profile of v9, /device:TPU:1, one launch (start us, length us, event | category | flops | bytes accessed | tf_op | source)
XLA Modules:
  0.0 64.6 jit_solution(7938680009042046749)
XLA Ops:
  0.6 62.3 %step.1 = (f32[128,128]{1,0:T(8,128)}, f32[2,6]{1,0:T(2,128)}) custom-call(f32[2,48,3072]{2,1,0:T(8,128)} %bitcast.5, f32[2,48,3072]{2,1,0:T(8,128)} %bitcast.6, f32[2,3072]{1,0:T(2,128)} %depth_hbm.1, s32[2,24]{1,0:T(2,128)} %target_hbm.1, f32[2,3]{1,0:T(2,128)} %bitcast.7, f32[2,3]{1,0:T(2,128)} %bitcast.8), custom_call_target="tpu_custom_call" | custom-call | tf_op jit(solution)/shard_map/step/pallas_call | solution.py:731
  62.9 1.6 %hand_over.1 = (f32[2,3072]{1,0:T(2,128)}, f32[2,6]{1,0:T(2,128)}) custom-call(f32[128,128]{1,0:T(8,128)} %get-tuple-element.6.recv_f, f32[2,6]{1,0:T(2,128)} %get-tuple-element.7.pose_ref), custom_call_target="tpu_custom_call" | custom-call | tf_op jit(solution)/shard_map/hand_over/pallas_call | solution.py:812
